TPU v7x, 256 devices: a whole 4x4x8 slice. The times are simulated.
256 devices in a mesh: row: 16 (over y, z_lo, core), col: 16 (over z_hi, x).
Axes of the slice: x: 4, y: 4, z: 8 (z_hi: 4, z_lo: 2; z = z_hi * 2 + z_lo), core: 2. Of those that a mesh axis runs over, the one named last changes fastest.
Arguments:
- upper_corner: bfloat16 [96, 96], P(None, 'row'), may hold values from -6 to 6
- right_corner: bfloat16 [96, 96], P(None, 'row'), may hold values from -6 to 6
- lower_corner: bfloat16 [96, 96], P(None, 'row'), may hold values from -6 to 6
- top_edge: bfloat16 [96, 96, 36], P('row', 'col'), may hold values from -0.625 to 0.625
- right_edge: bfloat16 [96, 96, 36], P('row', 'col'), may hold values from -0.625 to 0.625
- bottom_edge: bfloat16 [96, 96, 36], P('row', 'col'), may hold values from -0.625 to 0.625
- left_edge: bfloat16 [96, 96, 36], P('row', 'col'), may hold values from -0.625 to 0.625
- site_tensor: bfloat16 [1679616], replicated, may hold values from -0.15625 to 0.15625
- top_projector: bfloat16 [3456, 96], P('col'), may hold values from -0.109375 to 0.109375
- bottom_projector: bfloat16 [3456, 96], P('col'), may hold values from -0.109375 to 0.109375
Outputs:
- upper_half: bfloat16 [3456, 3456], P('row', 'col')
- left_half: bfloat16 [3456, 3456], P('col', 'row')
- corner_top: bfloat16 [96, 3456], P('col', 'row')
- corner_bottom: bfloat16 [96, 3456], P('col', 'row')
All inputs are finite; a program needn't handle non-finite values.
Results may differ from a plain program's by a relative error of at most 0.0081.
Values may be sent and summed in bfloat16 or wider, within the bound.
No kernel may reach another device: no remote copies, remote signals or barrier semaphores. Data moves between devices by JAX's collectives and lax.ppermute only.
A program may use at most 128 MiB of HBM per device.

v0:
```python
import jax
import jax.numpy as jnp
from jax import lax
from jax.sharding import PartitionSpec as P

D = 6
CHI = 96


def sent_to_all(value, axis):
    size = lax.axis_size(axis)
    return lax.all_to_all(
        jnp.broadcast_to(value[None], (size, *value.shape)), axis, 0, 0, tiled=True
    )


def taken_together(value, axis):
    everything = sent_to_all(value, axis)
    return jnp.sum(everything, axis=0)


def together(arrays, axis):
    ends = [0]
    for a in arrays:
        ends.append(ends[-1] + a.size)
    subtotal = taken_together(jnp.concatenate([a.ravel() for a in arrays]), axis)
    return tuple((subtotal[b:e].reshape(a.shape) for a, b, e in zip(arrays, ends, ends[1:])))


def sent_together(arrays, axis, dim, along):
    widths = [a.shape[along] for a in arrays]
    both = jnp.concatenate(arrays, axis=along)
    filled = lax.all_gather(both, axis, axis=dim, tiled=True)
    return tuple(jnp.split(filled, [sum(widths[:k]) for k in range(1, len(widths))], axis=along))


def in_order(tiles, dim):
    lengths = list(tiles.shape[1:])
    lengths[dim] *= tiles.shape[0]
    return jnp.moveaxis(tiles, 0, dim).reshape(lengths)


def collect(value, axis, dim):
    return in_order(sent_to_all(value, axis), dim)


def gather_turned(arrays, axis, dims):
    turned = [jnp.moveaxis(a, dim, 0) for a, dim in zip(arrays, dims)]
    both = jnp.concatenate([t.reshape(len(t), -1) for t in turned], axis=1)
    filled, at, gathered = (lax.all_gather(both, axis, axis=0, tiled=True), 0, [])
    for t, dim in zip(turned, dims):
        section = filled[:, at : at + t[0].size].reshape(-1, *t.shape[1:])
        gathered.append(jnp.moveaxis(section, 0, dim))
        at += t[0].size
    return tuple(gathered)


def cut_along(value, dim, size):
    before, after = (value.shape[:dim], value.shape[dim + 1 :])
    return jnp.moveaxis(value.reshape(*before, size, -1, *after), dim, 0)


def summed_on_arrival(value, axis, dim):
    size = lax.axis_size(axis)
    tiles = lax.all_to_all(cut_along(value, dim, size), axis, 0, 0, tiled=True)
    return jnp.sum(tiles, axis=0)


def contract(form, first, second):
    return jnp.einsum(form, first, second, preferred_element_type=jnp.float32).astype(jnp.bfloat16)


def flatten(block):
    return block.reshape(block.shape[0] * block.shape[1], block.shape[2] * block.shape[3])


def shards(
    upper_corner,
    right_corner,
    lower_corner,
    top_edge,
    right_edge,
    bottom_edge,
    left_edge,
    site_tensor,
    top_projector,
    bottom_projector,
):
    factor = (CHI * D * D) ** (-0.5)
    double = D * D
    site = site_tensor.reshape(double, double, double, double)
    summed = together(
        (
            jnp.einsum("cd,dbv->cbv", upper_corner, top_edge, preferred_element_type=jnp.float32),
            jnp.einsum("cd,dbv->cbv", right_corner, right_edge, preferred_element_type=jnp.float32),
            jnp.einsum(
                "cd,dbv->cbv", lower_corner, bottom_edge, preferred_element_type=jnp.float32
            ),
        ),
        "row",
    )
    absorbed_top = summed[0].astype(jnp.bfloat16)
    absorbed_right = summed[1].astype(jnp.bfloat16)
    absorbed_bottom = summed[2].astype(jnp.bfloat16)
    left_rows, top_rows = sent_together((left_edge, top_edge), "col", 1, 0)
    own_block = top_edge.shape[0]
    row_start = lax.axis_index("row") * own_block
    left_whole = collect(left_rows, "row", 0)
    left_columns = lax.dynamic_slice_in_dim(left_whole, row_start, own_block, 1)
    enlarged_top = flatten(
        contract("aubv,vust->asbt", contract("acu,cbv->aubv", left_rows, absorbed_top), site)
    )
    enlarged_right = flatten(
        contract("bvgw,vtsw->btgs", contract("bdv,dgw->bvgw", top_rows, absorbed_right), site)
    )
    enlarged_bottom = flatten(
        contract("aubv,suvt->asbt", contract("cau,cbv->aubv", left_columns, absorbed_bottom), site)
    )
    top_panel, bottom_panel = gather_turned((enlarged_top, enlarged_bottom), "col", (1, 1))
    upper_sum = jnp.dot(
        top_panel, collect(enlarged_right, "row", 0), preferred_element_type=jnp.float32
    )
    upper_half = (upper_sum * factor).astype(jnp.bfloat16)
    spread = collect(absorbed_bottom, "col", 1)
    bottom_slice = lax.dynamic_slice_in_dim(spread, row_start, own_block, 1)
    top_columns = flatten(
        contract("aubv,vust->asbt", contract("acu,cbv->aubv", left_whole, absorbed_top), site)
    )
    bottom_columns = flatten(
        contract("aubv,suvt->asbt", contract("cau,cbv->aubv", left_whole, bottom_slice), site)
    )
    left_sum = lax.dot_general(
        top_columns, bottom_columns, (((0,), (0,)), ((), ())), preferred_element_type=jnp.float32
    )
    left_half = (left_sum * factor).astype(jnp.bfloat16)
    top_term = lax.dot_general(
        top_projector, enlarged_top, (((0,), (1,)), ((), ())), preferred_element_type=jnp.float32
    )
    bottom_term = lax.dot_general(
        bottom_projector,
        enlarged_bottom,
        (((0,), (1,)), ((), ())),
        preferred_element_type=jnp.float32,
    )
    corners = summed_on_arrival(jnp.concatenate([top_term, bottom_term], axis=1), "col", 0)
    split_at = enlarged_top.shape[0]
    corner_top = corners[:, :split_at].astype(jnp.bfloat16)
    corner_bottom = corners[:, split_at:].astype(jnp.bfloat16)
    return (upper_half, left_half, corner_top, corner_bottom)


def solution(mesh):
    placed = (
        P(None, "row"),
        P(None, "row"),
        P(None, "row"),
        P("row", "col", None),
        P("row", "col", None),
        P("row", "col", None),
        P("row", "col", None),
        P(),
        P("col", None),
        P("col", None),
    )
    return jax.shard_map(
        shards,
        mesh=mesh,
        in_specs=placed,
        out_specs=(P("row", "col"), P("col", "row"), P("col", "row"), P("col", "row")),
        check_vma=False,
    )
```

profile of v0, /device:TPU:1, one launch (start us, length us, event | category | flops | bytes accessed | tf_op | source)
XLA Modules:
  0.0 300.0 jit_solution(15837449866923643637)
XLA Ops:
  7.2 0.8 copy.118
  8.0 0.7 copy.119
  8.7 42.7 %all_gather.6 = bf16[12,96,36]{2,0,1:T(8,128)(2,1)S(1)} all-gather(bf16[12,6,36]{2,0,1:T(8,128)(2,1)S(1)} %pad_maximum_fusion.3), channel_id=1, replica_groups=mesh['row'=16,'col'=16] {'col'}, dimensions={1}, use_global_device_ids=true | all-gather | bytes 88128 | tf_op jit(solution)/shard_map/all_gather | solution.py:33
  51.5 0.8 fusion.94
  52.2 0.2 copy.173
  52.4 1.1 broadcast_in_dim.11
  53.5 13.5 %all-to-all-start.1 = ((bf16[16,6,96,36]{2,3,1,0:T(8,128)(2,1)}), bf16[16,6,96,36]{2,3,1,0:T(8,128)(2,1)S(1)}, u32[]{:S(2)}, u32[]{:S(2)}) async-start(bf16[16,6,96,36]{2,3,1,0:T(8,128)(2,1)} %broadcast_in_dim.11), calls=%async_computation.1 | async-start | bytes 1966080 | tf_op jit(solution)/shard_map/all_to_all | solution.py:12
  67.1 0.2 fusion.89
  67.3 0.2 fusion.85
  67.5 0.2 copy.122
  67.7 0.2 reshape.96
  67.9 0.2 copy.124
  68.2 0.2 reshape.97
  68.4 0.2 fusion.83
  68.6 0.2 copy.126
  68.8 0.2 reshape.98
  69.1 13.0 %all-to-all-done.1 = bf16[16,6,96,36]{2,3,1,0:T(8,128)(2,1)S(1)} async-done(((bf16[16,6,96,36]{2,3,1,0:T(8,128)(2,1)}), bf16[16,6,96,36]{2,3,1,0:T(8,128)(2,1)S(1)}, u32[]{:S(2)}, u32[]{:S(2)}) %all-to-all-start.1) | async-done | bytes 663584 | tf_op jit(solution)/shard_map/all_to_all | solution.py:12
  82.0 1.0 copy-done.3
  83.0 4.1 %broadcast_in_dim.10 = f32[16,1,62208]{2,1,0:T(1,128)} broadcast(f32[62208]{0:T(1024)S(1)} %pad_maximum_fusion), dimensions={2} | broadcast | bytes 4230144 | tf_op jit(solution)/shard_map/broadcast_in_dim | solution.py:13
  87.1 5.5 %all-to-all-start = ((f32[16,1,62208]{2,1,0:T(1,128)}), f32[16,1,62208]{2,1,0:T(1,128)}, u32[]{:S(2)}, u32[]{:S(2)}) async-start(f32[16,1,62208]{2,1,0:T(1,128)} %broadcast_in_dim.10), calls=%async_computation | async-start | bytes 7962624 | tf_op jit(solution)/shard_map/all_to_all | solution.py:12
  92.6 0.3 all-gather.2.cloned.1.call-start
  92.9 21.2 %reshape.119 = bf16[36,36,36,36,1]{3,2,1,0,4:T(8,128)(2,1)} reshape(bf16[1679616]{0:T(1024)(128)(2,1)S(1)} %copy-done.2) | data formatting | bytes 6718464 | tf_op jit(solution)/shard_map/reshape | solution.py:91
  114.1 20.8 %reshape.99 = bf16[36,36,36,36]{3,2,1,0:T(8,128)(2,1)} reshape(bf16[1679616]{0:T(1024)(128)(2,1)S(1)} %copy-done.2) | data formatting | bytes 6718464 | tf_op jit(solution)/shard_map/reshape | solution.py:91
  134.9 1.7 copy.175
  136.6 20.9 %copy.141 = bf16[36,36,36,36]{0,3,1,2:T(8,128)(2,1)} copy(bf16[36,36,36,36]{3,2,1,0:T(8,128)(2,1)} %reshape.99) | data formatting | bytes 6718464 | tf_op jit(solution)/shard_map/reshape | solution.py:91
  157.5 0.3 constant_dynamic-slice_fusion
  157.9 0.6 copy.174
  158.5 4.6 %reduce_sum.18 = bf16[62208]{0:T(1024)(128)(2,1)S(1)} reduce(f32[16,1,62208]{2,1,0:T(1,128)} %all-to-all-done, f32[]{:T(128)} %constant.2.clone.1), dimensions={0,1}, to_apply=%region_0.0 | reduce | flops 933120 | bytes 4105732 | tf_op jit(solution)/shard_map/reduce_sum | solution.py:19
  163.1 0.2 convert_element_type.77
  163.3 0.2 copy.132
  163.5 0.3 fusion.51
  163.8 7.0 %fusion.46 = bf16[6,36,6,36]{3,2,1,0:T(8,128)(2,1)S(1)} fusion(bf16[36,36,36,36,1]{3,2,1,0,4:T(8,128)(2,1)} %reshape.119, bf16[6,36,6,36,1]{3,1,2,0,4:T(8,128)(2,1)S(1)} %fusion.51), kind=kOutput, calls=%fused_computation.32 | convolution fusion | flops 120979008 | bytes 3545856 | tf_op jit(solution)/shard_map/aubv,suvt->asbt/dot_general | solution.py:70
  170.8 0.2 reshape.102
  171.1 0.2 convert_element_type.73
  171.3 0.2 copy.128
  171.5 0.3 fusion.50
  171.8 9.0 %fusion.47 = bf16[6,36,6,36]{3,2,1,0:T(8,128)(2,1)S(1)} fusion(bf16[36,36,36,36]{3,2,1,0:T(8,128)(2,1)} %reshape.99, bf16[6,36,6,36,1]{3,1,2,0,4:T(8,128)(2,1)S(1)} %fusion.50), kind=kOutput, calls=%fused_computation.33 | convolution fusion | flops 120979008 | bytes 3545856 | tf_op jit(solution)/shard_map/aubv,vust->asbt/dot_general | solution.py:70
  180.8 0.2 reshape.100
  181.1 0.8 copy.134
  181.9 0.0 all-gather.2.cloned.1.call-update
  181.9 0.2 convolution_bitcast_fusion.1
  182.1 0.0 copy-done.10
  182.1 0.2 convolution_bitcast_fusion.2
  182.3 0.1 pad_maximum_fusion.2
  182.4 0.7 reshape.107
  183.2 3.9 %all-to-all-start.4 = ((f32[16,6,432]{2,1,0:T(8,128)}), f32[16,6,432]{2,1,0:T(8,128)S(1)}, u32[]{:S(2)}, u32[]{:S(2)}) async-start(f32[16,6,432]{2,1,0:T(8,128)} %reshape.107), calls=%async_computation.4 | async-start | bytes 524288 | tf_op jit(solution)/shard_map/all_to_all | solution.py:65
  187.1 9.3 %fusion.10 = bf16[96,36,6,36]{0,3,1,2:T(8,128)(2,1)S(1)} fusion(bf16[36,36,36,36]{0,3,1,2:T(8,128)(2,1)} %copy.141, bf16[96,96,36]{1,2,0:T(8,128)(2,1)S(1)} %bitcast.165, bf16[96,6,36,1]{2,1,0,3:T(8,128)(2,1)} %bitcast.169), kind=kOutput, calls=%fused_computation.12 | convolution fusion | flops 2079737856 | bytes 5557248 | tf_op jit(solution)/shard_map/aubv,vust->asbt/dot_general | solution.py:70
  196.4 0.9 convert_element_type.81
  197.4 1.7 copy.136
  199.1 2.0 broadcast_in_dim.14
  201.0 9.1 %all-to-all-start.3 = ((bf16[16,96,6,36]{1,3,2,0:T(8,128)(2,1)}), bf16[16,96,6,36]{1,3,2,0:T(8,128)(2,1)}, u32[]{:S(2)}, u32[]{:S(2)}) async-start(bf16[16,96,6,36]{1,3,2,0:T(8,128)(2,1)} %broadcast_in_dim.14), calls=%async_computation.3 | async-start | bytes 1966080 | tf_op jit(solution)/shard_map/all_to_all | solution.py:12
  210.1 1.1 fusion.52
  211.3 14.7 %fusion.43 = bf16[6,36,6,36]{3,2,1,0:T(8,128)(2,1)} fusion(bf16[36,36,36,36]{3,2,1,0:T(8,128)(2,1)} %reshape.99, bf16[6,36,6,36,1]{3,1,2,0,4:T(8,128)(2,1)S(1)} %fusion.52), kind=kOutput, calls=%fused_computation.31 | convolution fusion | flops 120979008 | bytes 3545856 | tf_op jit(solution)/shard_map/bvgw,vtsw->btgs/dot_general | solution.py:70
  225.9 1.9 broadcast_in_dim.12
  227.9 4.5 %copy.142 = bf16[96,36,6,36]{1,0,3,2:T(8,128)(2,1)} copy(bf16[96,36,6,36]{0,3,1,2:T(8,128)(2,1)S(1)} %fusion.10) | data formatting | bytes 2985984 | tf_op jit(solution)/shard_map/convert_element_type | solution.py:70
  232.4 10.8 %reshape.104 = bf16[3456,216]{0,1:T(8,128)(2,1)} reshape(bf16[96,36,6,36]{1,0,3,2:T(8,128)(2,1)} %copy.142) | data formatting | bytes 2985984 | tf_op jit(solution)/shard_map/reshape | solution.py:74
  243.2 0.7 fusion.96
  243.9 1.3 broadcast_in_dim.13
  245.2 20.2 %all-to-all-start.2 = ((bf16[16,216,216]{2,1,0:T(8,128)(2,1)}), bf16[16,216,216]{2,1,0:T(8,128)(2,1)}, u32[]{:S(2)}, u32[]{:S(2)}) async-start(bf16[16,216,216]{2,1,0:T(8,128)(2,1)} %broadcast_in_dim.13), calls=%async_computation.2 | async-start | bytes 3538944 | tf_op jit(solution)/shard_map/all_to_all | solution.py:12
  265.5 8.1 %fusion.11 = bf16[96,36,6,36]{0,3,1,2:T(8,128)(2,1)S(1)} fusion(bf16[36,36,36,36]{3,2,1,0:T(8,128)(2,1)} %reshape.99, bf16[96,96,36]{1,2,0:T(8,128)(2,1)S(1)} %bitcast.166, bf16[96,96,36]{0,2,1:T(8,128)(2,1)} %bitcast.40, s32[]{:T(128)S(6)} %select_n.4), kind=kOutput, calls=%fused_computation.13 | convolution fusion | flops 2079737856 | bytes 15489028 | tf_op jit(solution)/shard_map/aubv,suvt->asbt/dot_general | solution.py:70
  273.6 4.6 %copy.146 = bf16[96,36,6,36]{1,0,3,2:T(8,128)(2,1)} copy(bf16[96,36,6,36]{0,3,1,2:T(8,128)(2,1)S(1)} %fusion.11) | data formatting | bytes 2985984 | tf_op jit(solution)/shard_map/convert_element_type | solution.py:70
  278.1 10.2 %reshape.106 = bf16[3456,216]{0,1:T(8,128)(2,1)S(1)} reshape(bf16[96,36,6,36]{1,0,3,2:T(8,128)(2,1)} %copy.146) | data formatting | bytes 2985984 | tf_op jit(solution)/shard_map/reshape | solution.py:74
  288.3 1.2 fusion.56
  289.5 3.4 %fusion.57 = bf16[216,216]{1,0:T(8,128)(2,1)} fusion(bf16[3456,216]{1,0:T(8,128)(2,1)} %bitcast.29, bf16[3456,432]{1,0:T(8,128)(2,1)} %all-gather.2.cloned.1.call-done), kind=kOutput, calls=%fused_computation.40 | convolution fusion | flops 322579584 | bytes 3632256 | tf_op jit(solution)/shard_map/dot_general | solution.py:120
  (40 shorter events, 0.2 us)
Async XLA Ops:
  7.2 174.8 %copy-start = (bf16[216,96]{0,1:T(8,128)(2,1)S(1)}, bf16[216,96]{0,1:T(8,128)(2,1)}, u32[]{:S(2)}) copy-start(bf16[216,96]{0,1:T(8,128)(2,1)} %param.19) | copy-start | bytes 124420
  7.2 59.9 %copy-start.9 = (bf16[6,6,36]{2,1,0:T(8,128)(2,1)S(1)}, bf16[6,6,36]{2,1,0:T(8,128)(2,1)}, u32[]{:S(2)}) copy-start(bf16[6,6,36]{2,1,0:T(8,128)(2,1)} %param.13) | copy-start | bytes 7780
  7.2 59.9 %copy-start.13 = (bf16[96,6]{0,1:T(8,128)(2,1)S(1)}, bf16[96,6]{0,1:T(8,128)(2,1)}, u32[]{:S(2)}) copy-start(bf16[96,6]{0,1:T(8,128)(2,1)} %param.10) | copy-start | bytes 3460
  7.2 60.1 %copy-start.14 = (bf16[96,6]{0,1:T(8,128)(2,1)S(1)}, bf16[96,6]{0,1:T(8,128)(2,1)}, u32[]{:S(2)}) copy-start(bf16[96,6]{0,1:T(8,128)(2,1)} %param.11) | copy-start | bytes 3460
  7.2 60.1 %copy-start.11 = (bf16[6,6,36]{2,1,0:T(8,128)(2,1)S(1)}, bf16[6,6,36]{2,1,0:T(8,128)(2,1)}, u32[]{:S(2)}) copy-start(bf16[6,6,36]{2,1,0:T(8,128)(2,1)} %param.14) | copy-start | bytes 7780
  7.2 61.1 %copy-start.15 = (bf16[96,6]{0,1:T(8,128)(2,1)S(1)}, bf16[96,6]{0,1:T(8,128)(2,1)}, u32[]{:S(2)}) copy-start(bf16[96,6]{0,1:T(8,128)(2,1)} %param.12) | copy-start | bytes 3460
  7.2 61.1 %copy-start.12 = (bf16[6,6,36]{2,1,0:T(8,128)(2,1)S(1)}, bf16[6,6,36]{2,1,0:T(8,128)(2,1)}, u32[]{:S(2)}) copy-start(bf16[6,6,36]{2,1,0:T(8,128)(2,1)} %param.15) | copy-start | bytes 7780
  53.5 28.5 %all-to-all-start.1 = ((bf16[16,6,96,36]{2,3,1,0:T(8,128)(2,1)}), bf16[16,6,96,36]{2,3,1,0:T(8,128)(2,1)S(1)}, u32[]{:S(2)}, u32[]{:S(2)}) async-start(bf16[16,6,96,36]{2,3,1,0:T(8,128)(2,1)} %broadcast_in_dim.11), calls=%async_computation.1 | async-start | bytes 1966080 | tf_op jit(solution)/shard_map/all_to_all | solution.py:12
  82.0 1.0 copy-start.3
  87.1 5.8 %copy-start.2 = (bf16[1679616]{0:T(1024)(128)(2,1)S(1)}, bf16[1679616]{0:T(1024)(128)(2,1)}, u32[]{:S(2)}) copy-start(bf16[1679616]{0:T(1024)(128)(2,1)} %param.17) | copy-start | bytes 10077700
  87.1 71.4 %all-to-all-start = ((f32[16,1,62208]{2,1,0:T(1,128)}), f32[16,1,62208]{2,1,0:T(1,128)}, u32[]{:S(2)}, u32[]{:S(2)}) async-start(f32[16,1,62208]{2,1,0:T(1,128)} %broadcast_in_dim.10), calls=%async_computation | async-start | bytes 7962624 | tf_op jit(solution)/shard_map/all_to_all | solution.py:12
  92.6 197.0 %all-gather.2.cloned.1.call-start = ((), (), s32[]{:S(2)}) async-start(), calls=%async_computation.5 | async-start | bytes 3760128 | tf_op jit(solution)/shard_map/all_gather | solution.py:50
  136.6 20.9 %copy-start.4 = (bf16[16,6,96,36]{2,3,1,0:T(8,128)(2,1)S(1)}, bf16[16,6,96,36]{2,3,1,0:T(8,128)(2,1)}, u32[]{:S(2)}) copy-start(bf16[16,6,96,36]{2,3,1,0:T(8,128)(2,1)} %copy-done.3) | copy-start | bytes 1990660
  163.5 7.3 %copy-start.7 = (bf16[96,6,36]{0,2,1:T(8,128)(2,1)}, bf16[96,6,36]{0,2,1:T(8,128)(2,1)S(1)}, u32[]{:S(2)}) copy-start(bf16[96,6,36]{0,2,1:T(8,128)(2,1)S(1)} %copy.132) | copy-start | bytes 124420
  171.3 9.5 %copy-start.6 = (bf16[96,6,36]{2,1,0:T(8,128)(2,1)}, bf16[96,6,36]{2,1,0:T(8,128)(2,1)S(1)}, u32[]{:S(2)}) copy-start(bf16[96,6,36]{2,1,0:T(8,128)(2,1)S(1)} %convert_element_type.73) | copy-start | bytes 124420
  171.8 10.3 %copy-start.10 = (bf16[216,96]{0,1:T(8,128)(2,1)S(1)}, bf16[216,96]{0,1:T(8,128)(2,1)}, u32[]{:S(2)}) copy-start(bf16[216,96]{0,1:T(8,128)(2,1)} %param.18) | copy-start | bytes 124420
  183.2 15.9 %all-to-all-start.4 = ((f32[16,6,432]{2,1,0:T(8,128)}), f32[16,6,432]{2,1,0:T(8,128)S(1)}, u32[]{:S(2)}, u32[]{:S(2)}) async-start(f32[16,6,432]{2,1,0:T(8,128)} %reshape.107), calls=%async_computation.4 | async-start | bytes 524288 | tf_op jit(solution)/shard_map/all_to_all | solution.py:65
  201.0 42.8 %all-to-all-start.3 = ((bf16[16,96,6,36]{1,3,2,0:T(8,128)(2,1)}), bf16[16,96,6,36]{1,3,2,0:T(8,128)(2,1)}, u32[]{:S(2)}, u32[]{:S(2)}) async-start(bf16[16,96,6,36]{1,3,2,0:T(8,128)(2,1)} %broadcast_in_dim.14), calls=%async_computation.3 | async-start | bytes 1966080 | tf_op jit(solution)/shard_map/all_to_all | solution.py:12
  232.4 11.5 %copy-start.8 = (bf16[216,216]{1,0:T(8,128)(2,1)S(1)}, bf16[216,216]{1,0:T(8,128)(2,1)}, u32[]{:S(2)}) copy-start(bf16[216,216]{1,0:T(8,128)(2,1)} %broadcast_in_dim.12) | copy-start | bytes 279940
  245.2 44.3 %all-to-all-start.2 = ((bf16[16,216,216]{2,1,0:T(8,128)(2,1)}), bf16[16,216,216]{2,1,0:T(8,128)(2,1)}, u32[]{:S(2)}, u32[]{:S(2)}) async-start(bf16[16,216,216]{2,1,0:T(8,128)(2,1)} %broadcast_in_dim.13), calls=%async_computation.2 | async-start | bytes 3538944 | tf_op jit(solution)/shard_map/all_to_all | solution.py:12
  278.1 10.2 %copy-start.5 = (bf16[3456,216]{0,1:T(8,128)(2,1)S(1)}, bf16[3456,216]{0,1:T(8,128)(2,1)}, u32[]{:S(2)}) copy-start(bf16[3456,216]{0,1:T(8,128)(2,1)} %reshape.104) | copy-start | bytes 4478980
  278.1 14.8 %copy-start.1 = (bf16[216,96]{0,1:T(8,128)(2,1)S(1)}, bf16[216,96]{0,1:T(8,128)(2,1)}, u32[]{:S(2)}) copy-start(bf16[216,96]{0,1:T(8,128)(2,1)} %param.19) | copy-start | bytes 124420
Sparse Core Ops, SparseCore 0:
  182.1 73.0 all-gather.1
where the time goes:
time: 305 us; the launch traced here: 300 us
  local copies, waits for them, and re-layouts  117 us (38%)
  matrix products  55.3 us (18%)
  starting transfers between devices  52.6 us (17%)
  blocking collectives  42.7 us (14%)
  between operations  14.6 us (5%)
  waiting for transfers between devices  13 us (4%)
  other arithmetic  4.84 us (2%)
    reshape x3, local copies, waits for them, and re-layouts, shards(): site = site_tensor.reshape(double, double, double, double)  62.9 us
    dot_general x8, matrix products, contract(): jnp.einsum(form, first, second, preferred_element_type=jnp.float32)  49.8 us
    all_to_all x4, starting transfers between devices, sent_to_all(): lax.all_to_all(jnp.broadcast_to(value[None], (size, *value.shape)), axis,...  48.4 us
    all_gather x1, blocking collectives, sent_together(): filled = lax.all_gather(both, axis, axis=dim, tiled=True)  42.7 us
    reshape x4, local copies, waits for them, and re-layouts, flatten(): block.reshape(block.shape[0] * block.shape[1], block.shape[2] * block.sha...  21.4 us
    all_to_all x4, waiting for transfers between devices, sent_to_all(): lax.all_to_all(jnp.broadcast_to(value[None], (size, *value.shape)), axis,...  13 us
    broadcast_in_dim x5, local copies, waits for them, and re-layouts, sent_to_all(): jnp.broadcast_to(value[None], (size, *value.shape))  10.4 us
    convert_element_type x2, local copies, waits for them, and re-layouts, contract(): jnp.einsum(form, first, second, preferred_element_type=jnp.float32)  9.08 us
  transfers between devices with their start and end apart: 6, of which 1 were waited for; matrix products, arithmetic and copies ran while one was open for 47% of the time, Pallas kernels for 0%

commit v1 on v0

v1 whole, which is shorter than its diff:
```python
import jax
import jax.numpy as jnp
from jax import lax
from jax.experimental import pallas as pl
from jax.experimental.pallas import tpu as pltpu
from jax.sharding import PartitionSpec as P

F=jnp.float32; B=jnp.bfloat16
NN=(((1,),(0,)),((),()));NT=(((1,),(1,)),((),()))
def dot(x,y,dims=NN): return lax.dot_general(x,y,dims,preferred_element_type=F)
MCH=432
def expand(order_ref, buf_ref, off, dst):
    for rel in range(16):
        at=pl.multiple_of(order_ref[rel]*216,8)
        dst[pl.ds(at,216),:]=buf_ref[rel*496+off:rel*496+off+216,:].astype(F)
def to_bf16(src,dst):
    def f(i,_):
        at=pl.multiple_of(i*48,16)
        for a in range(6):
            dst[pl.ds(at,48),a*128:(a+1)*128]=src[a,pl.ds(at,48),:].astype(B)
        return 0
    lax.fori_loop(0,27,f,0)
def big(w_ref,p_ref,o_ref):
    def f(i,_):
        at=pl.multiple_of(i*MCH,16)
        res=dot(w_ref[pl.ds(at,MCH),:],p_ref[...])
        for a in range(6):
            o_ref[a,pl.ds(at,MCH),:]=res[:,a*128:(a+1)*128]
        return 0
    lax.fori_loop(0,1296//MCH,f,0)
    o_ref[:,1296:1440,:]=jnp.zeros((6,144,128),F)
def upper_kernel(order_ref, buf_ref, small_ref, wtop_ref, wright_ref, tpy_ref, out_ref, ct_ref, tef, pf, p1, p3, o1, o3):
    expand(order_ref, buf_ref, 0, tef)
    uc=small_ref[648:744,:]; rc=small_ref[744:840,:]
    ler=buf_ref[216:432,:]
    lu=dot(ler[:,:96],uc).astype(B)[:,:96]
    ar=dot(small_ref[216:432,:],rc,NT).astype(B)
    for v in range(36):
        te=tef[pl.ds(v,96,stride=36),:].astype(B)
        d1=dot(lu,te)
        for a in range(6):
            pf[a,v*36:(v+1)*36,:]=d1[a*36:(a+1)*36,:]
    to_bf16(pf,p1)
    for v in range(36):
        te=tef[pl.ds(v,96,stride=36),:].astype(B)
        d3=dot(ar,te[:,:96],NT)
        d3=jnp.concatenate([d3,jnp.zeros((216,32),F)],axis=1)
        for a in range(6):
            pf[a,v*36:(v+1)*36,:]=d3[a*36:(a+1)*36,:]
    to_bf16(pf,p3)
    big(wtop_ref,p1,o1)
    big(wright_ref,p3,o3)
    acc=jnp.zeros((240,248),F)
    for tp in range(18):
        xs=[];ys=[]
        for t in (2*tp,2*tp+1):
            xs.append(jnp.concatenate([o1[a,pl.ds(t,40,stride=36),:] for a in range(6)],axis=0).astype(B))
            ys.append(jnp.concatenate([o3[g,pl.ds(t,40,stride=36),:] for g in range(6)]+[tpy_ref[t*8:(t+1)*8,:].astype(F)],axis=0).astype(B))
        acc=acc+dot(jnp.concatenate(xs,axis=1),jnp.concatenate(ys,axis=1),NT)
    fac=jnp.float32(3456.0**-0.5)
    up=(acc[:,:240]*fac)
    for a in range(6):
        for g in range(6):
            out_ref[a*36:(a+1)*36,g*36:(g+1)*36]=up[a*40:a*40+36,g*40:g*40+36].astype(B)
    ct_ref[...]=acc[:,240:248]
def left_kernel(order_ref, buf_ref, small_ref, ber_ref, wtop_ref, wbot_ref, bpr_ref, out_ref, cb_ref, lef, pf, p2, p4, o2, o4):
    expand(order_ref, buf_ref, 216, lef)
    uc=small_ref[648:744,:]; lc=small_ref[840:936,:]
    at=dot(small_ref[0:216,:],uc,NT).astype(B)
    ab=dot(ber_ref[...],lc,NT).astype(B)
    for u in range(36):
        le=lef[pl.ds(u,96,stride=36),:].astype(B)
        d2=dot(at,le[:,:96],NT)
        d2=jnp.concatenate([d2,jnp.zeros((216,32),F)],axis=1)
        for b in range(6):
            pf[b,pl.ds(u,36,stride=36),:]=d2[b*36:(b+1)*36,:]
    to_bf16(pf,p2)
    for u in range(36):
        le=lef[pl.ds(u,96,stride=36),:].astype(B)
        d4=dot(ab,le)
        for b in range(6):
            pf[b,pl.ds(u,36,stride=36),:]=d4[b*36:(b+1)*36,:]
    to_bf16(pf,p4)
    big(wtop_ref,p2,o2)
    big(wbot_ref,p4,o4)
    acc=jnp.zeros((240,240),F)
    for sp in range(18):
        xs=[];ys=[]
        for s in (2*sp,2*sp+1):
            x=jnp.concatenate([o2[b,s*36:s*36+40,:] for b in range(6)],axis=0).astype(B)
            y=jnp.concatenate([o4[b,s*36:s*36+40,:] for b in range(6)],axis=0).astype(B)
            xs.append(x);ys.append(y)
            cb_ref[s*8:(s+1)*8,:]=dot(bpr_ref[...],y)
        acc=acc+dot(jnp.concatenate(xs,axis=1),jnp.concatenate(ys,axis=1),NT)
    lh=acc*jnp.float32(3456.0**-0.5)
    for a in range(6):
        for g in range(6):
            out_ref[a*36:(a+1)*36,g*36:(g+1)*36]=lh[a*40:a*40+36,g*40:g*40+36].astype(B)
VM=pl.BlockSpec(memory_space=pltpu.VMEM); SM=pl.BlockSpec(memory_space=pltpu.SMEM)
def scr(): return [pltpu.VMEM((3456,128),F),pltpu.VMEM((6,1296,128),F),pltpu.VMEM((1296,768),B),pltpu.VMEM((1296,768),B),pltpu.VMEM((6,1440,128),F),pltpu.VMEM((6,1440,128),F)]
def upper(order,buf,small,wtop,wright,tpy):
    return pl.pallas_call(upper_kernel,out_shape=(jax.ShapeDtypeStruct((216,216),B),jax.ShapeDtypeStruct((240,8),F)),
        in_specs=[SM]+[VM]*5,out_specs=(VM,VM),scratch_shapes=scr(),name="upper",
        compiler_params=pltpu.CompilerParams(vmem_limit_bytes=56<<20))(order,buf,small,wtop,wright,tpy)
def left(order,buf,small,ber,wtop,wbot,bpr):
    return pl.pallas_call(left_kernel,out_shape=(jax.ShapeDtypeStruct((216,216),B),jax.ShapeDtypeStruct((288,128),F)),
        in_specs=[SM]+[VM]*6,out_specs=(VM,VM),scratch_shapes=scr(),name="left",
        compiler_params=pltpu.CompilerParams(vmem_limit_bytes=56<<20))(order,buf,small,ber,wtop,wbot,bpr)


def lanes_shifted(a_ref, z_ref, pair):
    tile = (pair * 72) // 128
    base = pl.multiple_of(tile * 128, 128)
    off = pair * 72 - tile * 128
    k = lax.broadcasted_iota(jnp.int32, (256, 256), 0)
    n = lax.broadcasted_iota(jnp.int32, (256, 256), 1)
    w = n % 128
    sel = ((k == off + (n // 128) * 36 + w) & (w < 36)).astype(B)
    z_ref[...] = dot(a_ref[:, pl.ds(base, 256)], sel)
def realign(a_ref, z_ref, o_ref):
    def f(g, _):
        strips = []
        for h in range(2):
            lanes_shifted(a_ref, z_ref.at[h], 2 * g + h)
            for q in range(2):
                strips.append(jnp.concatenate([z_ref[h, k * 36:(k + 1) * 36, q * 128:q * 128 + 36] for k in range(36)], axis=1))
        at = pl.multiple_of(g * 144, 16)
        o_ref[pl.ds(at, 144), :] = jnp.concatenate(strips, axis=0).astype(B)
        return 0
    lax.fori_loop(0, 9, f, 0)
def site_kernel(s_ref, wtop_ref, wright_ref, wbot_ref, apad, z):
    zero = jnp.zeros((1296, 112), B)
    apad[:, 1296:1408] = zero
    apad[:, :1296] = s_ref[...]
    realign(apad, z, wright_ref)
    eye = (lax.broadcasted_iota(jnp.int32, (128, 128), 0) == lax.broadcasted_iota(jnp.int32, (128, 128), 1)).astype(B)
    for b in range(11):
        res = dot(eye, apad[:, b * 128:(b + 1) * 128], NT).astype(B)
        n = min(128, 1296 - b * 128)
        wtop_ref[b * 128:b * 128 + n, :] = res[:n]
    apad[:, :1296] = wtop_ref[...]
    realign(apad, z, wbot_ref)
def site_forms(s2):
    shape = jax.ShapeDtypeStruct((1296, 1296), B)
    return pl.pallas_call(site_kernel, out_shape=(shape,) * 3, in_specs=[VM], out_specs=(VM,) * 3,
        scratch_shapes=[pltpu.VMEM((1296, 1408), B), pltpu.VMEM((2, 1296, 256), F)], name="site",
        compiler_params=pltpu.CompilerParams(vmem_limit_bytes=56 << 20))(s2)

ROW, COL = "row", "col"


def row_permute(x, move):
    pairs = []
    for y in range(4):
        for z in range(2):
            for k in range(2):
                a, b, c = move(y, z, k)
                pairs.append((y * 4 + z * 2 + k, a * 4 + b * 2 + c))
    return lax.ppermute(x, ROW, pairs)


def col_permute(x, move):
    pairs = []
    for z in range(4):
        for i in range(4):
            a, b = move(z, i)
            pairs.append((z * 4 + i, a * 4 + b))
    return lax.ppermute(x, COL, pairs)


def swap_axes(x):
    pairs = [(r * 16 + c, c * 16 + r) for r in range(16) for c in range(16)]
    return lax.ppermute(x, (ROW, COL), pairs)


def stacked(own, received):
    return jnp.concatenate([own, *received], axis=0)


def shards(uc, rc, lc, te, re, be, le, site_flat, tp, bp):
    bf = jnp.bfloat16
    r = lax.axis_index(ROW)
    c = lax.axis_index(COL)
    y, zlo, core = r // 4, (r // 2) % 2, r % 2
    zhi, x = c // 4, c % 4

    tp_send = tp.reshape(216, 16, 6).transpose(1, 2, 0)
    tp_all = lax.all_to_all(tp_send, COL, 0, 0, tiled=True)
    tpy = tp_all.reshape(16, 6, 6, 36).transpose(3, 1, 0, 2).reshape(36, 6, 96)
    tpy = jnp.pad(tpy, ((0, 0), (0, 2), (0, 32))).reshape(288, 128)
    bp_row = swap_axes(bp)
    bpr = lax.dynamic_slice_in_dim(bp_row, c * 6, 6, 1).T.reshape(6, 6, 36)
    bpr = jnp.pad(bpr, ((0, 2), (0, 0), (0, 4))).reshape(8, 240)

    side = lambda e: jnp.pad(e.transpose(1, 0, 2).reshape(6, 216), ((0, 2), (0, 0)))
    piece = jnp.concatenate([side(te), side(le)], axis=0)
    piece = stacked(piece, [col_permute(piece, lambda z, i, s=s: ((z + s) % 4, i)) for s in (1, 2, 3)])
    piece = stacked(piece, [col_permute(piece, lambda z, i, s=s: (z, (i + s) % 4)) for s in (1, 2, 3)])
    at = jnp.arange(256)
    x_rel, z_rel, edge, j = at // 64, (at // 16) % 4, (at // 8) % 2, at % 8
    block = ((zhi - z_rel) % 4) * 4 + (x - x_rel) % 4
    target = jnp.where(j < 6, edge * 128 + block * 6 + j, -1)
    place = (target[:, None] == jnp.arange(256)[None, :]).astype(bf)
    rows = lax.dot_general(piece, place, (((0,), (0,)), ((), ())), preferred_element_type=jnp.float32).astype(bf)

    pack = jnp.concatenate([te.reshape(6, 216), re.reshape(6, 216), be.reshape(6, 216), uc.T, rc.T, lc.T], axis=1)
    pack = jnp.pad(pack, ((0, 2), (0, 88)))
    pack = pack.reshape(8, 8, 128).transpose(1, 0, 2).reshape(64, 128)
    buf = jnp.concatenate([rows[:, :128], rows[:, 128:], pack], axis=0)
    buf = stacked(buf, [row_permute(buf, lambda a, b, k: (a, 1 - b, k))])
    buf = stacked(buf, [row_permute(buf, lambda a, b, k, s=s: ((a + s) % 4, b, k)) for s in (1, 2, 3)])
    buf = stacked(buf, [row_permute(buf, lambda a, b, k: (a, b, 1 - k))])
    rel = jnp.arange(16)
    order = ((y - (rel // 2) % 4) % 4) * 4 + (zlo ^ (rel % 2)) * 2 + (core ^ (rel // 8))
    order = order.astype(jnp.int32)

    packs = buf.reshape(16, 496, 128)[:, 432:].reshape(16, 8, 8, 128).transpose(0, 2, 1, 3).reshape(128, 1024)
    at = jnp.arange(128)
    target = jnp.where(at % 8 < 6, jnp.repeat(order, 8) * 6 + at % 8, -1)
    place = (target[:, None] == jnp.arange(128)[None, :]).astype(bf)
    small = lax.dot_general(packs, place, (((0,), (0,)), ((), ())), preferred_element_type=jnp.float32).astype(bf)
    ber = swap_axes(small[432:648])

    wtop, wright, wbot = site_forms(site_flat.reshape(1296, 1296))

    up, ct = upper(order, buf, small, wtop, wright, tpy)
    lf, cb = left(order, buf, small, ber, wtop, wbot, bpr)
    corner_top = ct.reshape(6, 40, 8)[:, :36, :6].reshape(216, 6).T.astype(bf)
    part = cb.reshape(36, 8, 128)[:, :6, :96].reshape(36, 6, 16, 6).transpose(2, 1, 3, 0).reshape(16, 6, 216)
    corner_bottom = jnp.sum(lax.all_to_all(part, ROW, 0, 0, tiled=True), axis=0).astype(bf)
    return up, lf, corner_top, corner_bottom


def solution(mesh):
    placed = (
        P(None, ROW),
        P(None, ROW),
        P(None, ROW),
        P(ROW, COL, None),
        P(ROW, COL, None),
        P(ROW, COL, None),
        P(ROW, COL, None),
        P(),
        P(COL, None),
        P(COL, None),
    )
    return jax.shard_map(
        shards,
        mesh=mesh,
        in_specs=placed,
        out_specs=(P(ROW, COL), P(COL, ROW), P(COL, ROW), P(COL, ROW)),
        check_vma=False,
    )
```

time: 305 us -> 150 us (0.49); the launches traced: 300 us -> 149 us
  local copies, waits for them, and re-layouts: 117 us -> 23.8 us
  matrix products: 55.3 us -> 0.55 us
  Pallas kernels: 0 us -> 52.4 us
  blocking collectives: 42.7 us -> 0 us
  between operations: 14.6 us -> 0.95 us
  starting transfers between devices: 52.6 us -> 58.3 us
    reshape x11 -> x16, local copies, waits for them, and re-layouts: 85.6 us -> 13.7 us  [the longest x1 7.97 us: shards(): wtop, wright, wbot = site_forms(site_flat.reshape(1296, 1296))]
    dot_general x15 -> x2, matrix products: 55.3 us -> 0.55 us  [the longest x1 0.29 us: shards(): lax.dot_general(packs, place, (((0,), (0,)), ((), ())), preferred_element...]
    pallas_call x0 -> x3, Pallas kernels: none -> 52.4 us  [the longest x1 21.7 us: site_forms(): pl.pallas_call(site_kernel, out_shape=(shape,) * 3, in_specs=[VM], out_sp...]
    all_gather x1 -> x0, blocking collectives: 42.7 us -> none  [sent_together(): filled = lax.all_gather(both, axis, axis=dim, tiled=True)]
    ppermute x0 -> x13, starting transfers between devices: none -> 33.7 us  [the longest x6 16.4 us: col_permute(): return lax.ppermute(x, COL, pairs)]
    all_to_all x5 -> x2, starting transfers between devices: 52.3 us -> 24.7 us  [the longest x1 19.7 us: shards(): lax.all_to_all(part, ROW, 0, 0, tiled=True)]
    all_to_all x5 -> x2, waiting for transfers between devices: 13 us -> 0.01 us  [the longest x1 0.01 us: shards(): tp_all = lax.all_to_all(tp_send, COL, 0, 0, tiled=True)]
    convert_element_type x8 -> x1, local copies, waits for them, and re-layouts: 12.5 us -> 0.69 us  [shards(): corner_top = ct.reshape(6, 40, 8)[:, :36, :6].reshape(216, 6).T.astype(bf)]
  transfers between devices with their start and end apart: 6 -> 15, of which waited for: 1 -> 5; matrix products, arithmetic and copies ran while one was open for 47% -> 14% of each run, Pallas kernels for 0% -> 35%
where the time goes in v1:
time: 150 us; the launch traced here: 149 us
  starting transfers between devices  58.3 us (39%)
  Pallas kernels  52.4 us (35%)
  local copies, waits for them, and re-layouts  23.8 us (16%)
  waiting for transfers between devices  11.2 us (7%)
  other arithmetic  2.11 us (1%)
    pallas_call x1, Pallas kernels, site_forms(): pl.pallas_call(site_kernel, out_shape=(shape,) * 3, in_specs=[VM], out_sp...  21.7 us
    all_to_all x1, starting transfers between devices, shards(): lax.all_to_all(part, ROW, 0, 0, tiled=True)  19.7 us
    ppermute x6, starting transfers between devices, col_permute(): return lax.ppermute(x, COL, pairs)  16.4 us
    pallas_call x1, Pallas kernels, left(): pl.pallas_call(left_kernel, out_shape=(jax.ShapeDtypeStruct((216, 216), B...  15.6 us
    pallas_call x1, Pallas kernels, upper(): pl.pallas_call(upper_kernel, out_shape=(jax.ShapeDtypeStruct((216, 216),...  15.1 us
    ppermute x5, starting transfers between devices, row_permute(): return lax.ppermute(x, ROW, pairs)  11.5 us
    reshape x1, local copies, waits for them, and re-layouts, shards(): wtop, wright, wbot = site_forms(site_flat.reshape(1296, 1296))  7.97 us
    ppermute x5, waiting for transfers between devices, row_permute(): return lax.ppermute(x, ROW, pairs)  6.83 us
  transfers between devices with their start and end apart: 15, of which 5 were waited for; matrix products, arithmetic and copies ran while one was open for 14% of the time, Pallas kernels for 35%

profile of v1, /device:TPU:1, one launch (start us, length us, event | category | flops | bytes accessed | tf_op | source)
XLA Modules:
  0.0 149.3 jit_solution(8623497396224039837)
XLA Ops:
  0.6 0.7 copy.22
  1.3 0.1 reshape.184
  1.4 0.7 copy.23
  2.2 0.1 reshape.185
  2.3 3.9 %collective-permute-start = (bf16[16,216]{1,0:T(8,128)(2,1)S(1)}, bf16[16,216]{1,0:T(8,128)(2,1)S(1)}, u32[]{:S(2)}, u32[]{:S(2)}) collective-permute-start(bf16[16,216]{1,0:T(8,128)(2,1)S(1)} %pad_maximum_fusion.2), channel_id=1, source_target_pairs={{0,4},{1,5},{2,6},{3,7},{4,8},{5,9},{6,10},{7,11},{8,12},{9,13},{1... | collective-permute-start | bytes 20744 | tf_op jit(solution)/shard_map/ppermute | solution.py:168
  6.2 5.1 %collective-permute-start.1 = (bf16[16,216]{1,0:T(8,128)(2,1)S(1)}, bf16[16,216]{1,0:T(8,128)(2,1)S(1)}, u32[]{:S(2)}, u32[]{:S(2)}) collective-permute-start(bf16[16,216]{1,0:T(8,128)(2,1)S(1)} %pad_maximum_fusion.2), channel_id=1, source_target_pairs={{0,8},{1,9},{2,10},{3,11},{4,12},{5,13},{6,14},{7,15},{8,0},{9,1},... | collective-permute-start | bytes 20744 | tf_op jit(solution)/shard_map/ppermute | solution.py:168
  11.3 2.4 %collective-permute-start.2 = (bf16[16,216]{1,0:T(8,128)(2,1)S(1)}, bf16[16,216]{1,0:T(8,128)(2,1)S(1)}, u32[]{:S(2)}, u32[]{:S(2)}) collective-permute-start(bf16[16,216]{1,0:T(8,128)(2,1)S(1)} %pad_maximum_fusion.2), channel_id=1, source_target_pairs={{0,12},{1,13},{2,14},{3,15},{4,0},{5,1},{6,2},{7,3},{8,4},{9,5},{1... | collective-permute-start | bytes 20744 | tf_op jit(solution)/shard_map/ppermute | solution.py:168
  13.7 0.8 reshape.186
  14.4 0.8 reshape.187
  15.2 0.8 reshape.188
  16.0 0.8 concatenate.32
  16.9 0.0 collective-permute-done
  16.9 0.0 collective-permute-done.2
  16.9 1.3 collective-permute-start.3
  18.3 2.5 %collective-permute-start.4 = (bf16[64,216]{1,0:T(8,128)(2,1)S(1)}, bf16[64,216]{1,0:T(8,128)(2,1)S(1)}, u32[]{:S(2)}, u32[]{:S(2)}) collective-permute-start(bf16[64,216]{1,0:T(8,128)(2,1)S(1)} %get-tuple-element.34), channel_id=1, source_target_pairs={{0,2},{1,3},{2,0},{3,1},{4,6},{5,7},{6,4},{7,5},{8,10},{9,11},{10,... | collective-permute-start | bytes 82952 | tf_op jit(solution)/shard_map/ppermute | solution.py:168
  20.8 1.2 collective-permute-start.5
  21.9 0.7 collective-permute-done.4
  22.6 0.9 collective-permute-done.5
  23.6 0.3 convolution_convert_fusion.1
  23.8 0.0 copy-start.3
  23.8 0.6 constant_dynamic-update-slice_fusion.19
  24.5 0.6 constant_dynamic-update-slice_fusion.18
  25.1 0.8 collective-permute-start.6
  26.0 3.0 %collective-permute-done.6 = bf16[496,128]{1,0:T(8,128)(2,1)S(1)} collective-permute-done((bf16[496,128]{1,0:T(8,128)(2,1)S(1)}, bf16[496,128]{1,0:T(8,128)(2,1)S(1)}, u32[]{:S(2)}, u32[]{:S(2)}) %collective-permute-start.6) | collective-permute-done | bytes 127008 | tf_op jit(solution)/shard_map/ppermute | solution.py:159
  29.0 1.4 collective-permute-start.7
  30.4 2.7 %collective-permute-start.8 = (bf16[992,128]{1,0:T(8,128)(2,1)S(1)}, bf16[992,128]{1,0:T(8,128)(2,1)S(1)}, u32[]{:S(2)}, u32[]{:S(2)}) collective-permute-start(bf16[992,128]{1,0:T(8,128)(2,1)S(1)} %pad_maximum_fusion), channel_id=1, source_target_pairs={{0,128},{16,144},{32,160},{48,176},{64,192},{80,208},{96,224},{112... | collective-permute-start | bytes 761864 | tf_op jit(solution)/shard_map/ppermute | solution.py:159
  33.1 0.6 constant_dynamic-update-slice_fusion.17
  33.7 1.1 collective-permute-start.9
  34.8 0.7 constant_dynamic-update-slice_fusion.16
  35.5 0.0 collective-permute-done.7
  35.5 0.7 constant_dynamic-update-slice_fusion.15
  36.3 3.8 %collective-permute-done.8 = bf16[992,128]{1,0:T(8,128)(2,1)S(1)} collective-permute-done((bf16[992,128]{1,0:T(8,128)(2,1)S(1)}, bf16[992,128]{1,0:T(8,128)(2,1)S(1)}, u32[]{:S(2)}, u32[]{:S(2)}) %collective-permute-start.8) | collective-permute-done | bytes 253984 | tf_op jit(solution)/shard_map/ppermute | solution.py:159
  40.0 0.7 constant_dynamic-update-slice_fusion.14
  40.8 0.7 constant_dynamic-update-slice_fusion.13
  41.5 5.5 %collective-permute-start.10 = (bf16[3968,128]{1,0:T(8,128)(2,1)}, bf16[3968,128]{1,0:T(8,128)(2,1)S(1)}, u32[]{:S(2)}, u32[]{:S(2)}) collective-permute-start(bf16[3968,128]{1,0:T(8,128)(2,1)} %get-tuple-element.20), channel_id=1, source_target_pairs={{0,16},{16,0},{32,48},{48,32},{64,80},{80,64},{96,112},{112,96},{1... | collective-permute-start | bytes 3047432 | tf_op jit(solution)/shard_map/ppermute | solution.py:159
  47.0 0.7 reshape.195
  47.7 5.0 %all-to-all-start = ((bf16[16,6,216]{2,1,0:T(8,128)(2,1)}), bf16[16,6,216]{2,1,0:T(8,128)(2,1)S(1)}, u32[]{:S(2)}, u32[]{:S(2)}) async-start(bf16[16,6,216]{2,1,0:T(8,128)(2,1)} %bitcast.14), calls=%async_computation | async-start | bytes 131072 | tf_op jit(solution)/shard_map/all_to_all | solution.py:188
  52.7 3.9 %collective-permute-start.12 = (bf16[216,96]{0,1:T(8,128)(2,1)S(1)}, bf16[216,96]{0,1:T(8,128)(2,1)S(1)}, u32[]{:S(2)}, u32[]{:S(2)}) collective-permute-start(bf16[216,96]{0,1:T(8,128)(2,1)S(1)} %copy-done.4), channel_id=1, source_target_pairs={{0,0},{1,16},{2,32},{3,48},{4,64},{5,80},{6,96},{7,112},{8,128},{9... | collective-permute-start | bytes 124424 | tf_op jit(solution)/shard_map/ppermute | solution.py:173
  56.6 0.5 broadcast_multiply_fusion
  57.1 0.1 broadcast_in_dim.8
  57.2 0.1 mul.52
  57.3 8.0 %reshape.194.s_ref = bf16[1296,1296]{1,0:T(8,128)(2,1)} reshape(bf16[1679616]{0:T(1024)(128)(2,1)} %param.17) | data formatting | bytes 6718464 | tf_op jit(solution)/shard_map/reshape | solution.py:224
  65.3 21.7 %site.1 = (bf16[1296,1296]{1,0:T(8,128)(2,1)}, bf16[1296,1296]{1,0:T(8,128)(2,1)}, bf16[1296,1296]{1,0:T(8,128)(2,1)}) custom-call(bf16[1296,1296]{1,0:T(8,128)(2,1)} %reshape.194.s_ref), custom_call_target="tpu_custom_call" | custom-call | tf_op jit(solution)/shard_map/site/pallas_call | solution.py:145
  87.0 0.1 constant_dynamic-update-slice_fusion.20.buf_ref
  87.2 0.3 convolution_convert_fusion.small_ref
  87.5 1.9 %collective-permute-start.11 = (bf16[216,128]{1,0:T(8,128)(2,1)S(1)}, bf16[216,128]{1,0:T(8,128)(2,1)S(1)}, u32[]{:S(2)}, u32[]{:S(2)}) collective-permute-start(bf16[216,128]{1,0:T(8,128)(2,1)S(1)} %slice.28), channel_id=1, source_target_pairs={{0,0},{1,16},{2,32},{3,48},{4,64},{5,80},{6,96},{7,112},{8,128},{9... | collective-permute-start | bytes 165896 | tf_op jit(solution)/shard_map/ppermute | solution.py:173
  89.5 0.1 reshape.199
  89.6 0.7 reshape.200.bpr_ref
  90.2 2.7 %collective-permute-done.11.ber_ref = bf16[216,128]{1,0:T(8,128)(2,1)S(1)} collective-permute-done((bf16[216,128]{1,0:T(8,128)(2,1)S(1)}, bf16[216,128]{1,0:T(8,128)(2,1)S(1)}, u32[]{:S(2)}, u32[]{:S(2)}) %collective-permute-start.11) | collective-permute-done | bytes 55328 | tf_op jit(solution)/shard_map/ppermute | solution.py:173
  93.0 0.6 copy-done.2
  93.6 15.6 %left.1 = (bf16[216,216]{1,0:T(8,128)(2,1)}, f32[288,128]{1,0:T(8,128)}) custom-call(s32[16]{0:T(128)} %get-tuple-element.19.order_ref, bf16[7936,128]{1,0:T(8,128)(2,1)} %copy-done, bf16[1024,128]{1,0:T(8,128)(2,1)} %copy-done.1, bf16[216,128]{1,0:T(8,128)(2,1)} %copy-done.2, bf16[1296,1296]{1,0:T(8,128)(2,1)} %get-tuple-element.11.wtop_ref, ...), custom_call_target="tpu_custom_call" | custom-call | tf_op jit(solution)/shard_map/left/pallas_call | solution.py:106
  109.1 1.1 copy.29
  110.2 0.1 reshape.204
  110.4 0.7 copy.28
  111.1 19.7 %all-to-all-start.1 = ((f32[16,6,216]{2,1,0:T(8,128)}), f32[16,6,216]{2,1,0:T(8,128)S(1)}, u32[]{:S(2)}, u32[]{:S(2)}) async-start(f32[16,6,216]{2,1,0:T(8,128)} %copy.28), calls=%async_computation.1 | async-start | bytes 262144 | tf_op jit(solution)/shard_map/all_to_all | solution.py:230
  130.8 0.2 reshape.196
  131.0 0.1 reshape.197
  131.0 0.2 copy.30
  131.2 0.6 pad_bitcast_fusion.tpy_ref
  131.9 15.1 %upper.1 = (bf16[216,216]{1,0:T(8,128)(2,1)}, f32[240,8]{1,0:T(8,128)}) custom-call(s32[16]{0:T(128)} %get-tuple-element.19.order_ref, bf16[7936,128]{1,0:T(8,128)(2,1)} %copy-done, bf16[1024,128]{1,0:T(8,128)(2,1)} %copy-done.1, bf16[1296,1296]{1,0:T(8,128)(2,1)} %get-tuple-element.11.wtop_ref, bf16[1296,1296]{1,0:T(8,128)(2,1)} %get-tuple-element.12.wright_ref, ...), custom_call_target="tpu_custom_call" | custom-call | tf_op jit(solution)/shard_map/upper/pallas_call | solution.py:102
  147.0 0.9 convert.4
  147.9 0.1 copy.26
  148.0 0.7 convert_element_type.29
  148.7 0.6 reduce_sum.9
  (35 shorter events, 0.2 us)
Async XLA Ops:
  2.3 14.6 %collective-permute-start = (bf16[16,216]{1,0:T(8,128)(2,1)S(1)}, bf16[16,216]{1,0:T(8,128)(2,1)S(1)}, u32[]{:S(2)}, u32[]{:S(2)}) collective-permute-start(bf16[16,216]{1,0:T(8,128)(2,1)S(1)} %pad_maximum_fusion.2), channel_id=1, source_target_pairs={{0,4},{1,5},{2,6},{3,7},{4,8},{5,9},{6,10},{7,11},{8,12},{9,13},{1... | collective-permute-start | bytes 20744 | tf_op jit(solution)/shard_map/ppermute | solution.py:168
  6.2 10.7 %collective-permute-start.1 = (bf16[16,216]{1,0:T(8,128)(2,1)S(1)}, bf16[16,216]{1,0:T(8,128)(2,1)S(1)}, u32[]{:S(2)}, u32[]{:S(2)}) collective-permute-start(bf16[16,216]{1,0:T(8,128)(2,1)S(1)} %pad_maximum_fusion.2), channel_id=1, source_target_pairs={{0,8},{1,9},{2,10},{3,11},{4,12},{5,13},{6,14},{7,15},{8,0},{9,1},... | collective-permute-start | bytes 20744 | tf_op jit(solution)/shard_map/ppermute | solution.py:168
  11.3 5.7 %collective-permute-start.2 = (bf16[16,216]{1,0:T(8,128)(2,1)S(1)}, bf16[16,216]{1,0:T(8,128)(2,1)S(1)}, u32[]{:S(2)}, u32[]{:S(2)}) collective-permute-start(bf16[16,216]{1,0:T(8,128)(2,1)S(1)} %pad_maximum_fusion.2), channel_id=1, source_target_pairs={{0,12},{1,13},{2,14},{3,15},{4,0},{5,1},{6,2},{7,3},{8,4},{9,5},{1... | collective-permute-start | bytes 20744 | tf_op jit(solution)/shard_map/ppermute | solution.py:168
  16.9 5.0 %collective-permute-start.3 = (bf16[64,216]{1,0:T(8,128)(2,1)S(1)}, bf16[64,216]{1,0:T(8,128)(2,1)S(1)}, u32[]{:S(2)}, u32[]{:S(2)}) collective-permute-start(bf16[64,216]{1,0:T(8,128)(2,1)S(1)} %get-tuple-element.34), channel_id=1, source_target_pairs={{0,1},{1,2},{2,3},{3,0},{4,5},{5,6},{6,7},{7,4},{8,9},{9,10},{10,1... | collective-permute-start | bytes 82952 | tf_op jit(solution)/shard_map/ppermute | solution.py:168
  18.3 4.4 %collective-permute-start.4 = (bf16[64,216]{1,0:T(8,128)(2,1)S(1)}, bf16[64,216]{1,0:T(8,128)(2,1)S(1)}, u32[]{:S(2)}, u32[]{:S(2)}) collective-permute-start(bf16[64,216]{1,0:T(8,128)(2,1)S(1)} %get-tuple-element.34), channel_id=1, source_target_pairs={{0,2},{1,3},{2,0},{3,1},{4,6},{5,7},{6,4},{7,5},{8,10},{9,11},{10,... | collective-permute-start | bytes 82952 | tf_op jit(solution)/shard_map/ppermute | solution.py:168
  20.8 2.8 %collective-permute-start.5 = (bf16[64,216]{1,0:T(8,128)(2,1)S(1)}, bf16[64,216]{1,0:T(8,128)(2,1)S(1)}, u32[]{:S(2)}, u32[]{:S(2)}) collective-permute-start(bf16[64,216]{1,0:T(8,128)(2,1)S(1)} %get-tuple-element.34), channel_id=1, source_target_pairs={{0,3},{1,0},{2,1},{3,2},{4,7},{5,4},{6,5},{7,6},{8,11},{9,8},{10,9... | collective-permute-start | bytes 82952 | tf_op jit(solution)/shard_map/ppermute | solution.py:168
  23.8 23.2 %copy-start.3 = (bf16[216,96]{0,1:T(8,128)(2,1)S(1)}, bf16[216,96]{0,1:T(8,128)(2,1)}, u32[]{:S(2)}) copy-start(bf16[216,96]{0,1:T(8,128)(2,1)} %param.18) | copy-start | bytes 124420
  24.5 28.2 %copy-start.4 = (bf16[216,96]{0,1:T(8,128)(2,1)S(1)}, bf16[216,96]{0,1:T(8,128)(2,1)}, u32[]{:S(2)}) copy-start(bf16[216,96]{0,1:T(8,128)(2,1)} %param.19) | copy-start | bytes 124420
  25.1 3.9 %collective-permute-start.6 = (bf16[496,128]{1,0:T(8,128)(2,1)S(1)}, bf16[496,128]{1,0:T(8,128)(2,1)S(1)}, u32[]{:S(2)}, u32[]{:S(2)}) collective-permute-start(bf16[496,128]{1,0:T(8,128)(2,1)S(1)} %pad_maximum_fusion.1), channel_id=1, source_target_pairs={{0,32},{16,48},{32,0},{48,16},{64,96},{80,112},{96,64},{112,80},{1... | collective-permute-start | bytes 380936 | tf_op jit(solution)/shard_map/ppermute | solution.py:159
  29.0 6.5 %collective-permute-start.7 = (bf16[992,128]{1,0:T(8,128)(2,1)S(1)}, bf16[992,128]{1,0:T(8,128)(2,1)S(1)}, u32[]{:S(2)}, u32[]{:S(2)}) collective-permute-start(bf16[992,128]{1,0:T(8,128)(2,1)S(1)} %pad_maximum_fusion), channel_id=1, source_target_pairs={{0,64},{16,80},{32,96},{48,112},{64,128},{80,144},{96,160},{112,17... | collective-permute-start | bytes 761864 | tf_op jit(solution)/shard_map/ppermute | solution.py:159
  30.4 9.6 %collective-permute-start.8 = (bf16[992,128]{1,0:T(8,128)(2,1)S(1)}, bf16[992,128]{1,0:T(8,128)(2,1)S(1)}, u32[]{:S(2)}, u32[]{:S(2)}) collective-permute-start(bf16[992,128]{1,0:T(8,128)(2,1)S(1)} %pad_maximum_fusion), channel_id=1, source_target_pairs={{0,128},{16,144},{32,160},{48,176},{64,192},{80,208},{96,224},{112... | collective-permute-start | bytes 761864 | tf_op jit(solution)/shard_map/ppermute | solution.py:159
  33.7 7.0 %collective-permute-start.9 = (bf16[992,128]{1,0:T(8,128)(2,1)S(1)}, bf16[992,128]{1,0:T(8,128)(2,1)S(1)}, u32[]{:S(2)}, u32[]{:S(2)}) collective-permute-start(bf16[992,128]{1,0:T(8,128)(2,1)S(1)} %pad_maximum_fusion), channel_id=1, source_target_pairs={{0,192},{16,208},{32,224},{48,240},{64,0},{80,16},{96,32},{112,48}... | collective-permute-start | bytes 761864 | tf_op jit(solution)/shard_map/ppermute | solution.py:159
  41.5 45.5 %collective-permute-start.10 = (bf16[3968,128]{1,0:T(8,128)(2,1)}, bf16[3968,128]{1,0:T(8,128)(2,1)S(1)}, u32[]{:S(2)}, u32[]{:S(2)}) collective-permute-start(bf16[3968,128]{1,0:T(8,128)(2,1)} %get-tuple-element.20), channel_id=1, source_target_pairs={{0,16},{16,0},{32,48},{48,32},{64,80},{80,64},{96,112},{112,96},{1... | collective-permute-start | bytes 3047432 | tf_op jit(solution)/shard_map/ppermute | solution.py:159
  47.7 63.4 %all-to-all-start = ((bf16[16,6,216]{2,1,0:T(8,128)(2,1)}), bf16[16,6,216]{2,1,0:T(8,128)(2,1)S(1)}, u32[]{:S(2)}, u32[]{:S(2)}) async-start(bf16[16,6,216]{2,1,0:T(8,128)(2,1)} %bitcast.14), calls=%async_computation | async-start | bytes 131072 | tf_op jit(solution)/shard_map/all_to_all | solution.py:188
  52.7 36.8 %collective-permute-start.12 = (bf16[216,96]{0,1:T(8,128)(2,1)S(1)}, bf16[216,96]{0,1:T(8,128)(2,1)S(1)}, u32[]{:S(2)}, u32[]{:S(2)}) collective-permute-start(bf16[216,96]{0,1:T(8,128)(2,1)S(1)} %copy-done.4), channel_id=1, source_target_pairs={{0,0},{1,16},{2,32},{3,48},{4,64},{5,80},{6,96},{7,112},{8,128},{9... | collective-permute-start | bytes 124424 | tf_op jit(solution)/shard_map/ppermute | solution.py:173
  87.1 5.8 %copy-start = (bf16[7936,128]{1,0:T(8,128)(2,1)}, bf16[7936,128]{1,0:T(8,128)(2,1)S(1)}, u32[]{:S(2)}) copy-start(bf16[7936,128]{1,0:T(8,128)(2,1)S(1)} %constant_dynamic-update-slice_fusion.20.buf_ref) | copy-start | bytes 6094852
  87.4 5.5 %copy-start.1 = (bf16[1024,128]{1,0:T(8,128)(2,1)}, bf16[1024,128]{1,0:T(8,128)(2,1)S(1)}, u32[]{:S(2)}) copy-start(bf16[1024,128]{1,0:T(8,128)(2,1)S(1)} %convolution_convert_fusion.small_ref) | copy-start | bytes 786436
  87.5 5.5 %collective-permute-start.11 = (bf16[216,128]{1,0:T(8,128)(2,1)S(1)}, bf16[216,128]{1,0:T(8,128)(2,1)S(1)}, u32[]{:S(2)}, u32[]{:S(2)}) collective-permute-start(bf16[216,128]{1,0:T(8,128)(2,1)S(1)} %slice.28), channel_id=1, source_target_pairs={{0,0},{1,16},{2,32},{3,48},{4,64},{5,80},{6,96},{7,112},{8,128},{9... | collective-permute-start | bytes 165896 | tf_op jit(solution)/shard_map/ppermute | solution.py:173
  92.9 0.6 copy-start.2
  111.1 37.6 %all-to-all-start.1 = ((f32[16,6,216]{2,1,0:T(8,128)}), f32[16,6,216]{2,1,0:T(8,128)S(1)}, u32[]{:S(2)}, u32[]{:S(2)}) async-start(f32[16,6,216]{2,1,0:T(8,128)} %copy.28), calls=%async_computation.1 | async-start | bytes 262144 | tf_op jit(solution)/shard_map/all_to_all | solution.py:230

commit v2 on v1

v2 whole, which is shorter than its diff:
```python
import jax
import jax.numpy as jnp
from jax import lax
from jax.experimental import pallas as pl
from jax.experimental.pallas import tpu as pltpu
from jax.sharding import PartitionSpec as P

F = jnp.float32
B = jnp.bfloat16
NN = (((1,), (0,)), ((), ()))
NT = (((1,), (1,)), ((), ()))
VM = pl.BlockSpec(memory_space=pltpu.VMEM)
SM = pl.BlockSpec(memory_space=pltpu.SMEM)
BLOCK = 512
WIDE = 3456


def dot(x, y, dims=NN):
    return lax.dot_general(x, y, dims, preferred_element_type=F)


def shape_of(*dims, kind=B):
    return jax.ShapeDtypeStruct(dims, kind)


def params(mib):
    return pltpu.CompilerParams(vmem_limit_bytes=mib << 20)


def work(flops):
    return pl.CostEstimate(flops=flops, transcendentals=0, bytes_accessed=1 << 22)


def prepare_kernel(te, re, be, le, uct, rct, lct, piece, pack):
    zero = jnp.zeros((2, 216), B)
    for n, e in ((0, te), (1, le)):
        v = e[...].astype(F)
        piece[8 * n:8 * n + 8, :] = jnp.concatenate(
            [jnp.concatenate([v[i] for i in range(6)], axis=1).astype(B), zero], axis=0)
    parts = []
    for e in (te, re, be):
        v = e[...].astype(F)
        parts.append(jnp.concatenate([v[:, j, :] for j in range(6)], axis=1))
    for c in (uct, rct, lct):
        parts.append(c[...].astype(F))
    flat = jnp.concatenate(parts + [jnp.zeros((6, 88), F)], axis=1)
    flat = jnp.concatenate([flat, jnp.zeros((2, 1024), F)], axis=0).astype(B)
    for k in range(8):
        pack[8 * k:8 * k + 8, :] = flat[:, 128 * k:128 * k + 128]


def expand(order_ref, bufs, off, dst):
    for rel in range(16):
        at = pl.multiple_of(order_ref[rel] * 216, 8)
        start = (rel % 2) * BLOCK + off
        dst[pl.ds(at, 216), :] = bufs[rel // 2][start:start + 216, :].astype(F)


def gather_small_kernel(order_ref, *refs):
    bufs = refs[:8]
    out_ref, packs = refs[8:]
    for rel in range(16):
        at = pl.multiple_of(order_ref[rel] * 8, 8)
        start = (rel % 2) * BLOCK + 432
        for k in range(10):
            packs[k, pl.ds(at, 8), :] = bufs[rel // 2][start + 8 * k:start + 8 * k + 8, :].astype(F)
    row = lax.broadcasted_iota(jnp.int32, (128, 128), 0)
    lane = lax.broadcasted_iota(jnp.int32, (128, 128), 1)
    place = ((row % 8 < 6) & (lane == (row // 8) * 6 + row % 8)).astype(B)
    for k in range(10):
        out_ref[k * 128:(k + 1) * 128, :] = dot(jnp.transpose(packs[k]).astype(B), place).astype(B)


def gather_small(order, bufs):
    return pl.pallas_call(gather_small_kernel, out_shape=shape_of(1280, 128), in_specs=[SM] + [VM] * 8, out_specs=VM,
                          scratch_shapes=[pltpu.VMEM((10, 128, 128), F)], name="gather_small",
                          compiler_params=params(6))(order, *bufs)


def to_bf16(src, dst, rows):
    def f(i, _):
        at = pl.multiple_of(i * 48, 16)
        for a in range(6):
            dst[pl.ds(at, 48), a * 128:(a + 1) * 128] = src[a, pl.ds(at, 48), :].astype(B)
        return 0
    lax.fori_loop(0, rows // 48, f, 0)


def big(w_ref, p_ref, k, o_ref):
    def f(i, _):
        at = pl.multiple_of(i * 432, 16)
        res = dot(w_ref[pl.ds(at, 432), :], p_ref[:k, :])
        for a in range(6):
            o_ref[a, pl.ds(at, 432), :] = res[:, a * 128:(a + 1) * 128]
        return 0
    lax.fori_loop(0, 3, f, 0)
    o_ref[:, 1296:1440, :] = jnp.zeros((6, 144, 128), F)


def padded(x):
    return jnp.concatenate([x, jnp.zeros((x.shape[0], 32), F)], axis=1)


def clear_gaps(pf):
    for q in range(12):
        pf[:, q * 128 + 108:(q + 1) * 128, :] = jnp.zeros((6, 20, 128), F)


def compressed(x):
    return jnp.concatenate([x[:, g * 40:g * 40 + 36] for g in range(6)], axis=1)


def upper_kernel(order_ref, *refs):
    bufs = refs[:8]
    small_ref, wtop_ref, wright_ref, out_ref, ct_ref, tef, pf, p1, p3, o1, o3, tps = refs[8:]
    expand(order_ref, bufs, 0, tef)
    uc = small_ref[648:744, :]
    rc = small_ref[744:840, :]
    tps[0:216, :] = small_ref[1024:1240, :].astype(F)
    tps[216:320, :] = jnp.zeros((104, 128), F)
    lu = dot(bufs[0][216:432, :][:, :96], uc).astype(B)[:, :96]
    ar = dot(small_ref[216:432, :], rc, NT).astype(B)
    for v in range(36):
        te = tef[pl.ds(v, 96, stride=36), :].astype(B)
        d1 = dot(lu, te)
        for a in range(6):
            pf[a, v * 36:(v + 1) * 36, :] = d1[a * 36:(a + 1) * 36, :]
    to_bf16(pf, p1, 1296)
    clear_gaps(pf)
    for v in range(36):
        te = tef[pl.ds(v, 96, stride=36), :].astype(B)
        d3 = padded(dot(ar, te[:, :96], NT))
        at = (v // 3) * 128 + (v % 3) * 36
        for a in range(6):
            pf[a, at:at + 36, :] = d3[a * 36:(a + 1) * 36, :]
    to_bf16(pf, p3, 1536)
    big(wtop_ref, p1, 1296, o1)
    big(wright_ref, p3, 1536, o3)
    acc = jnp.zeros((240, 256), F)
    for tp in range(18):
        xs = []
        ys = []
        for t in (2 * tp, 2 * tp + 1):
            xs.append(jnp.concatenate([o1[a, pl.ds(t, 40, stride=36), :] for a in range(6)], axis=0).astype(B))
            ys.append(jnp.concatenate([o3[g, pl.ds(t, 40, stride=36), :] for g in range(6)]
                                      + [tps[pl.ds(t, 8, stride=36), :], jnp.zeros((8, 128), F)], axis=0).astype(B))
        acc = acc + dot(jnp.concatenate(xs, axis=1), jnp.concatenate(ys, axis=1), NT)
    up = compressed(acc[:, :240] * jnp.float32(WIDE ** -0.5))
    for a in range(6):
        out_ref[a * 36:(a + 1) * 36, :] = up[a * 40:a * 40 + 36, :].astype(B)
    ct = jnp.transpose(acc[:, 128:256])[112:120, :]
    ct_ref[...] = compressed(ct)[0:6, :].astype(B)


def left_kernel(order_ref, *refs):
    bufs = refs[:8]
    small_ref, ber_ref, wtop_ref, wbot_ref, bpr_ref, out_ref, cb_ref, lef, pf, p2, p4, o2, o4, cbs, abf = refs[8:]
    expand(order_ref, bufs, 216, lef)
    uc = small_ref[648:744, :]
    lc = small_ref[840:936, :]
    at = dot(small_ref[0:216, :], uc, NT).astype(B)
    abf[...] = padded(dot(ber_ref[...], lc, NT))
    ab = jnp.concatenate([abf[pl.ds(b * 36 + h, 12, stride=3), :] for b in range(6) for h in range(3)], axis=0).astype(B)[:, :96]
    for u in range(36):
        le = lef[pl.ds(u, 96, stride=36), :].astype(B)
        d2 = padded(dot(at, le[:, :96], NT))
        for b in range(6):
            pf[b, pl.ds(u, 36, stride=36), :] = d2[b * 36:(b + 1) * 36, :]
    to_bf16(pf, p2, 1296)
    clear_gaps(pf)
    for u in range(36):
        le = lef[pl.ds(u, 96, stride=36), :].astype(B)
        d4 = dot(ab, le)
        for b in range(6):
            for h in range(3):
                pf[b, pl.ds(h * 36 + u, 12, stride=128), :] = d4[b * 36 + h * 12:b * 36 + h * 12 + 12, :]
    to_bf16(pf, p4, 1536)
    big(wtop_ref, p2, 1296, o2)
    big(wbot_ref, p4, 1536, o4)
    acc = jnp.zeros((240, 240), F)
    for sp in range(18):
        xs = []
        ys = []
        for s in (2 * sp, 2 * sp + 1):
            x = jnp.concatenate([o2[b, s * 36:s * 36 + 40, :] for b in range(6)], axis=0).astype(B)
            y = jnp.concatenate([o4[b, s * 36:s * 36 + 40, :] for b in range(6)], axis=0).astype(B)
            xs.append(x)
            ys.append(y)
            cbs[pl.ds(s, 8, stride=36), :] = dot(bpr_ref[...], y)
        acc = acc + dot(jnp.concatenate(xs, axis=1), jnp.concatenate(ys, axis=1), NT)
    lh = compressed(acc * jnp.float32(WIDE ** -0.5))
    for a in range(6):
        out_ref[a * 36:(a + 1) * 36, :] = lh[a * 40:a * 40 + 36, :].astype(B)
    cb_ref[...] = cbs[0:216, :]


def scratch():
    return [pltpu.VMEM((WIDE, 128), F), pltpu.VMEM((6, 1536, 128), F), pltpu.VMEM((1536, 768), B),
            pltpu.VMEM((1536, 768), B), pltpu.VMEM((6, 1440, 128), F), pltpu.VMEM((6, 1440, 128), F)]


def prepare(te, re, be, le, uct, rct, lct):
    return pl.pallas_call(prepare_kernel, out_shape=(shape_of(16, 216), shape_of(64, 128)), in_specs=[VM] * 7,
                          out_specs=(VM, VM), name="prepare", compiler_params=params(4))(te, re, be, le, uct, rct, lct)


def upper(order, bufs, small, wtop, wright):
    return pl.pallas_call(
        upper_kernel, out_shape=(shape_of(216, 216), shape_of(6, 216)), in_specs=[SM] + [VM] * 11, out_specs=(VM, VM),
        scratch_shapes=scratch() + [pltpu.VMEM((320, 128), F)], name="upper", compiler_params=params(23),
        cost_estimate=work(8 << 30))(order, *bufs, small, wtop, wright)


def left(order, bufs, small, ber, wtop, wbot, bpr):
    return pl.pallas_call(
        left_kernel, out_shape=(shape_of(216, 216), shape_of(216, 128, kind=F)), in_specs=[SM] + [VM] * 13,
        out_specs=(VM, VM), scratch_shapes=scratch() + [pltpu.VMEM((288, 128), F), pltpu.VMEM((216, 128), F)], name="left",
        compiler_params=params(23), cost_estimate=work(8 << 30))(order, *bufs, small, ber, wtop, wbot, bpr)


def finish_kernel(at_ref, own, one, two, three, out_ref):
    total = (own[...] + one[...] + two[...] + three[...]).astype(B)
    lane = lax.broadcasted_iota(jnp.int32, (8, 128), 1)
    pick = (lane == at_ref[0] + lax.broadcasted_iota(jnp.int32, (8, 128), 0)).astype(B)
    res = dot(pick, total, NT)
    rows = [jnp.concatenate([res[a:a + 1, x * 36:(x + 1) * 36] for a in range(6)], axis=1) for x in range(6)]
    out_ref[...] = jnp.concatenate(rows, axis=0).astype(B)


def finish(at, *parts):
    return pl.pallas_call(finish_kernel, out_shape=shape_of(6, 216), in_specs=[SM] + [VM] * 4, out_specs=VM,
                          name="finish", compiler_params=params(4))(at, *parts)


def lanes_shifted(a_ref, z_ref, pair):
    tile = (pair * 72) // 128
    base = pl.multiple_of(tile * 128, 128)
    off = pair * 72 - tile * 128
    k = lax.broadcasted_iota(jnp.int32, (256, 256), 0)
    n = lax.broadcasted_iota(jnp.int32, (256, 256), 1)
    w = n % 128
    sel = ((k == off + (n // 128) * 36 + w % 36) & (w < 108)).astype(B)
    z_ref[...] = dot(a_ref[:, pl.ds(base, 256)], sel)


def realign(a_ref, z_ref, o_ref):
    lane = lax.broadcasted_iota(jnp.int32, (36, 128), 1)

    def f(g, _):
        strips = []
        for h in range(2):
            lanes_shifted(a_ref, z_ref.at[h], 2 * g + h)
        for h in range(2):
            for q in range(2):
                tiles = []
                for m in range(12):
                    z = [z_ref[h, (3 * m + e) * 36:(3 * m + e + 1) * 36, q * 128:(q + 1) * 128] for e in range(3)]
                    tiles.append(jnp.where(lane < 36, z[0], jnp.where(lane < 72, z[1], z[2])))
                strips.append(jnp.concatenate(tiles, axis=1))
        at = pl.multiple_of(g * 144, 16)
        o_ref[pl.ds(at, 144), :] = jnp.concatenate(strips, axis=0).astype(B)
        return 0
    lax.fori_loop(0, 9, f, 0)


def right_form_kernel(s_ref, wright_ref, apad, z):
    apad[:, 1296:1408] = jnp.zeros((1296, 112), B)
    apad[:, :1296] = s_ref[...]
    realign(apad, z, wright_ref)


def left_forms_kernel(s_ref, wtop_ref, wbot_ref, apad, z):
    eye = (lax.broadcasted_iota(jnp.int32, (128, 128), 0) == lax.broadcasted_iota(jnp.int32, (128, 128), 1)).astype(B)
    for b in range(11):
        n = min(128, 1296 - b * 128)
        res = dot(eye[:n, :n], s_ref[:, b * 128:b * 128 + n], NT).astype(B)
        wtop_ref[b * 128:b * 128 + n, :] = res
        apad[b * 128:b * 128 + n, :1296] = res
    apad[:, 1296:1408] = jnp.zeros((1296, 112), B)
    realign(apad, z, wbot_ref)


def form_scratch():
    return [pltpu.VMEM((1296, 1408), B), pltpu.VMEM((2, 1296, 256), F)]


def right_form(s2):
    return pl.pallas_call(right_form_kernel, out_shape=shape_of(1296, 1536), in_specs=[VM], out_specs=VM,
                          scratch_shapes=form_scratch(), name="right_form", compiler_params=params(9),
                          cost_estimate=work(3 << 30))(s2)


def left_forms(s2):
    return pl.pallas_call(left_forms_kernel, out_shape=(shape_of(1296, 1296), shape_of(1296, 1536)), in_specs=[VM],
                          out_specs=(VM, VM), scratch_shapes=form_scratch(), name="left_forms", compiler_params=params(9),
                          cost_estimate=work(4 << 30))(s2)


ROW, COL = "row", "col"


def row_permute(x, move):
    pairs = []
    for y in range(4):
        for z in range(2):
            for k in range(2):
                a, b, c = move(y, z, k)
                pairs.append((y * 4 + z * 2 + k, a * 4 + b * 2 + c))
    return lax.ppermute(x, ROW, pairs)


def col_permute(x, move):
    pairs = []
    for z in range(4):
        for i in range(4):
            a, b = move(z, i)
            pairs.append((z * 4 + i, a * 4 + b))
    return lax.ppermute(x, COL, pairs)


def swap_axes(x):
    pairs = [(r * 16 + c, c * 16 + r) for r in range(16) for c in range(16)]
    return lax.ppermute(x, (ROW, COL), pairs)


def stacked(own, received):
    return jnp.concatenate([own, *received], axis=0)


def other_core(x):
    return row_permute(x, lambda a, b, k: (a, b, 1 - k))


def other_z(x):
    return row_permute(x, lambda a, b, k: (a, 1 - b, k))


def along_y(x, s):
    return row_permute(x, lambda a, b, k: ((a + s) % 4, b, k))


def shards(uc, rc, lc, te, re, be, le, site_flat, tp, bp):
    r = lax.axis_index(ROW)
    c = lax.axis_index(COL)
    y, zlo, core = r // 4, (r // 2) % 2, r % 2
    zhi, x = c // 4, c % 4
    hold = lax.optimization_barrier

    piece, pack = prepare(te, re, be, le, uc.T, rc.T, lc.T)
    s2 = site_flat.reshape(1296, 1296)

    projectors = swap_axes(jnp.concatenate([tp, bp], axis=1))

    got = [col_permute(piece, lambda z, i, s=s: ((z + s) % 4, i)) for s in (1, 2, 3)]
    *got, s2 = hold((*got, s2))
    piece = stacked(piece, got)
    piece = stacked(piece, [col_permute(piece, lambda z, i, s=s: (z, (i + s) % 4)) for s in (1, 2, 3)])
    at = jnp.arange(256)
    x_rel, z_rel, edge, j = at // 64, (at // 16) % 4, (at // 8) % 2, at % 8
    block = ((zhi - z_rel) % 4) * 4 + (x - x_rel) % 4
    target = jnp.where(j < 6, edge * 128 + block * 6 + j, -1)
    place = (target[:, None] == jnp.arange(256)[None, :]).astype(B)
    rows = lax.dot_general(piece, place, (((0,), (0,)), ((), ())), preferred_element_type=F).astype(B)

    tpx = lax.dynamic_slice_in_dim(projectors, c * 6, 6, 1)
    tpx = tpx.reshape(6, 36, 6).transpose(0, 2, 1).reshape(6, 216)
    tpx = jnp.pad(tpx, ((0, 2), (0, 40))).reshape(8, 2, 128).transpose(1, 0, 2).reshape(16, 128)
    bpr = lax.dynamic_slice_in_dim(projectors, 96 + c * 6, 6, 1).T.reshape(6, 6, 36)
    bpr = jnp.pad(bpr, ((0, 2), (0, 0), (0, 4))).reshape(8, 240)
    own = jnp.concatenate([rows[:, :128], rows[:, 128:], pack, tpx], axis=0)
    near = stacked(own, [other_z(own)])
    far = [along_y(near, s) for s in (1, 2, 3)]
    near_twin = other_core(near)
    wtop, wbot = left_forms(hold((s2, near))[0])
    *far, near_twin, wtop = hold((*far, near_twin, wtop))
    far_twin = [other_core(f) for f in far]
    bufs = [near, *far, near_twin, *far_twin]
    rel = jnp.arange(16)
    order = ((y - (rel // 2) % 4) % 4) * 4 + (zlo ^ (rel % 2)) * 2 + (core ^ (rel // 8))
    order = order.astype(jnp.int32)

    small = gather_small(order, bufs)
    ber = swap_axes(small[432:648])

    lf, cb = left(order, bufs, small, ber, wtop, wbot, bpr)
    cb = cb + other_core(cb)
    cb_z = other_z(cb)
    wright = right_form(hold((s2, cb))[0])
    cb_z, wright = hold((cb_z, wright))
    cb = cb + cb_z
    cb_y = [along_y(cb, s) for s in (1, 2, 3)]
    order = hold((order, cb))[0]
    up, corner_top = upper(order, bufs, small, wtop, wright)
    *cb_y, up = hold((*cb_y, up))
    corner_bottom = finish((r * 6).astype(jnp.int32).reshape(1), cb, *cb_y)
    return up, lf, corner_top, corner_bottom


def solution(mesh):
    placed = (
        P(None, ROW),
        P(None, ROW),
        P(None, ROW),
        P(ROW, COL, None),
        P(ROW, COL, None),
        P(ROW, COL, None),
        P(ROW, COL, None),
        P(),
        P(COL, None),
        P(COL, None),
    )
    return jax.shard_map(
        shards,
        mesh=mesh,
        in_specs=placed,
        out_specs=(P(ROW, COL), P(COL, ROW), P(COL, ROW), P(COL, ROW)),
        check_vma=False,
    )
```

time: 150 us -> 125 us (0.83)
  Pallas kernels: 52.4 us -> 40.4 us
  starting transfers between devices: 58.3 us -> 46.8 us
  waiting for transfers between devices: 11.2 us -> 9.63 us
  local copies, waits for them, and re-layouts: 23.8 us -> 25.3 us
    all_to_all x2 -> x0, starting transfers between devices: 24.7 us -> none  [the longest x1 19.7 us: shards(): lax.all_to_all(part, ROW, 0, 0, tiled=True)]
    pallas_call x3 -> x7, Pallas kernels: 52.4 us -> 40.4 us  [the longest x1 14.4 us: left(): pl.pallas_call(left_kernel, out_shape=(shape_of(216, 216), shape_of(216,...]
    ppermute x5 -> x13, starting transfers between devices: 11.5 us -> 23.2 us  [row_permute(): return lax.ppermute(x, ROW, pairs)]
    unnamed x25 -> x36, local copies, waits for them, and re-layouts: 5.94 us -> 16.9 us
    reshape x15 -> x5, local copies, waits for them, and re-layouts: 13 us -> 8.24 us  [the longest x1 7.97 us: shards(): s2 = site_flat.reshape(1296, 1296)]
    ppermute x2, starting transfers between devices: 5.83 us -> 7.83 us  [swap_axes(): return lax.ppermute(x, (ROW, COL), pairs)]
    ppermute x5 -> x13, waiting for transfers between devices: 6.83 us -> 5.74 us  [row_permute(): return lax.ppermute(x, ROW, pairs)]
  transfers between devices with their start and end apart: 15 -> 21, of which waited for: 5 -> 9; matrix products, arithmetic and copies ran while one was open for 14% -> 8% of each run, Pallas kernels for 35% -> 19%
where the time goes in v2:
time: 125 us; the launch traced here: 124 us
  starting transfers between devices  46.8 us (37%)
  Pallas kernels  40.4 us (32%)
  local copies, waits for them, and re-layouts  25.3 us (20%)
  waiting for transfers between devices  9.63 us (8%)
    ppermute x13, starting transfers between devices, row_permute(): return lax.ppermute(x, ROW, pairs)  23.2 us
    unnamed x36, local copies, waits for them, and re-layouts  16.9 us
    ppermute x6, starting transfers between devices, col_permute(): return lax.ppermute(x, COL, pairs)  15.8 us
    pallas_call x1, Pallas kernels, left(): pl.pallas_call(left_kernel, out_shape=(shape_of(216, 216), shape_of(216,...  14.4 us
    pallas_call x1, Pallas kernels, upper(): pl.pallas_call(upper_kernel, out_shape=(shape_of(216, 216), shape_of(6, 2...  11.9 us
    reshape x1, local copies, waits for them, and re-layouts, shards(): s2 = site_flat.reshape(1296, 1296)  7.97 us
    ppermute x2, starting transfers between devices, swap_axes(): return lax.ppermute(x, (ROW, COL), pairs)  7.83 us
    pallas_call x1, Pallas kernels, left_forms(): pl.pallas_call(left_forms_kernel, out_shape=(shape_of(1296, 1296), shape_...  6.54 us
  transfers between devices with their start and end apart: 21, of which 9 were waited for; matrix products, arithmetic and copies ran while one was open for 8% of the time, Pallas kernels for 19%

profile of v2, /device:TPU:1, one launch (start us, length us, event | category | flops | bytes accessed | tf_op | source)
XLA Modules:
  0.0 124.2 jit_solution(3954789659832242035)
XLA Ops:
  0.6 0.7 copy-done.2
  1.3 0.7 copy-done.3
  2.1 0.7 copy-done.4
  2.8 0.7 copy-done.5
  3.5 0.7 copy-done.6
  4.1 0.7 copy-done.7
  4.8 0.7 copy-done.8
  5.5 0.2 prepare.1
  5.7 3.8 %collective-permute-start = (bf16[16,216]{1,0:T(8,128)(2,1)S(1)}, bf16[16,216]{1,0:T(8,128)(2,1)S(1)}, u32[]{:S(2)}, u32[]{:S(2)}) collective-permute-start(bf16[16,216]{1,0:T(8,128)(2,1)S(1)} %get-tuple-element.30), channel_id=1, source_target_pairs={{0,4},{1,5},{2,6},{3,7},{4,8},{5,9},{6,10},{7,11},{8,12},{9,13},{1... | collective-permute-start | bytes 20744 | tf_op jit(solution)/shard_map/ppermute | solution.py:318
  9.5 5.1 %collective-permute-start.1 = (bf16[16,216]{1,0:T(8,128)(2,1)S(1)}, bf16[16,216]{1,0:T(8,128)(2,1)S(1)}, u32[]{:S(2)}, u32[]{:S(2)}) collective-permute-start(bf16[16,216]{1,0:T(8,128)(2,1)S(1)} %get-tuple-element.30), channel_id=1, source_target_pairs={{0,8},{1,9},{2,10},{3,11},{4,12},{5,13},{6,14},{7,15},{8,0},{9,1},... | collective-permute-start | bytes 20744 | tf_op jit(solution)/shard_map/ppermute | solution.py:318
  14.6 2.4 %collective-permute-start.2 = (bf16[16,216]{1,0:T(8,128)(2,1)S(1)}, bf16[16,216]{1,0:T(8,128)(2,1)S(1)}, u32[]{:S(2)}, u32[]{:S(2)}) collective-permute-start(bf16[16,216]{1,0:T(8,128)(2,1)S(1)} %get-tuple-element.30), channel_id=1, source_target_pairs={{0,12},{1,13},{2,14},{3,15},{4,0},{5,1},{6,2},{7,3},{8,4},{9,5},{1... | collective-permute-start | bytes 20744 | tf_op jit(solution)/shard_map/ppermute | solution.py:318
  17.0 0.8 pad_maximum_fusion.1
  17.8 4.5 %collective-permute-start.6 = (bf16[216,192]{0,1:T(8,128)(2,1)S(1)}, bf16[216,192]{0,1:T(8,128)(2,1)S(1)}, u32[]{:S(2)}, u32[]{:S(2)}) collective-permute-start(bf16[216,192]{0,1:T(8,128)(2,1)S(1)} %pad_maximum_fusion.1), channel_id=1, source_target_pairs={{0,0},{1,16},{2,32},{3,48},{4,64},{5,80},{6,96},{7,112},{8,128},{9... | collective-permute-start | bytes 248840 | tf_op jit(solution)/shard_map/ppermute | solution.py:323
  22.4 8.0 %reshape.122.s_ref = bf16[1296,1296]{1,0:T(8,128)(2,1)} reshape(bf16[1679616]{0:T(1024)(128)(2,1)} %param.17) | data formatting | bytes 6718464 | tf_op jit(solution)/shard_map/reshape | solution.py:350
  30.4 0.0 collective-permute-done
  30.4 0.0 collective-permute-done.1
  30.4 0.0 collective-permute-done.2
  30.4 0.1 collective-permute-start.3
  30.5 2.7 %collective-permute-start.4 = (bf16[64,216]{1,0:T(8,128)(2,1)S(1)}, bf16[64,216]{1,0:T(8,128)(2,1)S(1)}, u32[]{:S(2)}, u32[]{:S(2)}) collective-permute-start(bf16[64,216]{1,0:T(8,128)(2,1)S(1)} %get-tuple-element.61), channel_id=1, source_target_pairs={{0,2},{1,3},{2,0},{3,1},{4,6},{5,7},{6,4},{7,5},{8,10},{9,11},{10,... | collective-permute-start | bytes 82952 | tf_op jit(solution)/shard_map/ppermute | solution.py:318
  33.2 1.7 %collective-permute-start.5 = (bf16[64,216]{1,0:T(8,128)(2,1)S(1)}, bf16[64,216]{1,0:T(8,128)(2,1)S(1)}, u32[]{:S(2)}, u32[]{:S(2)}) collective-permute-start(bf16[64,216]{1,0:T(8,128)(2,1)S(1)} %get-tuple-element.61), channel_id=1, source_target_pairs={{0,3},{1,0},{2,1},{3,2},{4,7},{5,4},{6,5},{7,6},{8,11},{9,8},{10,9... | collective-permute-start | bytes 82952 | tf_op jit(solution)/shard_map/ppermute | solution.py:318
  34.9 0.3 collective-permute-done.4
  35.2 1.6 %collective-permute-done.5 = bf16[64,216]{1,0:T(8,128)(2,1)S(1)} collective-permute-done((bf16[64,216]{1,0:T(8,128)(2,1)S(1)}, bf16[64,216]{1,0:T(8,128)(2,1)S(1)}, u32[]{:S(2)}, u32[]{:S(2)}) %collective-permute-start.5) | collective-permute-done | bytes 27680 | tf_op jit(solution)/shard_map/ppermute | solution.py:318
  36.8 0.3 convolution_convert_fusion
  37.2 0.0 collective-permute-done.6
  37.2 0.1 reshape.123
  37.3 0.1 reshape.124
  37.4 1.7 %collective-permute-start.7 = (bf16[512,128]{1,0:T(8,128)(2,1)S(1)}, bf16[512,128]{1,0:T(8,128)(2,1)S(1)}, u32[]{:S(2)}, u32[]{:S(2)}) collective-permute-start(bf16[512,128]{1,0:T(8,128)(2,1)S(1)} %pad_maximum_fusion), channel_id=1, source_target_pairs={{0,32},{16,48},{32,0},{48,16},{64,96},{80,112},{96,64},{112,80},{1... | collective-permute-start | bytes 393224 | tf_op jit(solution)/shard_map/ppermute | solution.py:309
  39.2 2.3 %collective-permute-done.7 = bf16[512,128]{1,0:T(8,128)(2,1)S(1)} collective-permute-done((bf16[512,128]{1,0:T(8,128)(2,1)S(1)}, bf16[512,128]{1,0:T(8,128)(2,1)S(1)}, u32[]{:S(2)}, u32[]{:S(2)}) %collective-permute-start.7) | collective-permute-done | bytes 131104 | tf_op jit(solution)/shard_map/ppermute | solution.py:309
  41.5 1.7 %collective-permute-start.10 = (bf16[1024,128]{1,0:T(8,128)(2,1)S(1)}, bf16[1024,128]{1,0:T(8,128)(2,1)S(1)}, u32[]{:S(2)}, u32[]{:S(2)}) collective-permute-start(bf16[1024,128]{1,0:T(8,128)(2,1)S(1)} %constant_dynamic-update-slice_fusion.11.refs_0_), channel_id=1, source_target_pairs={{0,192},{16,208},{32,224},{48,240},{64,0},{80,16},{96,32},{112,48}... | collective-permute-start | bytes 786440 | tf_op jit(solution)/shard_map/ppermute | solution.py:309
  43.2 3.2 %collective-permute-start.11 = (bf16[1024,128]{1,0:T(8,128)(2,1)S(1)}, bf16[1024,128]{1,0:T(8,128)(2,1)S(1)}, u32[]{:S(2)}, u32[]{:S(2)}) collective-permute-start(bf16[1024,128]{1,0:T(8,128)(2,1)S(1)} %constant_dynamic-update-slice_fusion.11.refs_0_), channel_id=1, source_target_pairs={{0,16},{16,0},{32,48},{48,32},{64,80},{80,64},{96,112},{112,96},{1... | collective-permute-start | bytes 786440 | tf_op jit(solution)/shard_map/ppermute | solution.py:309
  46.4 0.0 collective-permute-start.8
  46.4 1.6 %collective-permute-start.9 = (bf16[1024,128]{1,0:T(8,128)(2,1)S(1)}, bf16[1024,128]{1,0:T(8,128)(2,1)S(1)}, u32[]{:S(2)}, u32[]{:S(2)}) collective-permute-start(bf16[1024,128]{1,0:T(8,128)(2,1)S(1)} %constant_dynamic-update-slice_fusion.11.refs_0_), channel_id=1, source_target_pairs={{0,128},{16,144},{32,160},{48,176},{64,192},{80,208},{96,224},{112... | collective-permute-start | bytes 786440 | tf_op jit(solution)/shard_map/ppermute | solution.py:309
  48.1 2.0 %copy-done = bf16[1296,1296]{1,0:T(8,128)(2,1)S(1)} copy-done((bf16[1296,1296]{1,0:T(8,128)(2,1)S(1)}, bf16[1296,1296]{1,0:T(8,128)(2,1)}, u32[]{:S(2)}) %copy-start) | copy-done | bytes 3359256
  50.1 6.5 %left_forms.1 = (bf16[1296,1296]{1,0:T(8,128)(2,1)S(1)}, bf16[1296,1536]{1,0:T(8,128)(2,1)S(1)}) custom-call(bf16[1296,1296]{1,0:T(8,128)(2,1)S(1)} %copy-done), custom_call_target="tpu_custom_call" | custom-call | flops 4294967296 | bytes 4194304 | tf_op jit(solution)/shard_map/left_forms/pallas_call | solution.py:294
  56.7 1.9 %copy-done.9 = bf16[1296,1536]{1,0:T(8,128)(2,1)} copy-done((bf16[1296,1536]{1,0:T(8,128)(2,1)}, bf16[1296,1536]{1,0:T(8,128)(2,1)S(1)}, u32[]{:S(2)}) %copy-start.9) | copy-done | bytes 3981336
  58.6 1.9 %copy-done.11 = bf16[1296,1296]{1,0:T(8,128)(2,1)} copy-done((bf16[1296,1296]{1,0:T(8,128)(2,1)}, bf16[1296,1296]{1,0:T(8,128)(2,1)S(1)}, u32[]{:S(2)}) %copy-start.11) | copy-done | bytes 3359256
  60.4 0.0 collective-permute-done.11.refs_4_
  60.4 0.7 collective-permute-done.8.refs_1_
  61.1 0.9 collective-permute-start.12
  62.0 0.0 collective-permute-start.13
  62.0 0.5 collective-permute-start.14
  62.5 0.6 collective-permute-done.12.refs_5_
  63.1 0.4 collective-permute-done.13.refs_6_
  63.5 0.4 collective-permute-done.14.refs_7_
  63.9 0.9 gather_small.1.refs_8_
  64.8 3.3 %collective-permute-start.15 = (bf16[216,128]{1,0:T(8,128)(2,1)S(1)}, bf16[216,128]{1,0:T(8,128)(2,1)S(1)}, u32[]{:S(2)}, u32[]{:S(2)}) collective-permute-start(bf16[216,128]{1,0:T(8,128)(2,1)S(1)} %slice.14), channel_id=1, source_target_pairs={{0,0},{1,16},{2,32},{3,48},{4,64},{5,80},{6,96},{7,112},{8,128},{9... | collective-permute-start | bytes 165896 | tf_op jit(solution)/shard_map/ppermute | solution.py:323
  68.1 0.1 reshape.127
  68.2 0.1 reshape.128.refs_12_
  68.3 2.0 %collective-permute-done.15.refs_9_ = bf16[216,128]{1,0:T(8,128)(2,1)S(1)} collective-permute-done((bf16[216,128]{1,0:T(8,128)(2,1)S(1)}, bf16[216,128]{1,0:T(8,128)(2,1)S(1)}, u32[]{:S(2)}, u32[]{:S(2)}) %collective-permute-start.15) | collective-permute-done | bytes 55328 | tf_op jit(solution)/shard_map/ppermute | solution.py:323
  70.3 2.1 %copy-done.10 = bf16[1296,1536]{1,0:T(8,128)(2,1)S(1)} copy-done((bf16[1296,1536]{1,0:T(8,128)(2,1)S(1)}, bf16[1296,1536]{1,0:T(8,128)(2,1)}, u32[]{:S(2)}) %copy-start.10) | copy-done | bytes 3981336
  72.4 2.0 %copy-done.12 = bf16[1296,1296]{1,0:T(8,128)(2,1)S(1)} copy-done((bf16[1296,1296]{1,0:T(8,128)(2,1)S(1)}, bf16[1296,1296]{1,0:T(8,128)(2,1)}, u32[]{:S(2)}) %copy-start.12) | copy-done | bytes 3359256
  74.5 14.4 %left.1 = (bf16[216,216]{1,0:T(8,128)(2,1)}, f32[216,128]{1,0:T(8,128)S(1)}) custom-call(s32[16]{0:T(128)S(1)} %fusion.17.order_ref, bf16[1024,128]{1,0:T(8,128)(2,1)S(1)} %constant_dynamic-update-slice_fusion.11.refs_0_, bf16[1024,128]{1,0:T(8,128)(2,1)S(1)} %collective-permute-done.8.refs_1_, bf16[1024,128]{1,0:T(8,128)(2,1)S(1)} %collective-permute-done.9.refs_2_, ...), custom_call_target="tpu_custom_call" | custom-call | flops 8589934592 | bytes 4194304 | tf_op jit(solution)/shard_map/left/pallas_call | solution.py:215
  88.9 0.0 collective-permute-start.16
  88.9 1.3 %collective-permute-done.16 = f32[216,128]{1,0:T(8,128)S(1)} collective-permute-done((f32[216,128]{1,0:T(8,128)S(1)}, f32[216,128]{1,0:T(8,128)S(1)}, u32[]{:S(2)}, u32[]{:S(2)}) %collective-permute-start.16) | collective-permute-done | bytes 110624 | tf_op jit(solution)/shard_map/ppermute | solution.py:309
  90.2 5.7 %collective-permute-start.17 = (f32[216,128]{1,0:T(8,128)S(1)}, f32[216,128]{1,0:T(8,128)S(1)}, u32[]{:S(2)}, u32[]{:S(2)}) collective-permute-start(f32[216,128]{1,0:T(8,128)S(1)} %add.151), channel_id=1, source_target_pairs={{0,32},{16,48},{32,0},{48,16},{64,96},{80,112},{96,64},{112,80},{1... | collective-permute-start | bytes 331784 | tf_op jit(solution)/shard_map/ppermute | solution.py:309
  95.9 2.0 %copy-done.1 = bf16[1296,1296]{1,0:T(8,128)(2,1)S(1)} copy-done((bf16[1296,1296]{1,0:T(8,128)(2,1)S(1)}, bf16[1296,1296]{1,0:T(8,128)(2,1)}, u32[]{:S(2)}) %copy-start.1) | copy-done | bytes 3359256
  98.0 5.6 %right_form.1.refs_10_ = bf16[1296,1536]{1,0:T(8,128)(2,1)S(1)} custom-call(bf16[1296,1296]{1,0:T(8,128)(2,1)S(1)} %copy-done.1), custom_call_target="tpu_custom_call" | custom-call | flops 3221225472 | bytes 4194304 | tf_op jit(solution)/shard_map/right_form/pallas_call | solution.py:288
  103.6 0.0 collective-permute-done.17
  103.6 2.3 %collective-permute-start.18 = (f32[216,128]{1,0:T(8,128)S(1)}, f32[216,128]{1,0:T(8,128)S(1)}, u32[]{:S(2)}, u32[]{:S(2)}) collective-permute-start(f32[216,128]{1,0:T(8,128)S(1)} %add.152.own), channel_id=1, source_target_pairs={{0,64},{16,80},{32,96},{48,112},{64,128},{80,144},{96,160},{112,17... | collective-permute-start | bytes 331784 | tf_op jit(solution)/shard_map/ppermute | solution.py:309
  105.9 3.6 %collective-permute-start.19 = (f32[216,128]{1,0:T(8,128)S(1)}, f32[216,128]{1,0:T(8,128)S(1)}, u32[]{:S(2)}, u32[]{:S(2)}) collective-permute-start(f32[216,128]{1,0:T(8,128)S(1)} %add.152.own), channel_id=1, source_target_pairs={{0,128},{16,144},{32,160},{48,176},{64,192},{80,208},{96,224},{112... | collective-permute-start | bytes 331784 | tf_op jit(solution)/shard_map/ppermute | solution.py:309
  109.5 2.0 %collective-permute-start.20 = (f32[216,128]{1,0:T(8,128)S(1)}, f32[216,128]{1,0:T(8,128)S(1)}, u32[]{:S(2)}, u32[]{:S(2)}) collective-permute-start(f32[216,128]{1,0:T(8,128)S(1)} %add.152.own), channel_id=1, source_target_pairs={{0,192},{16,208},{32,224},{48,240},{64,0},{80,16},{96,32},{112,48}... | collective-permute-start | bytes 331784 | tf_op jit(solution)/shard_map/ppermute | solution.py:309
  111.5 11.9 %upper.1 = (bf16[216,216]{1,0:T(8,128)(2,1)}, bf16[6,216]{1,0:T(8,128)(2,1)}) custom-call(s32[16]{0:T(128)S(1)} %fusion.17.order_ref, bf16[1024,128]{1,0:T(8,128)(2,1)S(1)} %constant_dynamic-update-slice_fusion.11.refs_0_, bf16[1024,128]{1,0:T(8,128)(2,1)S(1)} %collective-permute-done.8.refs_1_, bf16[1024,128]{1,0:T(8,128)(2,1)S(1)} %collective-permute-done.9.refs_2_, ...), custom_call_target="tpu_custom_call" | custom-call | flops 8589934592 | bytes 4194304 | tf_op jit(solution)/shard_map/upper/pallas_call | solution.py:208
  123.4 0.0 collective-permute-done.20.three
  123.4 0.9 finish.1
  (42 shorter events, 0.3 us)
Async XLA Ops:
  0.6 0.7 copy-start.2
  1.3 0.7 copy-start.3
  2.0 0.7 copy-start.4
  2.8 0.7 copy-start.5
  3.5 0.7 copy-start.6
  4.1 0.7 copy-start.7
  4.8 0.7 copy-start.8
  5.7 24.7 %collective-permute-start = (bf16[16,216]{1,0:T(8,128)(2,1)S(1)}, bf16[16,216]{1,0:T(8,128)(2,1)S(1)}, u32[]{:S(2)}, u32[]{:S(2)}) collective-permute-start(bf16[16,216]{1,0:T(8,128)(2,1)S(1)} %get-tuple-element.30), channel_id=1, source_target_pairs={{0,4},{1,5},{2,6},{3,7},{4,8},{5,9},{6,10},{7,11},{8,12},{9,13},{1... | collective-permute-start | bytes 20744 | tf_op jit(solution)/shard_map/ppermute | solution.py:318
  9.5 20.9 %collective-permute-start.1 = (bf16[16,216]{1,0:T(8,128)(2,1)S(1)}, bf16[16,216]{1,0:T(8,128)(2,1)S(1)}, u32[]{:S(2)}, u32[]{:S(2)}) collective-permute-start(bf16[16,216]{1,0:T(8,128)(2,1)S(1)} %get-tuple-element.30), channel_id=1, source_target_pairs={{0,8},{1,9},{2,10},{3,11},{4,12},{5,13},{6,14},{7,15},{8,0},{9,1},... | collective-permute-start | bytes 20744 | tf_op jit(solution)/shard_map/ppermute | solution.py:318
  14.6 15.8 %collective-permute-start.2 = (bf16[16,216]{1,0:T(8,128)(2,1)S(1)}, bf16[16,216]{1,0:T(8,128)(2,1)S(1)}, u32[]{:S(2)}, u32[]{:S(2)}) collective-permute-start(bf16[16,216]{1,0:T(8,128)(2,1)S(1)} %get-tuple-element.30), channel_id=1, source_target_pairs={{0,12},{1,13},{2,14},{3,15},{4,0},{5,1},{6,2},{7,3},{8,4},{9,5},{1... | collective-permute-start | bytes 20744 | tf_op jit(solution)/shard_map/ppermute | solution.py:318
  17.8 19.3 %collective-permute-start.6 = (bf16[216,192]{0,1:T(8,128)(2,1)S(1)}, bf16[216,192]{0,1:T(8,128)(2,1)S(1)}, u32[]{:S(2)}, u32[]{:S(2)}) collective-permute-start(bf16[216,192]{0,1:T(8,128)(2,1)S(1)} %pad_maximum_fusion.1), channel_id=1, source_target_pairs={{0,0},{1,16},{2,32},{3,48},{4,64},{5,80},{6,96},{7,112},{8,128},{9... | collective-permute-start | bytes 248840 | tf_op jit(solution)/shard_map/ppermute | solution.py:323
  30.4 4.5 %collective-permute-start.3 = (bf16[64,216]{1,0:T(8,128)(2,1)S(1)}, bf16[64,216]{1,0:T(8,128)(2,1)S(1)}, u32[]{:S(2)}, u32[]{:S(2)}) collective-permute-start(bf16[64,216]{1,0:T(8,128)(2,1)S(1)} %get-tuple-element.61), channel_id=1, source_target_pairs={{0,1},{1,2},{2,3},{3,0},{4,5},{5,6},{6,7},{7,4},{8,9},{9,10},{10,1... | collective-permute-start | bytes 82952 | tf_op jit(solution)/shard_map/ppermute | solution.py:318
  30.5 4.6 %collective-permute-start.4 = (bf16[64,216]{1,0:T(8,128)(2,1)S(1)}, bf16[64,216]{1,0:T(8,128)(2,1)S(1)}, u32[]{:S(2)}, u32[]{:S(2)}) collective-permute-start(bf16[64,216]{1,0:T(8,128)(2,1)S(1)} %get-tuple-element.61), channel_id=1, source_target_pairs={{0,2},{1,3},{2,0},{3,1},{4,6},{5,7},{6,4},{7,5},{8,10},{9,11},{10,... | collective-permute-start | bytes 82952 | tf_op jit(solution)/shard_map/ppermute | solution.py:318
  33.2 3.6 %collective-permute-start.5 = (bf16[64,216]{1,0:T(8,128)(2,1)S(1)}, bf16[64,216]{1,0:T(8,128)(2,1)S(1)}, u32[]{:S(2)}, u32[]{:S(2)}) collective-permute-start(bf16[64,216]{1,0:T(8,128)(2,1)S(1)} %get-tuple-element.61), channel_id=1, source_target_pairs={{0,3},{1,0},{2,1},{3,2},{4,7},{5,4},{6,5},{7,6},{8,11},{9,8},{10,9... | collective-permute-start | bytes 82952 | tf_op jit(solution)/shard_map/ppermute | solution.py:318
  37.4 4.1 %collective-permute-start.7 = (bf16[512,128]{1,0:T(8,128)(2,1)S(1)}, bf16[512,128]{1,0:T(8,128)(2,1)S(1)}, u32[]{:S(2)}, u32[]{:S(2)}) collective-permute-start(bf16[512,128]{1,0:T(8,128)(2,1)S(1)} %pad_maximum_fusion), channel_id=1, source_target_pairs={{0,32},{16,48},{32,0},{48,16},{64,96},{80,112},{96,64},{112,80},{1... | collective-permute-start | bytes 393224 | tf_op jit(solution)/shard_map/ppermute | solution.py:309
  41.5 18.9 %collective-permute-start.10 = (bf16[1024,128]{1,0:T(8,128)(2,1)S(1)}, bf16[1024,128]{1,0:T(8,128)(2,1)S(1)}, u32[]{:S(2)}, u32[]{:S(2)}) collective-permute-start(bf16[1024,128]{1,0:T(8,128)(2,1)S(1)} %constant_dynamic-update-slice_fusion.11.refs_0_), channel_id=1, source_target_pairs={{0,192},{16,208},{32,224},{48,240},{64,0},{80,16},{96,32},{112,48}... | collective-permute-start | bytes 786440 | tf_op jit(solution)/shard_map/ppermute | solution.py:309
  43.2 17.2 %collective-permute-start.11 = (bf16[1024,128]{1,0:T(8,128)(2,1)S(1)}, bf16[1024,128]{1,0:T(8,128)(2,1)S(1)}, u32[]{:S(2)}, u32[]{:S(2)}) collective-permute-start(bf16[1024,128]{1,0:T(8,128)(2,1)S(1)} %constant_dynamic-update-slice_fusion.11.refs_0_), channel_id=1, source_target_pairs={{0,16},{16,0},{32,48},{48,32},{64,80},{80,64},{96,112},{112,96},{1... | collective-permute-start | bytes 786440 | tf_op jit(solution)/shard_map/ppermute | solution.py:309
  46.4 14.7 %collective-permute-start.8 = (bf16[1024,128]{1,0:T(8,128)(2,1)S(1)}, bf16[1024,128]{1,0:T(8,128)(2,1)S(1)}, u32[]{:S(2)}, u32[]{:S(2)}) collective-permute-start(bf16[1024,128]{1,0:T(8,128)(2,1)S(1)} %constant_dynamic-update-slice_fusion.11.refs_0_), channel_id=1, source_target_pairs={{0,64},{16,80},{32,96},{48,112},{64,128},{80,144},{96,160},{112,17... | collective-permute-start | bytes 786440 | tf_op jit(solution)/shard_map/ppermute | solution.py:309
  46.4 14.7 %collective-permute-start.9 = (bf16[1024,128]{1,0:T(8,128)(2,1)S(1)}, bf16[1024,128]{1,0:T(8,128)(2,1)S(1)}, u32[]{:S(2)}, u32[]{:S(2)}) collective-permute-start(bf16[1024,128]{1,0:T(8,128)(2,1)S(1)} %constant_dynamic-update-slice_fusion.11.refs_0_), channel_id=1, source_target_pairs={{0,128},{16,144},{32,160},{48,176},{64,192},{80,208},{96,224},{112... | collective-permute-start | bytes 786440 | tf_op jit(solution)/shard_map/ppermute | solution.py:309
  48.1 2.0 %copy-start = (bf16[1296,1296]{1,0:T(8,128)(2,1)S(1)}, bf16[1296,1296]{1,0:T(8,128)(2,1)}, u32[]{:S(2)}) copy-start(bf16[1296,1296]{1,0:T(8,128)(2,1)} %reshape.122.s_ref) | copy-start | bytes 10077700
  56.7 1.9 %copy-start.9 = (bf16[1296,1536]{1,0:T(8,128)(2,1)}, bf16[1296,1536]{1,0:T(8,128)(2,1)S(1)}, u32[]{:S(2)}) copy-start(bf16[1296,1536]{1,0:T(8,128)(2,1)S(1)} %get-tuple-element.43.refs_11_) | copy-start | bytes 11943940
  58.5 1.9 %copy-start.11 = (bf16[1296,1296]{1,0:T(8,128)(2,1)}, bf16[1296,1296]{1,0:T(8,128)(2,1)S(1)}, u32[]{:S(2)}) copy-start(bf16[1296,1296]{1,0:T(8,128)(2,1)S(1)} %get-tuple-element.42.refs_10_.refs_9_) | copy-start | bytes 10077700
  61.1 2.0 %collective-permute-start.12 = (bf16[1024,128]{1,0:T(8,128)(2,1)S(1)}, bf16[1024,128]{1,0:T(8,128)(2,1)S(1)}, u32[]{:S(2)}, u32[]{:S(2)}) collective-permute-start(bf16[1024,128]{1,0:T(8,128)(2,1)S(1)} %collective-permute-done.8.refs_1_), channel_id=1, source_target_pairs={{0,16},{16,0},{32,48},{48,32},{64,80},{80,64},{96,112},{112,96},{1... | collective-permute-start | bytes 786440 | tf_op jit(solution)/shard_map/ppermute | solution.py:309
  62.0 1.5 %collective-permute-start.13 = (bf16[1024,128]{1,0:T(8,128)(2,1)S(1)}, bf16[1024,128]{1,0:T(8,128)(2,1)S(1)}, u32[]{:S(2)}, u32[]{:S(2)}) collective-permute-start(bf16[1024,128]{1,0:T(8,128)(2,1)S(1)} %collective-permute-done.9.refs_2_), channel_id=1, source_target_pairs={{0,16},{16,0},{32,48},{48,32},{64,80},{80,64},{96,112},{112,96},{1... | collective-permute-start | bytes 786440 | tf_op jit(solution)/shard_map/ppermute | solution.py:309
  62.0 1.9 %collective-permute-start.14 = (bf16[1024,128]{1,0:T(8,128)(2,1)S(1)}, bf16[1024,128]{1,0:T(8,128)(2,1)S(1)}, u32[]{:S(2)}, u32[]{:S(2)}) collective-permute-start(bf16[1024,128]{1,0:T(8,128)(2,1)S(1)} %collective-permute-done.10.refs_3_), channel_id=1, source_target_pairs={{0,16},{16,0},{32,48},{48,32},{64,80},{80,64},{96,112},{112,96},{1... | collective-permute-start | bytes 786440 | tf_op jit(solution)/shard_map/ppermute | solution.py:309
  64.8 5.5 %collective-permute-start.15 = (bf16[216,128]{1,0:T(8,128)(2,1)S(1)}, bf16[216,128]{1,0:T(8,128)(2,1)S(1)}, u32[]{:S(2)}, u32[]{:S(2)}) collective-permute-start(bf16[216,128]{1,0:T(8,128)(2,1)S(1)} %slice.14), channel_id=1, source_target_pairs={{0,0},{1,16},{2,32},{3,48},{4,64},{5,80},{6,96},{7,112},{8,128},{9... | collective-permute-start | bytes 165896 | tf_op jit(solution)/shard_map/ppermute | solution.py:323
  70.3 2.1 %copy-start.10 = (bf16[1296,1536]{1,0:T(8,128)(2,1)S(1)}, bf16[1296,1536]{1,0:T(8,128)(2,1)}, u32[]{:S(2)}) copy-start(bf16[1296,1536]{1,0:T(8,128)(2,1)} %copy-done.9) | copy-start | bytes 11943940
  72.4 2.0 %copy-start.12 = (bf16[1296,1296]{1,0:T(8,128)(2,1)S(1)}, bf16[1296,1296]{1,0:T(8,128)(2,1)}, u32[]{:S(2)}) copy-start(bf16[1296,1296]{1,0:T(8,128)(2,1)} %copy-done.11) | copy-start | bytes 10077700
  88.9 1.3 %collective-permute-start.16 = (f32[216,128]{1,0:T(8,128)S(1)}, f32[216,128]{1,0:T(8,128)S(1)}, u32[]{:S(2)}, u32[]{:S(2)}) collective-permute-start(f32[216,128]{1,0:T(8,128)S(1)} %get-tuple-element.44), channel_id=1, source_target_pairs={{0,16},{16,0},{32,48},{48,32},{64,80},{80,64},{96,112},{112,96},{1... | collective-permute-start | bytes 331784 | tf_op jit(solution)/shard_map/ppermute | solution.py:309
  90.2 13.3 %collective-permute-start.17 = (f32[216,128]{1,0:T(8,128)S(1)}, f32[216,128]{1,0:T(8,128)S(1)}, u32[]{:S(2)}, u32[]{:S(2)}) collective-permute-start(f32[216,128]{1,0:T(8,128)S(1)} %add.151), channel_id=1, source_target_pairs={{0,32},{16,48},{32,0},{48,16},{64,96},{80,112},{96,64},{112,80},{1... | collective-permute-start | bytes 331784 | tf_op jit(solution)/shard_map/ppermute | solution.py:309
  95.9 2.0 %copy-start.1 = (bf16[1296,1296]{1,0:T(8,128)(2,1)S(1)}, bf16[1296,1296]{1,0:T(8,128)(2,1)}, u32[]{:S(2)}) copy-start(bf16[1296,1296]{1,0:T(8,128)(2,1)} %reshape.122.s_ref) | copy-start | bytes 10077700
  98.0 13.5 %copy-start.13 = (bf16[1296,1296]{1,0:T(8,128)(2,1)S(1)}, bf16[1296,1296]{1,0:T(8,128)(2,1)}, u32[]{:S(2)}) copy-start(bf16[1296,1296]{1,0:T(8,128)(2,1)} %copy-done.11) | copy-start | bytes 10077700
  103.6 19.7 %collective-permute-start.18 = (f32[216,128]{1,0:T(8,128)S(1)}, f32[216,128]{1,0:T(8,128)S(1)}, u32[]{:S(2)}, u32[]{:S(2)}) collective-permute-start(f32[216,128]{1,0:T(8,128)S(1)} %add.152.own), channel_id=1, source_target_pairs={{0,64},{16,80},{32,96},{48,112},{64,128},{80,144},{96,160},{112,17... | collective-permute-start | bytes 331784 | tf_op jit(solution)/shard_map/ppermute | solution.py:309
  105.9 17.4 %collective-permute-start.19 = (f32[216,128]{1,0:T(8,128)S(1)}, f32[216,128]{1,0:T(8,128)S(1)}, u32[]{:S(2)}, u32[]{:S(2)}) collective-permute-start(f32[216,128]{1,0:T(8,128)S(1)} %add.152.own), channel_id=1, source_target_pairs={{0,128},{16,144},{32,160},{48,176},{64,192},{80,208},{96,224},{112... | collective-permute-start | bytes 331784 | tf_op jit(solution)/shard_map/ppermute | solution.py:309
  109.5 13.8 %collective-permute-start.20 = (f32[216,128]{1,0:T(8,128)S(1)}, f32[216,128]{1,0:T(8,128)S(1)}, u32[]{:S(2)}, u32[]{:S(2)}) collective-permute-start(f32[216,128]{1,0:T(8,128)S(1)} %add.152.own), channel_id=1, source_target_pairs={{0,192},{16,208},{32,224},{48,240},{64,0},{80,16},{96,32},{112,48}... | collective-permute-start | bytes 331784 | tf_op jit(solution)/shard_map/ppermute | solution.py:309

commit v3 on v2

--- a/solution.py
+++ b/solution.py
@@ -11,6 +11,7 @@
 NT = (((1,), (1,)), ((), ()))
 VM = pl.BlockSpec(memory_space=pltpu.VMEM)
 SM = pl.BlockSpec(memory_space=pltpu.SMEM)
+HB = pl.BlockSpec(memory_space=pltpu.HBM)
 BLOCK = 512
 WIDE = 3456
 
@@ -31,7 +32,18 @@
     return pl.CostEstimate(flops=flops, transcendentals=0, bytes_accessed=1 << 22)
 
 
-def prepare_kernel(te, re, be, le, uct, rct, lct, piece, pack):
+def load(pairs, sems):
+    copies = [pltpu.make_async_copy(src, dst, sems.at[n]) for n, (src, dst) in enumerate(pairs)]
+    for cp in copies:
+        cp.start()
+    return copies
+
+
+def prepare_kernel(*refs):
+    hbm, (piece, pack, turned), local, sems = refs[:9], refs[9:12], refs[12:21], refs[21]
+    for cp in load(list(zip(hbm, local)), sems):
+        cp.wait()
+    te, re, be, le, uct, rct, lct, tpt, bpt = local
     zero = jnp.zeros((2, 216), B)
     for n, e in ((0, te), (1, le)):
         v = e[...].astype(F)
@@ -41,12 +53,33 @@
     for e in (te, re, be):
         v = e[...].astype(F)
         parts.append(jnp.concatenate([v[:, j, :] for j in range(6)], axis=1))
+    turned[0:96, :] = tpt[...]
+    turned[96:192, :] = bpt[...]
+    turned[192:200, :] = jnp.concatenate([parts[2].astype(B), zero], axis=0)
     for c in (uct, rct, lct):
         parts.append(c[...].astype(F))
     flat = jnp.concatenate(parts + [jnp.zeros((6, 88), F)], axis=1)
     flat = jnp.concatenate([flat, jnp.zeros((2, 1024), F)], axis=0).astype(B)
     for k in range(8):
         pack[8 * k:8 * k + 8, :] = flat[:, 128 * k:128 * k + 128]
+
+
+def pieces_kernel(at_ref, turned, piece, out, tpx, bpr):
+    out[0:16, :] = piece[...]
+    out[16:24, :] = turned[192:200, :]
+    row = lax.broadcasted_iota(jnp.int32, (8, 96), 0)
+    lane = lax.broadcasted_iota(jnp.int32, (8, 96), 1)
+    pick = ((lane == at_ref[0] + row) & (row < 6)).astype(B)
+    top = dot(pick, turned[0:96, :])
+    flat = jnp.concatenate(
+        [jnp.concatenate([top[x:x + 1, b * 36:(b + 1) * 36] for x in range(6)], axis=1) for b in range(6)], axis=0)
+    flat = jnp.concatenate([flat, jnp.zeros((6, 40), F)], axis=1)
+    flat = jnp.concatenate([flat, jnp.zeros((2, 256), F)], axis=0).astype(B)
+    tpx[0:8, :] = flat[:, :128]
+    tpx[8:16, :] = flat[:, 128:]
+    bottom = dot(pick, turned[96:192, :])
+    gap = jnp.zeros((8, 4), F)
+    bpr[...] = jnp.concatenate([y for b in range(6) for y in (bottom[:, b * 36:(b + 1) * 36], gap)], axis=1).astype(B)
 
 
 def expand(order_ref, bufs, off, dst):
@@ -89,7 +122,7 @@
 def big(w_ref, p_ref, k, o_ref):
     def f(i, _):
         at = pl.multiple_of(i * 432, 16)
-        res = dot(w_ref[pl.ds(at, 432), :], p_ref[:k, :])
+        res = dot(w_ref[pl.ds(at, 432), :k], p_ref[:k, :])
         for a in range(6):
             o_ref[a, pl.ds(at, 432), :] = res[:, a * 128:(a + 1) * 128]
         return 0
@@ -112,7 +145,8 @@
 
 def upper_kernel(order_ref, *refs):
     bufs = refs[:8]
-    small_ref, wtop_ref, wright_ref, out_ref, ct_ref, tef, pf, p1, p3, o1, o3, tps = refs[8:]
+    small_ref, wtop_hbm, wright_hbm, out_ref, ct_ref, tef, pf, p1, p3, o1, o3, tps, wtop_ref, wright_ref, sems = refs[8:]
+    copies = load([(wtop_hbm, wtop_ref), (wright_hbm, wright_ref)], sems)
     expand(order_ref, bufs, 0, tef)
     uc = small_ref[648:744, :]
     rc = small_ref[744:840, :]
@@ -134,7 +168,9 @@
         for a in range(6):
             pf[a, at:at + 36, :] = d3[a * 36:(a + 1) * 36, :]
     to_bf16(pf, p3, 1536)
+    copies[0].wait()
     big(wtop_ref, p1, 1296, o1)
+    copies[1].wait()
     big(wright_ref, p3, 1536, o3)
     acc = jnp.zeros((240, 256), F)
     for tp in range(18):
@@ -154,12 +190,13 @@
 
 def left_kernel(order_ref, *refs):
     bufs = refs[:8]
-    small_ref, ber_ref, wtop_ref, wbot_ref, bpr_ref, out_ref, cb_ref, lef, pf, p2, p4, o2, o4, cbs, abf = refs[8:]
+    small_ref, ber_ref, wtop_hbm, wbot_hbm, bpr_ref, out_ref, cb_ref, lef, pf, p2, p4, o2, o4, cbs, abf, wtop_ref, wbot_ref, sems = refs[8:]
+    copies = load([(wtop_hbm, wtop_ref), (wbot_hbm, wbot_ref)], sems)
     expand(order_ref, bufs, 216, lef)
     uc = small_ref[648:744, :]
     lc = small_ref[840:936, :]
     at = dot(small_ref[0:216, :], uc, NT).astype(B)
-    abf[...] = padded(dot(ber_ref[...], lc, NT))
+    abf[0:216, :] = padded(dot(ber_ref[...], lc, NT))
     ab = jnp.concatenate([abf[pl.ds(b * 36 + h, 12, stride=3), :] for b in range(6) for h in range(3)], axis=0).astype(B)[:, :96]
     for u in range(36):
         le = lef[pl.ds(u, 96, stride=36), :].astype(B)
@@ -175,7 +212,9 @@
             for h in range(3):
                 pf[b, pl.ds(h * 36 + u, 12, stride=128), :] = d4[b * 36 + h * 12:b * 36 + h * 12 + 12, :]
     to_bf16(pf, p4, 1536)
+    copies[0].wait()
     big(wtop_ref, p2, 1296, o2)
+    copies[1].wait()
     big(wbot_ref, p4, 1536, o4)
     acc = jnp.zeros((240, 240), F)
     for sp in range(18):
@@ -191,45 +230,60 @@
     lh = compressed(acc * jnp.float32(WIDE ** -0.5))
     for a in range(6):
         out_ref[a * 36:(a + 1) * 36, :] = lh[a * 40:a * 40 + 36, :].astype(B)
-    cb_ref[...] = cbs[0:216, :]
+    sums = jnp.transpose(cbs[0:256, :])
+    cb_ref[...] = jnp.zeros((128, 256), F)
+    for m in range(16):
+        at = ((m % 4) * 4 + ((m // 4) % 2) * 2 + m // 8) * 6
+        cb_ref[8 * m:8 * m + 6, :] = sums[at:at + 6, :]
 
 
 def scratch():
-    return [pltpu.VMEM((WIDE, 128), F), pltpu.VMEM((6, 1536, 128), F), pltpu.VMEM((1536, 768), B),
+    return [pltpu.VMEM((WIDE, 128), F), pltpu.VMEM((6, 2048, 128), F), pltpu.VMEM((1536, 768), B),
             pltpu.VMEM((1536, 768), B), pltpu.VMEM((6, 1440, 128), F), pltpu.VMEM((6, 1440, 128), F)]
 
 
-def prepare(te, re, be, le, uct, rct, lct):
-    return pl.pallas_call(prepare_kernel, out_shape=(shape_of(16, 216), shape_of(64, 128)), in_specs=[VM] * 7,
-                          out_specs=(VM, VM), name="prepare", compiler_params=params(4))(te, re, be, le, uct, rct, lct)
+def prepare(*args):
+    return pl.pallas_call(
+        prepare_kernel, out_shape=(shape_of(16, 216), shape_of(64, 128), shape_of(200, 216)),
+        in_specs=[HB] * 9, out_specs=(VM,) * 3,
+        scratch_shapes=[pltpu.VMEM(x.shape, B) for x in args] + [pltpu.SemaphoreType.DMA((9,))],
+        name="prepare")(*args)
+
+
+def pieces(at, turned, piece):
+    return pl.pallas_call(pieces_kernel, out_shape=(shape_of(24, 216), shape_of(16, 128), shape_of(8, 240)),
+                          in_specs=[SM, VM, VM], out_specs=(VM,) * 3, name="pieces",
+                          compiler_params=params(4))(at, turned, piece)
+
+
+def form_copies():
+    return [pltpu.VMEM((1296, 1408), B), pltpu.VMEM((1296, 1536), B), pltpu.SemaphoreType.DMA((2,))]
 
 
 def upper(order, bufs, small, wtop, wright):
     return pl.pallas_call(
-        upper_kernel, out_shape=(shape_of(216, 216), shape_of(6, 216)), in_specs=[SM] + [VM] * 11, out_specs=(VM, VM),
-        scratch_shapes=scratch() + [pltpu.VMEM((320, 128), F)], name="upper", compiler_params=params(23),
-        cost_estimate=work(8 << 30))(order, *bufs, small, wtop, wright)
+        upper_kernel, out_shape=(shape_of(216, 216), shape_of(6, 216)), in_specs=[SM] + [VM] * 9 + [HB] * 2,
+        out_specs=(VM, VM), scratch_shapes=scratch() + [pltpu.VMEM((320, 128), F)] + form_copies(), name="upper",
+        compiler_params=params(50), cost_estimate=work(8 << 30))(order, *bufs, small, wtop, wright)
 
 
 def left(order, bufs, small, ber, wtop, wbot, bpr):
     return pl.pallas_call(
-        left_kernel, out_shape=(shape_of(216, 216), shape_of(216, 128, kind=F)), in_specs=[SM] + [VM] * 13,
-        out_specs=(VM, VM), scratch_shapes=scratch() + [pltpu.VMEM((288, 128), F), pltpu.VMEM((216, 128), F)], name="left",
-        compiler_params=params(23), cost_estimate=work(8 << 30))(order, *bufs, small, ber, wtop, wbot, bpr)
-
-
-def finish_kernel(at_ref, own, one, two, three, out_ref):
-    total = (own[...] + one[...] + two[...] + three[...]).astype(B)
-    lane = lax.broadcasted_iota(jnp.int32, (8, 128), 1)
-    pick = (lane == at_ref[0] + lax.broadcasted_iota(jnp.int32, (8, 128), 0)).astype(B)
-    res = dot(pick, total, NT)
+        left_kernel, out_shape=(shape_of(216, 216), shape_of(128, 256, kind=F)),
+        in_specs=[SM] + [VM] * 10 + [HB] * 2 + [VM], out_specs=(VM, VM),
+        scratch_shapes=scratch() + [pltpu.VMEM((288, 128), F), pltpu.VMEM((232, 128), F)] + form_copies(), name="left",
+        compiler_params=params(50), cost_estimate=work(8 << 30))(order, *bufs, small, ber, wtop, wbot, bpr)
+
+
+def finish_kernel(own, one, two, three, out_ref):
+    res = own[...] + one[...] + two[...] + three[...]
     rows = [jnp.concatenate([res[a:a + 1, x * 36:(x + 1) * 36] for a in range(6)], axis=1) for x in range(6)]
     out_ref[...] = jnp.concatenate(rows, axis=0).astype(B)
 
 
-def finish(at, *parts):
-    return pl.pallas_call(finish_kernel, out_shape=shape_of(6, 216), in_specs=[SM] + [VM] * 4, out_specs=VM,
-                          name="finish", compiler_params=params(4))(at, *parts)
+def finish(*parts):
+    return pl.pallas_call(finish_kernel, out_shape=shape_of(6, 216), in_specs=[VM] * 4, out_specs=VM,
+                          name="finish", compiler_params=params(4))(*parts)
 
 
 def lanes_shifted(a_ref, z_ref, pair):
@@ -243,7 +297,7 @@
     z_ref[...] = dot(a_ref[:, pl.ds(base, 256)], sel)
 
 
-def realign(a_ref, z_ref, o_ref):
+def realign(a_ref, z_ref, o_ref, out_hbm, sem):
     lane = lax.broadcasted_iota(jnp.int32, (36, 128), 1)
 
     def f(g, _):
@@ -259,41 +313,94 @@
                 strips.append(jnp.concatenate(tiles, axis=1))
         at = pl.multiple_of(g * 144, 16)
         o_ref[pl.ds(at, 144), :] = jnp.concatenate(strips, axis=0).astype(B)
+        pltpu.make_async_copy(o_ref.at[pl.ds(at, 144), :], out_hbm.at[pl.ds(at, 144), :], sem.at[g]).start()
         return 0
     lax.fori_loop(0, 9, f, 0)
 
-
-def right_form_kernel(s_ref, wright_ref, apad, z):
-    apad[:, 1296:1408] = jnp.zeros((1296, 112), B)
-    apad[:, :1296] = s_ref[...]
-    realign(apad, z, wright_ref)
-
-
-def left_forms_kernel(s_ref, wtop_ref, wbot_ref, apad, z):
+    def w(g, _):
+        at = pl.multiple_of(g * 144, 16)
+        pltpu.make_async_copy(o_ref.at[pl.ds(at, 144), :], out_hbm.at[pl.ds(at, 144), :], sem.at[g]).wait()
+        return 0
+    lax.fori_loop(0, 9, w, 0)
+
+
+def right_form_kernel(s_hbm, wright_hbm, apad, z, o, sems, done):
+    load([(s_hbm, apad)], sems)[0].wait()
+    realign(apad, z, o, wright_hbm, done)
+
+
+def left_forms_kernel(s_hbm, wtop_hbm, wbot_hbm, apad, z, o, sems, done, s_ref):
+    load([(s_hbm, s_ref)], sems)[0].wait()
     eye = (lax.broadcasted_iota(jnp.int32, (128, 128), 0) == lax.broadcasted_iota(jnp.int32, (128, 128), 1)).astype(B)
     for b in range(11):
         n = min(128, 1296 - b * 128)
-        res = dot(eye[:n, :n], s_ref[:, b * 128:b * 128 + n], NT).astype(B)
-        wtop_ref[b * 128:b * 128 + n, :] = res
-        apad[b * 128:b * 128 + n, :1296] = res
+        apad[b * 128:b * 128 + n, :1296] = dot(eye[:n, :n], s_ref[:, b * 128:b * 128 + n], NT).astype(B)
     apad[:, 1296:1408] = jnp.zeros((1296, 112), B)
-    realign(apad, z, wbot_ref)
+    out = pltpu.make_async_copy(apad, wtop_hbm, sems.at[0])
+    out.start()
+    realign(apad, z, o, wbot_hbm, done)
+    out.wait()
+
+
+def flat_form_kernel(x_ref, s_hbm, wide, tiles, s_ref, sems):
+    def widen(i, _):
+        at = pl.multiple_of(i * 256, 16)
+        wide[pl.ds(at, 256), :] = x_ref[pl.ds(at, 256), :].astype(F)
+        return 0
+    lax.fori_loop(0, 51, widen, 0)
+    wide[13056:13122, :] = x_ref[13056:13122, :].astype(F)
+    lane = lax.broadcasted_iota(jnp.int32, (162, 128), 1)
+    for i in range(8):
+        def turn(j):
+            v = wide[pl.ds(10 * i + j, 162, stride=81), :]
+            return pltpu.roll(v, 128 - 16 * i, 1) if i else v
+        here = turn(0)
+        for j in range(11):
+            if j == 10:
+                tile = jnp.where(lane < 16, here, 0.0)
+            else:
+                after = turn(j + 1)
+                tile = jnp.where(lane < 128 - 16 * i, here, after) if i else here
+                here = after
+            tiles[j, pl.ds(i, 162, stride=8), :] = tile
+
+    def narrow(g, _):
+        at = pl.multiple_of(g * 144, 16)
+        for j in range(11):
+            s_ref[pl.ds(at, 144), 128 * j:128 * j + 128] = tiles[j, pl.ds(at, 144), :].astype(B)
+        pltpu.make_async_copy(s_ref.at[pl.ds(at, 144), :], s_hbm.at[pl.ds(at, 144), :], sems.at[g]).start()
+        return 0
+    lax.fori_loop(0, 9, narrow, 0)
+
+    def w(g, _):
+        at = pl.multiple_of(g * 144, 16)
+        pltpu.make_async_copy(s_ref.at[pl.ds(at, 144), :], s_hbm.at[pl.ds(at, 144), :], sems.at[g]).wait()
+        return 0
+    lax.fori_loop(0, 9, w, 0)
 
 
 def form_scratch():
-    return [pltpu.VMEM((1296, 1408), B), pltpu.VMEM((2, 1296, 256), F)]
+    return [pltpu.VMEM((1296, 1408), B), pltpu.VMEM((2, 1296, 256), F), pltpu.VMEM((1296, 1536), B),
+            pltpu.SemaphoreType.DMA((1,)), pltpu.SemaphoreType.DMA((9,))]
+
+
+def flat_form(flat):
+    return pl.pallas_call(flat_form_kernel, out_shape=shape_of(1296, 1408), in_specs=[VM], out_specs=HB,
+                          scratch_shapes=[pltpu.VMEM((13616, 128), F), pltpu.VMEM((11, 1344, 128), F),
+                                          pltpu.VMEM((1296, 1408), B), pltpu.SemaphoreType.DMA((9,))],
+                          name="flat_form", compiler_params=params(60), cost_estimate=work(3 << 30))(flat)
 
 
 def right_form(s2):
-    return pl.pallas_call(right_form_kernel, out_shape=shape_of(1296, 1536), in_specs=[VM], out_specs=VM,
-                          scratch_shapes=form_scratch(), name="right_form", compiler_params=params(9),
+    return pl.pallas_call(right_form_kernel, out_shape=shape_of(1296, 1536), in_specs=[HB], out_specs=HB,
+                          scratch_shapes=form_scratch(), name="right_form", compiler_params=params(60),
                           cost_estimate=work(3 << 30))(s2)
 
 
 def left_forms(s2):
-    return pl.pallas_call(left_forms_kernel, out_shape=(shape_of(1296, 1296), shape_of(1296, 1536)), in_specs=[VM],
-                          out_specs=(VM, VM), scratch_shapes=form_scratch(), name="left_forms", compiler_params=params(9),
-                          cost_estimate=work(4 << 30))(s2)
+    return pl.pallas_call(left_forms_kernel, out_shape=(shape_of(1296, 1408), shape_of(1296, 1536)), in_specs=[HB],
+                          out_specs=(HB, HB), scratch_shapes=form_scratch() + [pltpu.VMEM((1296, 1408), B)],
+                          name="left_forms", compiler_params=params(60), cost_estimate=work(4 << 30))(s2)
 
 
 ROW, COL = "row", "col"
@@ -346,28 +453,23 @@
     zhi, x = c // 4, c % 4
     hold = lax.optimization_barrier
 
-    piece, pack = prepare(te, re, be, le, uc.T, rc.T, lc.T)
-    s2 = site_flat.reshape(1296, 1296)
-
-    projectors = swap_axes(jnp.concatenate([tp, bp], axis=1))
-
-    got = [col_permute(piece, lambda z, i, s=s: ((z + s) % 4, i)) for s in (1, 2, 3)]
-    *got, s2 = hold((*got, s2))
-    piece = stacked(piece, got)
+    piece, pack, turned = prepare(te, re, be, le, uc.T, rc.T, lc.T, tp.T, bp.T)
+    swapped = swap_axes(turned)
+    s2 = flat_form(hold((site_flat, turned))[0].reshape(13122, 128))
+    swapped, s2 = hold((swapped, s2))
+    piece, tpx, bpr = pieces((c * 6).astype(jnp.int32).reshape(1), swapped, piece)
+
+    piece = stacked(piece, [col_permute(piece, lambda z, i, s=s: ((z + s) % 4, i)) for s in (1, 2, 3)])
     piece = stacked(piece, [col_permute(piece, lambda z, i, s=s: (z, (i + s) % 4)) for s in (1, 2, 3)])
-    at = jnp.arange(256)
-    x_rel, z_rel, edge, j = at // 64, (at // 16) % 4, (at // 8) % 2, at % 8
+    at = jnp.arange(384)
+    x_rel, z_rel, edge, j = at // 96, (at // 24) % 4, (at // 8) % 3, at % 8
     block = ((zhi - z_rel) % 4) * 4 + (x - x_rel) % 4
     target = jnp.where(j < 6, edge * 128 + block * 6 + j, -1)
-    place = (target[:, None] == jnp.arange(256)[None, :]).astype(B)
+    place = (target[:, None] == at[None, :]).astype(B)
     rows = lax.dot_general(piece, place, (((0,), (0,)), ((), ())), preferred_element_type=F).astype(B)
-
-    tpx = lax.dynamic_slice_in_dim(projectors, c * 6, 6, 1)
-    tpx = tpx.reshape(6, 36, 6).transpose(0, 2, 1).reshape(6, 216)
-    tpx = jnp.pad(tpx, ((0, 2), (0, 40))).reshape(8, 2, 128).transpose(1, 0, 2).reshape(16, 128)
-    bpr = lax.dynamic_slice_in_dim(projectors, 96 + c * 6, 6, 1).T.reshape(6, 6, 36)
-    bpr = jnp.pad(bpr, ((0, 2), (0, 0), (0, 4))).reshape(8, 240)
-    own = jnp.concatenate([rows[:, :128], rows[:, 128:], pack, tpx], axis=0)
+    ber = rows[:, 256:]
+
+    own = jnp.concatenate([rows[:, :128], rows[:, 128:256], pack, tpx], axis=0)
     near = stacked(own, [other_z(own)])
     far = [along_y(near, s) for s in (1, 2, 3)]
     near_twin = other_core(near)
@@ -380,19 +482,19 @@
     order = order.astype(jnp.int32)
 
     small = gather_small(order, bufs)
-    ber = swap_axes(small[432:648])
 
     lf, cb = left(order, bufs, small, ber, wtop, wbot, bpr)
-    cb = cb + other_core(cb)
-    cb_z = other_z(cb)
+    part = lambda v, n, size: lax.dynamic_slice_in_dim(v, n * size, size, 0)
+    cb = part(cb, core, 64) + other_core(part(cb, 1 - core, 64))
+    cb_z = other_z(part(cb, 1 - zlo, 32))
     wright = right_form(hold((s2, cb))[0])
     cb_z, wright = hold((cb_z, wright))
-    cb = cb + cb_z
-    cb_y = [along_y(cb, s) for s in (1, 2, 3)]
+    cb = part(cb, zlo, 32) + cb_z
+    cb_y = [along_y(part(cb, (y + s) % 4, 8), s) for s in (1, 2, 3)]
     order = hold((order, cb))[0]
     up, corner_top = upper(order, bufs, small, wtop, wright)
     *cb_y, up = hold((*cb_y, up))
-    corner_bottom = finish((r * 6).astype(jnp.int32).reshape(1), cb, *cb_y)
+    corner_bottom = finish(part(cb, y, 8), *cb_y)
     return up, lf, corner_top, corner_bottom
 
 

time: 125 us -> 110 us (0.88)
  local copies, waits for them, and re-layouts: 25.3 us -> 0.16 us
  Pallas kernels: 40.4 us -> 54.5 us
  starting transfers between devices: 46.8 us -> 40.9 us
  waiting for transfers between devices: 9.63 us -> 12.7 us
    unnamed x36 -> x12, local copies, waits for them, and re-layouts: 16.9 us -> 0.06 us
    pallas_call x3 -> x5, Pallas kernels: 21.9 us -> 31.7 us  [the longest x1 14.5 us: left(): pl.pallas_call(left_kernel, out_shape=(shape_of(216, 216), shape_of(128,...]
    ppermute x13, starting transfers between devices: 23.2 us -> 14.1 us  [row_permute(): return lax.ppermute(x, ROW, pairs)]
    reshape x6 -> x0, local copies, waits for them, and re-layouts: 8.33 us -> none  [the longest x1 7.97 us: shards(): s2 = site_flat.reshape(1296, 1296)]
    ppermute x6, starting transfers between devices: 15.8 us -> 22.3 us  [col_permute(): return lax.ppermute(x, COL, pairs)]
    ppermute x2 -> x1, starting transfers between devices: 7.83 us -> 4.5 us  [swap_axes(): return lax.ppermute(x, (ROW, COL), pairs)]
    ppermute x13, waiting for transfers between devices: 5.74 us -> 8.58 us  [row_permute(): return lax.ppermute(x, ROW, pairs)]
    pallas_call x1, Pallas kernels: 5.59 us -> 8.18 us  [right_form(): pl.pallas_call(right_form_kernel, out_shape=shape_of(1296, 1536), in_spec...]
  transfers between devices with their start and end apart: 21 -> 20, of which waited for: 9 -> 10; matrix products, arithmetic and copies ran while one was open for 8% -> 0% of each run, Pallas kernels for 19% -> 33%
where the time goes in v3:
time: 110 us
  Pallas kernels  54.5 us (50%)
  starting transfers between devices  40.9 us (37%)
  waiting for transfers between devices  12.7 us (12%)
    ppermute x6, starting transfers between devices, col_permute(): return lax.ppermute(x, COL, pairs)  22.3 us
    pallas_call x1, Pallas kernels, left(): pl.pallas_call(left_kernel, out_shape=(shape_of(216, 216), shape_of(128,...  14.5 us
    ppermute x13, starting transfers between devices, row_permute(): return lax.ppermute(x, ROW, pairs)  14.1 us
    pallas_call x1, Pallas kernels, upper(): pl.pallas_call(upper_kernel, out_shape=(shape_of(216, 216), shape_of(6, 2...  11.9 us
    pallas_call x1, Pallas kernels, left_forms(): pl.pallas_call(left_forms_kernel, out_shape=(shape_of(1296, 1408), shape_...  9.46 us
    ppermute x13, waiting for transfers between devices, row_permute(): return lax.ppermute(x, ROW, pairs)  8.58 us
    pallas_call x1, Pallas kernels, right_form(): pl.pallas_call(right_form_kernel, out_shape=shape_of(1296, 1536), in_spec...  8.18 us
    pallas_call x1, Pallas kernels, flat_form(): pl.pallas_call(flat_form_kernel, out_shape=shape_of(1296, 1408), in_specs...  6.89 us
  transfers between devices with their start and end apart: 20, of which 10 were waited for; matrix products, arithmetic and copies ran while one was open for 0% of the time, Pallas kernels for 33%

profile of v3, /device:TPU:1, one launch (start us, length us, event | category | flops | bytes accessed | tf_op | source)
XLA Modules:
  0.0 109.7 jit_solution(9477000735032168206)
XLA Ops:
  0.6 1.8 %prepare.1 = (bf16[16,216]{1,0:T(8,128)(2,1)}, bf16[64,128]{1,0:T(8,128)(2,1)}, bf16[200,216]{1,0:T(8,128)(2,1)}) custom-call(bf16[6,6,36]{2,1,0:T(8,128)(2,1)} %refs_0_.1, bf16[6,6,36]{2,1,0:T(8,128)(2,1)} %refs_1_.1, bf16[6,6,36]{2,1,0:T(8,128)(2,1)} %refs_2_.1, bf16[6,6,36]{2,1,0:T(8,128)(2,1)} %refs_3_.1, bf16[6,96]{1,0:T(8,128)(2,1)} %bitcast.10, ...), custom_call_target="tpu_custom_call" | custom-call | tf_op jit(solution)/shard_map/prepare/pallas_call | solution.py:246
  2.5 4.5 %collective-permute-start = (bf16[200,216]{1,0:T(8,128)(2,1)}, bf16[200,216]{1,0:T(8,128)(2,1)S(1)}, u32[]{:S(2)}, u32[]{:S(2)}) collective-permute-start(bf16[200,216]{1,0:T(8,128)(2,1)} %get-tuple-element.33), channel_id=1, source_target_pairs={{0,0},{1,16},{2,32},{3,48},{4,64},{5,80},{6,96},{7,112},{8,128},{9... | collective-permute-start | bytes 259208 | tf_op jit(solution)/shard_map/ppermute | solution.py:430
  7.0 0.0 copy-start
  7.0 0.0 copy-start.1
  7.0 6.9 %flat_form.1.s_hbm = bf16[1296,1408]{1,0:T(8,128)(2,1)} custom-call(bf16[13122,128]{1,0:T(8,128)(2,1)} %bitcast.13), custom_call_target="tpu_custom_call" | custom-call | flops 3221225472 | bytes 4194304 | tf_op jit(solution)/shard_map/flat_form/pallas_call | solution.py:388
  13.9 0.0 collective-permute-done.turned
  13.9 0.0 copy-done
  13.9 0.2 pieces.1
  14.2 3.2 %collective-permute-start.1 = (bf16[24,216]{1,0:T(8,128)(2,1)S(1)}, bf16[24,216]{1,0:T(8,128)(2,1)S(1)}, u32[]{:S(2)}, u32[]{:S(2)}) collective-permute-start(bf16[24,216]{1,0:T(8,128)(2,1)S(1)} %get-tuple-element.37), channel_id=1, source_target_pairs={{0,4},{1,5},{2,6},{3,7},{4,8},{5,9},{6,10},{7,11},{8,12},{9,13},{1... | collective-permute-start | bytes 31112 | tf_op jit(solution)/shard_map/ppermute | solution.py:425
  17.3 7.8 %collective-permute-start.2 = (bf16[24,216]{1,0:T(8,128)(2,1)S(1)}, bf16[24,216]{1,0:T(8,128)(2,1)S(1)}, u32[]{:S(2)}, u32[]{:S(2)}) collective-permute-start(bf16[24,216]{1,0:T(8,128)(2,1)S(1)} %get-tuple-element.37), channel_id=1, source_target_pairs={{0,8},{1,9},{2,10},{3,11},{4,12},{5,13},{6,14},{7,15},{8,0},{9,1},... | collective-permute-start | bytes 31112 | tf_op jit(solution)/shard_map/ppermute | solution.py:425
  25.1 3.5 %collective-permute-start.3 = (bf16[24,216]{1,0:T(8,128)(2,1)S(1)}, bf16[24,216]{1,0:T(8,128)(2,1)S(1)}, u32[]{:S(2)}, u32[]{:S(2)}) collective-permute-start(bf16[24,216]{1,0:T(8,128)(2,1)S(1)} %get-tuple-element.37), channel_id=1, source_target_pairs={{0,12},{1,13},{2,14},{3,15},{4,0},{5,1},{6,2},{7,3},{8,4},{9,5},{1... | collective-permute-start | bytes 31112 | tf_op jit(solution)/shard_map/ppermute | solution.py:425
  28.6 0.0 collective-permute-done.1
  28.6 0.0 collective-permute-done.2
  28.6 0.8 collective-permute-done.3
  29.4 0.0 collective-permute-start.4
  29.5 7.8 %collective-permute-start.5 = (bf16[96,216]{1,0:T(8,128)(2,1)S(1)}, bf16[96,216]{1,0:T(8,128)(2,1)S(1)}, u32[]{:S(2)}, u32[]{:S(2)}) collective-permute-start(bf16[96,216]{1,0:T(8,128)(2,1)S(1)} %get-tuple-element.70), channel_id=1, source_target_pairs={{0,2},{1,3},{2,0},{3,1},{4,6},{5,7},{6,4},{7,5},{8,10},{9,11},{10,... | collective-permute-start | bytes 124424 | tf_op jit(solution)/shard_map/ppermute | solution.py:425
  37.3 0.0 collective-permute-start.6
  37.3 0.2 collective-permute-done.4
  37.5 1.7 %collective-permute-done.5 = bf16[96,216]{1,0:T(8,128)(2,1)S(1)} collective-permute-done((bf16[96,216]{1,0:T(8,128)(2,1)S(1)}, bf16[96,216]{1,0:T(8,128)(2,1)S(1)}, u32[]{:S(2)}, u32[]{:S(2)}) %collective-permute-start.5) | collective-permute-done | bytes 41504 | tf_op jit(solution)/shard_map/ppermute | solution.py:425
  39.2 1.4 %collective-permute-done.6 = bf16[96,216]{1,0:T(8,128)(2,1)S(1)} collective-permute-done((bf16[96,216]{1,0:T(8,128)(2,1)S(1)}, bf16[96,216]{1,0:T(8,128)(2,1)S(1)}, u32[]{:S(2)}, u32[]{:S(2)}) %collective-permute-start.6) | collective-permute-done | bytes 41504 | tf_op jit(solution)/shard_map/ppermute | solution.py:425
  40.7 0.4 convolution_convert_fusion
  41.1 0.0 copy-done.1
  41.1 0.1 collective-permute-start.7
  41.3 3.8 %collective-permute-done.7 = bf16[512,128]{1,0:T(8,128)(2,1)S(1)} collective-permute-done((bf16[512,128]{1,0:T(8,128)(2,1)S(1)}, bf16[512,128]{1,0:T(8,128)(2,1)S(1)}, u32[]{:S(2)}, u32[]{:S(2)}) %collective-permute-start.7) | collective-permute-done | bytes 131104 | tf_op jit(solution)/shard_map/ppermute | solution.py:416
  45.0 0.8 collective-permute-start.10
  45.9 4.2 %collective-permute-start.11 = (bf16[1024,128]{1,0:T(8,128)(2,1)S(1)}, bf16[1024,128]{1,0:T(8,128)(2,1)S(1)}, u32[]{:S(2)}, u32[]{:S(2)}) collective-permute-start(bf16[1024,128]{1,0:T(8,128)(2,1)S(1)} %constant_dynamic-update-slice_fusion.11.refs_0_), channel_id=1, source_target_pairs={{0,16},{16,0},{32,48},{48,32},{64,80},{80,64},{96,112},{112,96},{1... | collective-permute-start | bytes 786440 | tf_op jit(solution)/shard_map/ppermute | solution.py:416
  50.0 1.3 %collective-permute-start.8 = (bf16[1024,128]{1,0:T(8,128)(2,1)S(1)}, bf16[1024,128]{1,0:T(8,128)(2,1)S(1)}, u32[]{:S(2)}, u32[]{:S(2)}) collective-permute-start(bf16[1024,128]{1,0:T(8,128)(2,1)S(1)} %constant_dynamic-update-slice_fusion.11.refs_0_), channel_id=1, source_target_pairs={{0,64},{16,80},{32,96},{48,112},{64,128},{80,144},{96,160},{112,17... | collective-permute-start | bytes 786440 | tf_op jit(solution)/shard_map/ppermute | solution.py:416
  51.4 2.7 %collective-permute-start.9 = (bf16[1024,128]{1,0:T(8,128)(2,1)S(1)}, bf16[1024,128]{1,0:T(8,128)(2,1)S(1)}, u32[]{:S(2)}, u32[]{:S(2)}) collective-permute-start(bf16[1024,128]{1,0:T(8,128)(2,1)S(1)} %constant_dynamic-update-slice_fusion.11.refs_0_), channel_id=1, source_target_pairs={{0,128},{16,144},{32,160},{48,176},{64,192},{80,208},{96,224},{112... | collective-permute-start | bytes 786440 | tf_op jit(solution)/shard_map/ppermute | solution.py:416
  54.1 9.5 %left_forms.1 = (bf16[1296,1408]{1,0:T(8,128)(2,1)}, bf16[1296,1536]{1,0:T(8,128)(2,1)}) custom-call(bf16[1296,1408]{1,0:T(8,128)(2,1)} %flat_form.1.s_hbm), custom_call_target="tpu_custom_call" | custom-call | flops 4294967296 | bytes 4194304 | tf_op jit(solution)/shard_map/left_forms/pallas_call | solution.py:401
  63.5 0.0 collective-permute-done.10.refs_3_
  63.5 0.0 collective-permute-done.11.refs_4_
  63.5 0.0 collective-permute-done.8.refs_1_
  63.5 2.5 %collective-permute-done.9.refs_2_ = bf16[1024,128]{1,0:T(8,128)(2,1)S(1)} collective-permute-done((bf16[1024,128]{1,0:T(8,128)(2,1)S(1)}, bf16[1024,128]{1,0:T(8,128)(2,1)S(1)}, u32[]{:S(2)}, u32[]{:S(2)}) %collective-permute-start.9) | collective-permute-done | bytes 262176 | tf_op jit(solution)/shard_map/ppermute | solution.py:416
  66.1 0.9 collective-permute-start.12
  66.9 0.0 collective-permute-start.13
  66.9 0.5 collective-permute-start.14
  67.5 0.6 collective-permute-done.12.refs_5_
  68.1 0.4 collective-permute-done.13.refs_6_
  68.5 0.4 collective-permute-done.14.refs_7_
  68.8 0.9 gather_small.1.refs_8_
  69.8 14.5 %left.1 = (bf16[216,216]{1,0:T(8,128)(2,1)}, f32[128,256]{1,0:T(8,128)S(1)}) custom-call(s32[16]{0:T(128)S(1)} %fusion.26.order_ref, bf16[1024,128]{1,0:T(8,128)(2,1)S(1)} %constant_dynamic-update-slice_fusion.11.refs_0_, bf16[1024,128]{1,0:T(8,128)(2,1)S(1)} %collective-permute-done.8.refs_1_, bf16[1024,128]{1,0:T(8,128)(2,1)S(1)} %collective-permute-done.9.refs_2_, ...), custom_call_target="tpu_custom_call" | custom-call | flops 8589934592 | bytes 4194304 | tf_op jit(solution)/shard_map/left/pallas_call | solution.py:271
  84.3 0.5 collective-permute-start.15
  84.7 0.9 collective-permute-done.15
  85.7 0.1 collective-permute-start.16
  85.8 8.2 %right_form.1.refs_10_ = bf16[1296,1536]{1,0:T(8,128)(2,1)} custom-call(bf16[1296,1408]{1,0:T(8,128)(2,1)} %flat_form.1.s_hbm), custom_call_target="tpu_custom_call" | custom-call | flops 3221225472 | bytes 4194304 | tf_op jit(solution)/shard_map/right_form/pallas_call | solution.py:395
  94.0 0.0 collective-permute-done.16
  94.0 0.1 collective-permute-start.17
  94.1 1.0 collective-permute-start.18
  95.1 2.0 %collective-permute-start.19 = (f32[8,256]{1,0:T(8,128)S(1)}, f32[8,256]{1,0:T(8,128)S(1)}, u32[]{:S(2)}, u32[]{:S(2)}) collective-permute-start(f32[8,256]{1,0:T(8,128)S(1)} %get-tuple-element.67), channel_id=1, source_target_pairs={{0,192},{16,208},{32,224},{48,240},{64,0},{80,16},{96,32},{112,48}... | collective-permute-start | bytes 24584 | tf_op jit(solution)/shard_map/ppermute | solution.py:416
  97.1 11.9 %upper.1 = (bf16[216,216]{1,0:T(8,128)(2,1)}, bf16[6,216]{1,0:T(8,128)(2,1)}) custom-call(s32[16]{0:T(128)S(1)} %fusion.26.order_ref, bf16[1024,128]{1,0:T(8,128)(2,1)S(1)} %constant_dynamic-update-slice_fusion.11.refs_0_, bf16[1024,128]{1,0:T(8,128)(2,1)S(1)} %collective-permute-done.8.refs_1_, bf16[1024,128]{1,0:T(8,128)(2,1)S(1)} %collective-permute-done.9.refs_2_, ...), custom_call_target="tpu_custom_call" | custom-call | flops 8589934592 | bytes 4194304 | tf_op jit(solution)/shard_map/upper/pallas_call | solution.py:264
  109.0 0.0 collective-permute-done.17.one
  109.0 0.0 collective-permute-done.18.two
  109.0 0.0 collective-permute-done.19.three
  109.0 0.7 finish.1
  (20 shorter events, 0.2 us)
Async XLA Ops:
  2.5 11.4 %collective-permute-start = (bf16[200,216]{1,0:T(8,128)(2,1)}, bf16[200,216]{1,0:T(8,128)(2,1)S(1)}, u32[]{:S(2)}, u32[]{:S(2)}) collective-permute-start(bf16[200,216]{1,0:T(8,128)(2,1)} %get-tuple-element.33), channel_id=1, source_target_pairs={{0,0},{1,16},{2,32},{3,48},{4,64},{5,80},{6,96},{7,112},{8,128},{9... | collective-permute-start | bytes 259208 | tf_op jit(solution)/shard_map/ppermute | solution.py:430
  7.0 7.0 %copy-start = (bf16[16,216]{1,0:T(8,128)(2,1)S(1)}, bf16[16,216]{1,0:T(8,128)(2,1)}, u32[]{:S(2)}) copy-start(bf16[16,216]{1,0:T(8,128)(2,1)} %get-tuple-element.36.piece) | copy-start | bytes 20740
  7.0 34.1 %copy-start.1 = (bf16[64,128]{1,0:T(8,128)(2,1)S(1)}, bf16[64,128]{1,0:T(8,128)(2,1)}, u32[]{:S(2)}) copy-start(bf16[64,128]{1,0:T(8,128)(2,1)} %get-tuple-element.38) | copy-start | bytes 49156
  14.2 14.4 %collective-permute-start.1 = (bf16[24,216]{1,0:T(8,128)(2,1)S(1)}, bf16[24,216]{1,0:T(8,128)(2,1)S(1)}, u32[]{:S(2)}, u32[]{:S(2)}) collective-permute-start(bf16[24,216]{1,0:T(8,128)(2,1)S(1)} %get-tuple-element.37), channel_id=1, source_target_pairs={{0,4},{1,5},{2,6},{3,7},{4,8},{5,9},{6,10},{7,11},{8,12},{9,13},{1... | collective-permute-start | bytes 31112 | tf_op jit(solution)/shard_map/ppermute | solution.py:425
  17.3 11.3 %collective-permute-start.2 = (bf16[24,216]{1,0:T(8,128)(2,1)S(1)}, bf16[24,216]{1,0:T(8,128)(2,1)S(1)}, u32[]{:S(2)}, u32[]{:S(2)}) collective-permute-start(bf16[24,216]{1,0:T(8,128)(2,1)S(1)} %get-tuple-element.37), channel_id=1, source_target_pairs={{0,8},{1,9},{2,10},{3,11},{4,12},{5,13},{6,14},{7,15},{8,0},{9,1},... | collective-permute-start | bytes 31112 | tf_op jit(solution)/shard_map/ppermute | solution.py:425
  25.1 4.3 %collective-permute-start.3 = (bf16[24,216]{1,0:T(8,128)(2,1)S(1)}, bf16[24,216]{1,0:T(8,128)(2,1)S(1)}, u32[]{:S(2)}, u32[]{:S(2)}) collective-permute-start(bf16[24,216]{1,0:T(8,128)(2,1)S(1)} %get-tuple-element.37), channel_id=1, source_target_pairs={{0,12},{1,13},{2,14},{3,15},{4,0},{5,1},{6,2},{7,3},{8,4},{9,5},{1... | collective-permute-start | bytes 31112 | tf_op jit(solution)/shard_map/ppermute | solution.py:425
  29.4 8.1 %collective-permute-start.4 = (bf16[96,216]{1,0:T(8,128)(2,1)S(1)}, bf16[96,216]{1,0:T(8,128)(2,1)S(1)}, u32[]{:S(2)}, u32[]{:S(2)}) collective-permute-start(bf16[96,216]{1,0:T(8,128)(2,1)S(1)} %get-tuple-element.70), channel_id=1, source_target_pairs={{0,1},{1,2},{2,3},{3,0},{4,5},{5,6},{6,7},{7,4},{8,9},{9,10},{10,1... | collective-permute-start | bytes 124424 | tf_op jit(solution)/shard_map/ppermute | solution.py:425
  29.5 9.8 %collective-permute-start.5 = (bf16[96,216]{1,0:T(8,128)(2,1)S(1)}, bf16[96,216]{1,0:T(8,128)(2,1)S(1)}, u32[]{:S(2)}, u32[]{:S(2)}) collective-permute-start(bf16[96,216]{1,0:T(8,128)(2,1)S(1)} %get-tuple-element.70), channel_id=1, source_target_pairs={{0,2},{1,3},{2,0},{3,1},{4,6},{5,7},{6,4},{7,5},{8,10},{9,11},{10,... | collective-permute-start | bytes 124424 | tf_op jit(solution)/shard_map/ppermute | solution.py:425
  37.3 3.4 %collective-permute-start.6 = (bf16[96,216]{1,0:T(8,128)(2,1)S(1)}, bf16[96,216]{1,0:T(8,128)(2,1)S(1)}, u32[]{:S(2)}, u32[]{:S(2)}) collective-permute-start(bf16[96,216]{1,0:T(8,128)(2,1)S(1)} %get-tuple-element.70), channel_id=1, source_target_pairs={{0,3},{1,0},{2,1},{3,2},{4,7},{5,4},{6,5},{7,6},{8,11},{9,8},{10,9... | collective-permute-start | bytes 124424 | tf_op jit(solution)/shard_map/ppermute | solution.py:425
  41.1 3.9 %collective-permute-start.7 = (bf16[512,128]{1,0:T(8,128)(2,1)S(1)}, bf16[512,128]{1,0:T(8,128)(2,1)S(1)}, u32[]{:S(2)}, u32[]{:S(2)}) collective-permute-start(bf16[512,128]{1,0:T(8,128)(2,1)S(1)} %pad_maximum_fusion), channel_id=1, source_target_pairs={{0,32},{16,48},{32,0},{48,16},{64,96},{80,112},{96,64},{112,80},{1... | collective-permute-start | bytes 393224 | tf_op jit(solution)/shard_map/ppermute | solution.py:416
  45.0 18.5 %collective-permute-start.10 = (bf16[1024,128]{1,0:T(8,128)(2,1)S(1)}, bf16[1024,128]{1,0:T(8,128)(2,1)S(1)}, u32[]{:S(2)}, u32[]{:S(2)}) collective-permute-start(bf16[1024,128]{1,0:T(8,128)(2,1)S(1)} %constant_dynamic-update-slice_fusion.11.refs_0_), channel_id=1, source_target_pairs={{0,192},{16,208},{32,224},{48,240},{64,0},{80,16},{96,32},{112,48}... | collective-permute-start | bytes 786440 | tf_op jit(solution)/shard_map/ppermute | solution.py:416
  45.9 17.7 %collective-permute-start.11 = (bf16[1024,128]{1,0:T(8,128)(2,1)S(1)}, bf16[1024,128]{1,0:T(8,128)(2,1)S(1)}, u32[]{:S(2)}, u32[]{:S(2)}) collective-permute-start(bf16[1024,128]{1,0:T(8,128)(2,1)S(1)} %constant_dynamic-update-slice_fusion.11.refs_0_), channel_id=1, source_target_pairs={{0,16},{16,0},{32,48},{48,32},{64,80},{80,64},{96,112},{112,96},{1... | collective-permute-start | bytes 786440 | tf_op jit(solution)/shard_map/ppermute | solution.py:416
  50.0 13.5 %collective-permute-start.8 = (bf16[1024,128]{1,0:T(8,128)(2,1)S(1)}, bf16[1024,128]{1,0:T(8,128)(2,1)S(1)}, u32[]{:S(2)}, u32[]{:S(2)}) collective-permute-start(bf16[1024,128]{1,0:T(8,128)(2,1)S(1)} %constant_dynamic-update-slice_fusion.11.refs_0_), channel_id=1, source_target_pairs={{0,64},{16,80},{32,96},{48,112},{64,128},{80,144},{96,160},{112,17... | collective-permute-start | bytes 786440 | tf_op jit(solution)/shard_map/ppermute | solution.py:416
  51.4 14.7 %collective-permute-start.9 = (bf16[1024,128]{1,0:T(8,128)(2,1)S(1)}, bf16[1024,128]{1,0:T(8,128)(2,1)S(1)}, u32[]{:S(2)}, u32[]{:S(2)}) collective-permute-start(bf16[1024,128]{1,0:T(8,128)(2,1)S(1)} %constant_dynamic-update-slice_fusion.11.refs_0_), channel_id=1, source_target_pairs={{0,128},{16,144},{32,160},{48,176},{64,192},{80,208},{96,224},{112... | collective-permute-start | bytes 786440 | tf_op jit(solution)/shard_map/ppermute | solution.py:416
  66.1 2.0 %collective-permute-start.12 = (bf16[1024,128]{1,0:T(8,128)(2,1)S(1)}, bf16[1024,128]{1,0:T(8,128)(2,1)S(1)}, u32[]{:S(2)}, u32[]{:S(2)}) collective-permute-start(bf16[1024,128]{1,0:T(8,128)(2,1)S(1)} %collective-permute-done.8.refs_1_), channel_id=1, source_target_pairs={{0,16},{16,0},{32,48},{48,32},{64,80},{80,64},{96,112},{112,96},{1... | collective-permute-start | bytes 786440 | tf_op jit(solution)/shard_map/ppermute | solution.py:416
  66.9 1.5 %collective-permute-start.13 = (bf16[1024,128]{1,0:T(8,128)(2,1)S(1)}, bf16[1024,128]{1,0:T(8,128)(2,1)S(1)}, u32[]{:S(2)}, u32[]{:S(2)}) collective-permute-start(bf16[1024,128]{1,0:T(8,128)(2,1)S(1)} %collective-permute-done.9.refs_2_), channel_id=1, source_target_pairs={{0,16},{16,0},{32,48},{48,32},{64,80},{80,64},{96,112},{112,96},{1... | collective-permute-start | bytes 786440 | tf_op jit(solution)/shard_map/ppermute | solution.py:416
  66.9 1.9 %collective-permute-start.14 = (bf16[1024,128]{1,0:T(8,128)(2,1)S(1)}, bf16[1024,128]{1,0:T(8,128)(2,1)S(1)}, u32[]{:S(2)}, u32[]{:S(2)}) collective-permute-start(bf16[1024,128]{1,0:T(8,128)(2,1)S(1)} %collective-permute-done.10.refs_3_), channel_id=1, source_target_pairs={{0,16},{16,0},{32,48},{48,32},{64,80},{80,64},{96,112},{112,96},{1... | collective-permute-start | bytes 786440 | tf_op jit(solution)/shard_map/ppermute | solution.py:416
  84.3 1.4 %collective-permute-start.15 = (f32[64,256]{1,0:T(8,128)S(1)}, f32[64,256]{1,0:T(8,128)S(1)}, u32[]{:S(2)}, u32[]{:S(2)}) collective-permute-start(f32[64,256]{1,0:T(8,128)S(1)} %constant_dynamic-slice_fusion.5), channel_id=1, source_target_pairs={{0,16},{16,0},{32,48},{48,32},{64,80},{80,64},{96,112},{112,96},{1... | collective-permute-start | bytes 196616 | tf_op jit(solution)/shard_map/ppermute | solution.py:416
  85.7 8.3 %collective-permute-start.16 = (f32[32,256]{1,0:T(8,128)S(1)}, f32[32,256]{1,0:T(8,128)S(1)}, u32[]{:S(2)}, u32[]{:S(2)}) collective-permute-start(f32[32,256]{1,0:T(8,128)S(1)} %constant_dynamic-slice_fusion.4), channel_id=1, source_target_pairs={{0,32},{16,48},{32,0},{48,16},{64,96},{80,112},{96,64},{112,80},{1... | collective-permute-start | bytes 98312 | tf_op jit(solution)/shard_map/ppermute | solution.py:416
  94.0 15.0 %collective-permute-start.17 = (f32[8,256]{1,0:T(8,128)S(1)}, f32[8,256]{1,0:T(8,128)S(1)}, u32[]{:S(2)}, u32[]{:S(2)}) collective-permute-start(f32[8,256]{1,0:T(8,128)S(1)} %get-tuple-element.69), channel_id=1, source_target_pairs={{0,64},{16,80},{32,96},{48,112},{64,128},{80,144},{96,160},{112,17... | collective-permute-start | bytes 24584 | tf_op jit(solution)/shard_map/ppermute | solution.py:416
  94.1 14.9 %collective-permute-start.18 = (f32[8,256]{1,0:T(8,128)S(1)}, f32[8,256]{1,0:T(8,128)S(1)}, u32[]{:S(2)}, u32[]{:S(2)}) collective-permute-start(f32[8,256]{1,0:T(8,128)S(1)} %get-tuple-element.68), channel_id=1, source_target_pairs={{0,128},{16,144},{32,160},{48,176},{64,192},{80,208},{96,224},{112... | collective-permute-start | bytes 24584 | tf_op jit(solution)/shard_map/ppermute | solution.py:416
  95.1 13.9 %collective-permute-start.19 = (f32[8,256]{1,0:T(8,128)S(1)}, f32[8,256]{1,0:T(8,128)S(1)}, u32[]{:S(2)}, u32[]{:S(2)}) collective-permute-start(f32[8,256]{1,0:T(8,128)S(1)} %get-tuple-element.67), channel_id=1, source_target_pairs={{0,192},{16,208},{32,224},{48,240},{64,0},{80,16},{96,32},{112,48}... | collective-permute-start | bytes 24584 | tf_op jit(solution)/shard_map/ppermute | solution.py:416

commit v4 on v3

--- a/solution.py
+++ b/solution.py
@@ -39,7 +39,7 @@
     return copies
 
 
-def prepare_kernel(*refs):
+def prepare_kernel(at_ref, *refs):
     hbm, (piece, pack, turned), local, sems = refs[:9], refs[9:12], refs[12:21], refs[21]
     for cp in load(list(zip(hbm, local)), sems):
         cp.wait()
@@ -53,9 +53,12 @@
     for e in (te, re, be):
         v = e[...].astype(F)
         parts.append(jnp.concatenate([v[:, j, :] for j in range(6)], axis=1))
-    turned[0:96, :] = tpt[...]
-    turned[96:192, :] = bpt[...]
-    turned[192:200, :] = jnp.concatenate([parts[2].astype(B), zero], axis=0)
+    row = lax.broadcasted_iota(jnp.int32, (8, 96), 0)
+    lane = lax.broadcasted_iota(jnp.int32, (8, 96), 1)
+    pick = ((lane == at_ref[0] + row) & (row < 6)).astype(B)
+    turned[0:8, :] = dot(pick, tpt[...]).astype(B)
+    turned[8:16, :] = dot(pick, bpt[...]).astype(B)
+    turned[16:24, :] = jnp.concatenate([parts[2].astype(B), zero], axis=0)
     for c in (uct, rct, lct):
         parts.append(c[...].astype(F))
     flat = jnp.concatenate(parts + [jnp.zeros((6, 88), F)], axis=1)
@@ -64,20 +67,17 @@
         pack[8 * k:8 * k + 8, :] = flat[:, 128 * k:128 * k + 128]
 
 
-def pieces_kernel(at_ref, turned, piece, out, tpx, bpr):
+def pieces_kernel(turned, piece, out, tpx, bpr):
     out[0:16, :] = piece[...]
-    out[16:24, :] = turned[192:200, :]
-    row = lax.broadcasted_iota(jnp.int32, (8, 96), 0)
-    lane = lax.broadcasted_iota(jnp.int32, (8, 96), 1)
-    pick = ((lane == at_ref[0] + row) & (row < 6)).astype(B)
-    top = dot(pick, turned[0:96, :])
+    out[16:24, :] = turned[16:24, :]
+    top = turned[0:8, :].astype(F)
     flat = jnp.concatenate(
         [jnp.concatenate([top[x:x + 1, b * 36:(b + 1) * 36] for x in range(6)], axis=1) for b in range(6)], axis=0)
     flat = jnp.concatenate([flat, jnp.zeros((6, 40), F)], axis=1)
     flat = jnp.concatenate([flat, jnp.zeros((2, 256), F)], axis=0).astype(B)
     tpx[0:8, :] = flat[:, :128]
     tpx[8:16, :] = flat[:, 128:]
-    bottom = dot(pick, turned[96:192, :])
+    bottom = turned[8:16, :].astype(F)
     gap = jnp.zeros((8, 4), F)
     bpr[...] = jnp.concatenate([y for b in range(6) for y in (bottom[:, b * 36:(b + 1) * 36], gap)], axis=1).astype(B)
 
@@ -242,18 +242,18 @@
             pltpu.VMEM((1536, 768), B), pltpu.VMEM((6, 1440, 128), F), pltpu.VMEM((6, 1440, 128), F)]
 
 
-def prepare(*args):
+def prepare(at, *args):
     return pl.pallas_call(
-        prepare_kernel, out_shape=(shape_of(16, 216), shape_of(64, 128), shape_of(200, 216)),
-        in_specs=[HB] * 9, out_specs=(VM,) * 3,
+        prepare_kernel, out_shape=(shape_of(16, 216), shape_of(64, 128), shape_of(24, 216)),
+        in_specs=[SM] + [HB] * 9, out_specs=(VM,) * 3,
         scratch_shapes=[pltpu.VMEM(x.shape, B) for x in args] + [pltpu.SemaphoreType.DMA((9,))],
-        name="prepare")(*args)
-
-
-def pieces(at, turned, piece):
+        name="prepare")(at, *args)
+
+
+def pieces(turned, piece):
     return pl.pallas_call(pieces_kernel, out_shape=(shape_of(24, 216), shape_of(16, 128), shape_of(8, 240)),
-                          in_specs=[SM, VM, VM], out_specs=(VM,) * 3, name="pieces",
-                          compiler_params=params(4))(at, turned, piece)
+                          in_specs=[VM, VM], out_specs=(VM,) * 3, name="pieces",
+                          compiler_params=params(4))(turned, piece)
 
 
 def form_copies():
@@ -297,10 +297,19 @@
     z_ref[...] = dot(a_ref[:, pl.ds(base, 256)], sel)
 
 
-def realign(a_ref, z_ref, o_ref, out_hbm, sem):
+def column_chunks(src, dst, sems):
+    ends = (0, 384, 768, 1152, 1408)
+    return load([(src.at[:, p:q], dst.at[:, p:q]) for p, q in zip(ends, ends[1:])], sems)
+
+
+def realign(a_ref, z_ref, o_ref, out_hbm, sem, chunks=()):
     lane = lax.broadcasted_iota(jnp.int32, (36, 128), 1)
 
     def f(g, _):
+        for n, cp in zip((0, 2, 4, 7), chunks):
+            @pl.when(g == n)
+            def _(cp=cp):
+                cp.wait()
         strips = []
         for h in range(2):
             lanes_shifted(a_ref, z_ref.at[h], 2 * g + h)
@@ -325,15 +334,16 @@
 
 
 def right_form_kernel(s_hbm, wright_hbm, apad, z, o, sems, done):
-    load([(s_hbm, apad)], sems)[0].wait()
-    realign(apad, z, o, wright_hbm, done)
+    realign(apad, z, o, wright_hbm, done, column_chunks(s_hbm, apad, sems))
 
 
 def left_forms_kernel(s_hbm, wtop_hbm, wbot_hbm, apad, z, o, sems, done, s_ref):
-    load([(s_hbm, s_ref)], sems)[0].wait()
+    chunks = column_chunks(s_hbm, s_ref, sems)
     eye = (lax.broadcasted_iota(jnp.int32, (128, 128), 0) == lax.broadcasted_iota(jnp.int32, (128, 128), 1)).astype(B)
     for b in range(11):
         n = min(128, 1296 - b * 128)
+        if b % 3 == 0:
+            chunks[b // 3].wait()
         apad[b * 128:b * 128 + n, :1296] = dot(eye[:n, :n], s_ref[:, b * 128:b * 128 + n], NT).astype(B)
     apad[:, 1296:1408] = jnp.zeros((1296, 112), B)
     out = pltpu.make_async_copy(apad, wtop_hbm, sems.at[0])
@@ -381,7 +391,7 @@
 
 def form_scratch():
     return [pltpu.VMEM((1296, 1408), B), pltpu.VMEM((2, 1296, 256), F), pltpu.VMEM((1296, 1536), B),
-            pltpu.SemaphoreType.DMA((1,)), pltpu.SemaphoreType.DMA((9,))]
+            pltpu.SemaphoreType.DMA((4,)), pltpu.SemaphoreType.DMA((9,))]
 
 
 def flat_form(flat):
@@ -453,11 +463,11 @@
     zhi, x = c // 4, c % 4
     hold = lax.optimization_barrier
 
-    piece, pack, turned = prepare(te, re, be, le, uc.T, rc.T, lc.T, tp.T, bp.T)
+    piece, pack, turned = prepare((r * 6).astype(jnp.int32).reshape(1), te, re, be, le, uc.T, rc.T, lc.T, tp.T, bp.T)
     swapped = swap_axes(turned)
     s2 = flat_form(hold((site_flat, turned))[0].reshape(13122, 128))
     swapped, s2 = hold((swapped, s2))
-    piece, tpx, bpr = pieces((c * 6).astype(jnp.int32).reshape(1), swapped, piece)
+    piece, tpx, bpr = pieces(swapped, piece)
 
     piece = stacked(piece, [col_permute(piece, lambda z, i, s=s: ((z + s) % 4, i)) for s in (1, 2, 3)])
     piece = stacked(piece, [col_permute(piece, lambda z, i, s=s: (z, (i + s) % 4)) for s in (1, 2, 3)])

time: 110 us -> 106 us (0.964)
  starting transfers between devices: 40.9 us -> 36.8 us
  waiting for transfers between devices: 12.7 us -> 14.1 us
  Pallas kernels: 54.5 us -> 53.3 us
    ppermute x6, starting transfers between devices: 22.3 us -> 16.7 us  [col_permute(): return lax.ppermute(x, COL, pairs)]
    ppermute x13, waiting for transfers between devices: 8.58 us -> 10.6 us  [row_permute(): return lax.ppermute(x, ROW, pairs)]
    ppermute x13, starting transfers between devices: 14.1 us -> 15.7 us  [row_permute(): return lax.ppermute(x, ROW, pairs)]
  transfers between devices with their start and end apart: 20 -> 20, of which waited for: 10 -> 9; matrix products, arithmetic and copies ran while one was open for 0% -> 0% of each run, Pallas kernels for 33% -> 33%
where the time goes in v4:
time: 106 us
  Pallas kernels  53.3 us (50%)
  starting transfers between devices  36.8 us (35%)
  waiting for transfers between devices  14.1 us (13%)
    ppermute x6, starting transfers between devices, col_permute(): return lax.ppermute(x, COL, pairs)  16.7 us
    ppermute x13, starting transfers between devices, row_permute(): return lax.ppermute(x, ROW, pairs)  15.7 us
    pallas_call x1, Pallas kernels, left(): pl.pallas_call(left_kernel, out_shape=(shape_of(216, 216), shape_of(128,...  14.5 us
    pallas_call x1, Pallas kernels, upper(): pl.pallas_call(upper_kernel, out_shape=(shape_of(216, 216), shape_of(6, 2...  11.9 us
    ppermute x13, waiting for transfers between devices, row_permute(): return lax.ppermute(x, ROW, pairs)  10.6 us
    pallas_call x1, Pallas kernels, left_forms(): pl.pallas_call(left_forms_kernel, out_shape=(shape_of(1296, 1408), shape_...  9.15 us
    pallas_call x1, Pallas kernels, right_form(): pl.pallas_call(right_form_kernel, out_shape=shape_of(1296, 1536), in_spec...  7.38 us
    pallas_call x1, Pallas kernels, flat_form(): pl.pallas_call(flat_form_kernel, out_shape=shape_of(1296, 1408), in_specs...  6.89 us
  transfers between devices with their start and end apart: 20, of which 9 were waited for; matrix products, arithmetic and copies ran while one was open for 0% of the time, Pallas kernels for 33%

profile of v4, /device:TPU:1, one launch (start us, length us, event | category | flops | bytes accessed | tf_op | source)
XLA Modules:
  0.0 105.8 jit_solution(15497971199861131132)
XLA Ops:
  0.6 1.8 %prepare.1 = (bf16[16,216]{1,0:T(8,128)(2,1)}, bf16[64,128]{1,0:T(8,128)(2,1)}, bf16[24,216]{1,0:T(8,128)(2,1)}) custom-call(s32[1]{0:T(128)} %bitcast.at_ref, bf16[6,6,36]{2,1,0:T(8,128)(2,1)} %refs_0_.1, bf16[6,6,36]{2,1,0:T(8,128)(2,1)} %refs_1_.1, bf16[6,6,36]{2,1,0:T(8,128)(2,1)} %refs_2_.1, bf16[6,6,36]{2,1,0:T(8,128)(2,1)} %refs_3_.1, ...), custom_call_target="tpu_custom_call" | custom-call | tf_op jit(solution)/shard_map/prepare/pallas_call | solution.py:246
  2.4 4.5 %collective-permute-start = (bf16[24,216]{1,0:T(8,128)(2,1)}, bf16[24,216]{1,0:T(8,128)(2,1)S(1)}, u32[]{:S(2)}, u32[]{:S(2)}) collective-permute-start(bf16[24,216]{1,0:T(8,128)(2,1)} %get-tuple-element.33), channel_id=1, source_target_pairs={{0,0},{1,16},{2,32},{3,48},{4,64},{5,80},{6,96},{7,112},{8,128},{9... | collective-permute-start | bytes 31112 | tf_op jit(solution)/shard_map/ppermute | solution.py:440
  6.9 0.0 copy-start
  6.9 0.0 copy-start.1
  7.0 6.9 %flat_form.1.s_hbm = bf16[1296,1408]{1,0:T(8,128)(2,1)} custom-call(bf16[13122,128]{1,0:T(8,128)(2,1)} %bitcast.13), custom_call_target="tpu_custom_call" | custom-call | flops 3221225472 | bytes 4194304 | tf_op jit(solution)/shard_map/flat_form/pallas_call | solution.py:398
  13.9 0.0 collective-permute-done.turned
  13.9 0.0 copy-done
  13.9 0.1 pieces.1
  14.0 3.2 %collective-permute-start.1 = (bf16[24,216]{1,0:T(8,128)(2,1)S(1)}, bf16[24,216]{1,0:T(8,128)(2,1)S(1)}, u32[]{:S(2)}, u32[]{:S(2)}) collective-permute-start(bf16[24,216]{1,0:T(8,128)(2,1)S(1)} %get-tuple-element.37), channel_id=1, source_target_pairs={{0,4},{1,5},{2,6},{3,7},{4,8},{5,9},{6,10},{7,11},{8,12},{9,13},{1... | collective-permute-start | bytes 31112 | tf_op jit(solution)/shard_map/ppermute | solution.py:435
  17.2 5.8 %collective-permute-start.2 = (bf16[24,216]{1,0:T(8,128)(2,1)S(1)}, bf16[24,216]{1,0:T(8,128)(2,1)S(1)}, u32[]{:S(2)}, u32[]{:S(2)}) collective-permute-start(bf16[24,216]{1,0:T(8,128)(2,1)S(1)} %get-tuple-element.37), channel_id=1, source_target_pairs={{0,8},{1,9},{2,10},{3,11},{4,12},{5,13},{6,14},{7,15},{8,0},{9,1},... | collective-permute-start | bytes 31112 | tf_op jit(solution)/shard_map/ppermute | solution.py:435
  22.9 3.5 %collective-permute-start.3 = (bf16[24,216]{1,0:T(8,128)(2,1)S(1)}, bf16[24,216]{1,0:T(8,128)(2,1)S(1)}, u32[]{:S(2)}, u32[]{:S(2)}) collective-permute-start(bf16[24,216]{1,0:T(8,128)(2,1)S(1)} %get-tuple-element.37), channel_id=1, source_target_pairs={{0,12},{1,13},{2,14},{3,15},{4,0},{5,1},{6,2},{7,3},{8,4},{9,5},{1... | collective-permute-start | bytes 31112 | tf_op jit(solution)/shard_map/ppermute | solution.py:435
  26.4 0.0 collective-permute-done.1
  26.4 0.0 collective-permute-done.2
  26.4 0.8 collective-permute-done.3
  27.2 0.0 collective-permute-start.4
  27.3 3.9 %collective-permute-start.5 = (bf16[96,216]{1,0:T(8,128)(2,1)S(1)}, bf16[96,216]{1,0:T(8,128)(2,1)S(1)}, u32[]{:S(2)}, u32[]{:S(2)}) collective-permute-start(bf16[96,216]{1,0:T(8,128)(2,1)S(1)} %get-tuple-element.70), channel_id=1, source_target_pairs={{0,2},{1,3},{2,0},{3,1},{4,6},{5,7},{6,4},{7,5},{8,10},{9,11},{10,... | collective-permute-start | bytes 124424 | tf_op jit(solution)/shard_map/ppermute | solution.py:435
  31.2 0.4 collective-permute-start.6
  31.5 0.0 collective-permute-done.4
  31.5 1.5 %collective-permute-done.5 = bf16[96,216]{1,0:T(8,128)(2,1)S(1)} collective-permute-done((bf16[96,216]{1,0:T(8,128)(2,1)S(1)}, bf16[96,216]{1,0:T(8,128)(2,1)S(1)}, u32[]{:S(2)}, u32[]{:S(2)}) %collective-permute-start.5) | collective-permute-done | bytes 41504 | tf_op jit(solution)/shard_map/ppermute | solution.py:435
  33.0 1.2 %collective-permute-done.6 = bf16[96,216]{1,0:T(8,128)(2,1)S(1)} collective-permute-done((bf16[96,216]{1,0:T(8,128)(2,1)S(1)}, bf16[96,216]{1,0:T(8,128)(2,1)S(1)}, u32[]{:S(2)}, u32[]{:S(2)}) %collective-permute-start.6) | collective-permute-done | bytes 41504 | tf_op jit(solution)/shard_map/ppermute | solution.py:435
  34.3 0.4 convolution_convert_fusion
  34.7 0.0 copy-done.1
  34.7 0.1 collective-permute-start.7
  34.9 3.8 %collective-permute-done.7 = bf16[512,128]{1,0:T(8,128)(2,1)S(1)} collective-permute-done((bf16[512,128]{1,0:T(8,128)(2,1)S(1)}, bf16[512,128]{1,0:T(8,128)(2,1)S(1)}, u32[]{:S(2)}, u32[]{:S(2)}) %collective-permute-start.7) | collective-permute-done | bytes 131104 | tf_op jit(solution)/shard_map/ppermute | solution.py:426
  38.6 3.5 %collective-permute-start.10 = (bf16[1024,128]{1,0:T(8,128)(2,1)S(1)}, bf16[1024,128]{1,0:T(8,128)(2,1)S(1)}, u32[]{:S(2)}, u32[]{:S(2)}) collective-permute-start(bf16[1024,128]{1,0:T(8,128)(2,1)S(1)} %constant_dynamic-update-slice_fusion.11.refs_0_), channel_id=1, source_target_pairs={{0,192},{16,208},{32,224},{48,240},{64,0},{80,16},{96,32},{112,48}... | collective-permute-start | bytes 786440 | tf_op jit(solution)/shard_map/ppermute | solution.py:426
  42.1 4.5 %collective-permute-start.11 = (bf16[1024,128]{1,0:T(8,128)(2,1)S(1)}, bf16[1024,128]{1,0:T(8,128)(2,1)S(1)}, u32[]{:S(2)}, u32[]{:S(2)}) collective-permute-start(bf16[1024,128]{1,0:T(8,128)(2,1)S(1)} %constant_dynamic-update-slice_fusion.11.refs_0_), channel_id=1, source_target_pairs={{0,16},{16,0},{32,48},{48,32},{64,80},{80,64},{96,112},{112,96},{1... | collective-permute-start | bytes 786440 | tf_op jit(solution)/shard_map/ppermute | solution.py:426
  46.6 0.0 collective-permute-start.8
  46.6 1.0 collective-permute-start.9
  47.6 9.2 %left_forms.1 = (bf16[1296,1408]{1,0:T(8,128)(2,1)}, bf16[1296,1536]{1,0:T(8,128)(2,1)}) custom-call(bf16[1296,1408]{1,0:T(8,128)(2,1)} %flat_form.1.s_hbm), custom_call_target="tpu_custom_call" | custom-call | flops 4294967296 | bytes 4194304 | tf_op jit(solution)/shard_map/left_forms/pallas_call | solution.py:411
  56.8 0.0 collective-permute-done.10.refs_3_
  56.8 0.0 collective-permute-done.11.refs_4_
  56.8 4.5 %collective-permute-done.8.refs_1_ = bf16[1024,128]{1,0:T(8,128)(2,1)S(1)} collective-permute-done((bf16[1024,128]{1,0:T(8,128)(2,1)S(1)}, bf16[1024,128]{1,0:T(8,128)(2,1)S(1)}, u32[]{:S(2)}, u32[]{:S(2)}) %collective-permute-start.8) | collective-permute-done | bytes 262176 | tf_op jit(solution)/shard_map/ppermute | solution.py:426
  61.3 0.0 collective-permute-done.9.refs_2_
  61.3 0.9 collective-permute-start.12
  62.2 0.0 collective-permute-start.13
  62.2 0.5 collective-permute-start.14
  62.7 0.6 collective-permute-done.12.refs_5_
  63.3 0.4 collective-permute-done.13.refs_6_
  63.7 0.4 collective-permute-done.14.refs_7_
  64.1 0.9 gather_small.1.refs_8_
  65.0 14.5 %left.1 = (bf16[216,216]{1,0:T(8,128)(2,1)}, f32[128,256]{1,0:T(8,128)S(1)}) custom-call(s32[16]{0:T(128)S(1)} %fusion.26.order_ref, bf16[1024,128]{1,0:T(8,128)(2,1)S(1)} %constant_dynamic-update-slice_fusion.11.refs_0_, bf16[1024,128]{1,0:T(8,128)(2,1)S(1)} %collective-permute-done.8.refs_1_, bf16[1024,128]{1,0:T(8,128)(2,1)S(1)} %collective-permute-done.9.refs_2_, ...), custom_call_target="tpu_custom_call" | custom-call | flops 8589934592 | bytes 4194304 | tf_op jit(solution)/shard_map/left/pallas_call | solution.py:271
  79.5 0.5 collective-permute-start.15
  80.0 0.9 collective-permute-done.15
  80.9 1.8 %collective-permute-start.16 = (f32[32,256]{1,0:T(8,128)S(1)}, f32[32,256]{1,0:T(8,128)S(1)}, u32[]{:S(2)}, u32[]{:S(2)}) collective-permute-start(f32[32,256]{1,0:T(8,128)S(1)} %constant_dynamic-slice_fusion.4), channel_id=1, source_target_pairs={{0,32},{16,48},{32,0},{48,16},{64,96},{80,112},{96,64},{112,80},{1... | collective-permute-start | bytes 98312 | tf_op jit(solution)/shard_map/ppermute | solution.py:426
  82.7 7.4 %right_form.1.refs_10_ = bf16[1296,1536]{1,0:T(8,128)(2,1)} custom-call(bf16[1296,1408]{1,0:T(8,128)(2,1)} %flat_form.1.s_hbm), custom_call_target="tpu_custom_call" | custom-call | flops 3221225472 | bytes 4194304 | tf_op jit(solution)/shard_map/right_form/pallas_call | solution.py:405
  90.1 0.0 collective-permute-done.16
  90.2 0.3 collective-permute-start.17
  90.5 0.4 collective-permute-start.18
  90.9 2.2 %collective-permute-start.19 = (f32[8,256]{1,0:T(8,128)S(1)}, f32[8,256]{1,0:T(8,128)S(1)}, u32[]{:S(2)}, u32[]{:S(2)}) collective-permute-start(f32[8,256]{1,0:T(8,128)S(1)} %get-tuple-element.67), channel_id=1, source_target_pairs={{0,192},{16,208},{32,224},{48,240},{64,0},{80,16},{96,32},{112,48}... | collective-permute-start | bytes 24584 | tf_op jit(solution)/shard_map/ppermute | solution.py:426
  93.2 11.9 %upper.1 = (bf16[216,216]{1,0:T(8,128)(2,1)}, bf16[6,216]{1,0:T(8,128)(2,1)}) custom-call(s32[16]{0:T(128)S(1)} %fusion.26.order_ref, bf16[1024,128]{1,0:T(8,128)(2,1)S(1)} %constant_dynamic-update-slice_fusion.11.refs_0_, bf16[1024,128]{1,0:T(8,128)(2,1)S(1)} %collective-permute-done.8.refs_1_, bf16[1024,128]{1,0:T(8,128)(2,1)S(1)} %collective-permute-done.9.refs_2_, ...), custom_call_target="tpu_custom_call" | custom-call | flops 8589934592 | bytes 4194304 | tf_op jit(solution)/shard_map/upper/pallas_call | solution.py:264
  105.0 0.0 collective-permute-done.17.one
  105.0 0.0 collective-permute-done.18.two
  105.1 0.0 collective-permute-done.19.three
  105.1 0.7 finish.1
  (20 shorter events, 0.2 us)
Async XLA Ops:
  2.4 11.4 %collective-permute-start = (bf16[24,216]{1,0:T(8,128)(2,1)}, bf16[24,216]{1,0:T(8,128)(2,1)S(1)}, u32[]{:S(2)}, u32[]{:S(2)}) collective-permute-start(bf16[24,216]{1,0:T(8,128)(2,1)} %get-tuple-element.33), channel_id=1, source_target_pairs={{0,0},{1,16},{2,32},{3,48},{4,64},{5,80},{6,96},{7,112},{8,128},{9... | collective-permute-start | bytes 31112 | tf_op jit(solution)/shard_map/ppermute | solution.py:440
  6.9 6.9 %copy-start = (bf16[16,216]{1,0:T(8,128)(2,1)S(1)}, bf16[16,216]{1,0:T(8,128)(2,1)}, u32[]{:S(2)}) copy-start(bf16[16,216]{1,0:T(8,128)(2,1)} %get-tuple-element.36.piece) | copy-start | bytes 20740
  6.9 27.7 %copy-start.1 = (bf16[64,128]{1,0:T(8,128)(2,1)S(1)}, bf16[64,128]{1,0:T(8,128)(2,1)}, u32[]{:S(2)}) copy-start(bf16[64,128]{1,0:T(8,128)(2,1)} %get-tuple-element.38) | copy-start | bytes 49156
  14.0 12.4 %collective-permute-start.1 = (bf16[24,216]{1,0:T(8,128)(2,1)S(1)}, bf16[24,216]{1,0:T(8,128)(2,1)S(1)}, u32[]{:S(2)}, u32[]{:S(2)}) collective-permute-start(bf16[24,216]{1,0:T(8,128)(2,1)S(1)} %get-tuple-element.37), channel_id=1, source_target_pairs={{0,4},{1,5},{2,6},{3,7},{4,8},{5,9},{6,10},{7,11},{8,12},{9,13},{1... | collective-permute-start | bytes 31112 | tf_op jit(solution)/shard_map/ppermute | solution.py:435
  17.2 9.2 %collective-permute-start.2 = (bf16[24,216]{1,0:T(8,128)(2,1)S(1)}, bf16[24,216]{1,0:T(8,128)(2,1)S(1)}, u32[]{:S(2)}, u32[]{:S(2)}) collective-permute-start(bf16[24,216]{1,0:T(8,128)(2,1)S(1)} %get-tuple-element.37), channel_id=1, source_target_pairs={{0,8},{1,9},{2,10},{3,11},{4,12},{5,13},{6,14},{7,15},{8,0},{9,1},... | collective-permute-start | bytes 31112 | tf_op jit(solution)/shard_map/ppermute | solution.py:435
  22.9 4.3 %collective-permute-start.3 = (bf16[24,216]{1,0:T(8,128)(2,1)S(1)}, bf16[24,216]{1,0:T(8,128)(2,1)S(1)}, u32[]{:S(2)}, u32[]{:S(2)}) collective-permute-start(bf16[24,216]{1,0:T(8,128)(2,1)S(1)} %get-tuple-element.37), channel_id=1, source_target_pairs={{0,12},{1,13},{2,14},{3,15},{4,0},{5,1},{6,2},{7,3},{8,4},{9,5},{1... | collective-permute-start | bytes 31112 | tf_op jit(solution)/shard_map/ppermute | solution.py:435
  27.2 4.3 %collective-permute-start.4 = (bf16[96,216]{1,0:T(8,128)(2,1)S(1)}, bf16[96,216]{1,0:T(8,128)(2,1)S(1)}, u32[]{:S(2)}, u32[]{:S(2)}) collective-permute-start(bf16[96,216]{1,0:T(8,128)(2,1)S(1)} %get-tuple-element.70), channel_id=1, source_target_pairs={{0,1},{1,2},{2,3},{3,0},{4,5},{5,6},{6,7},{7,4},{8,9},{9,10},{10,1... | collective-permute-start | bytes 124424 | tf_op jit(solution)/shard_map/ppermute | solution.py:435
  27.3 5.8 %collective-permute-start.5 = (bf16[96,216]{1,0:T(8,128)(2,1)S(1)}, bf16[96,216]{1,0:T(8,128)(2,1)S(1)}, u32[]{:S(2)}, u32[]{:S(2)}) collective-permute-start(bf16[96,216]{1,0:T(8,128)(2,1)S(1)} %get-tuple-element.70), channel_id=1, source_target_pairs={{0,2},{1,3},{2,0},{3,1},{4,6},{5,7},{6,4},{7,5},{8,10},{9,11},{10,... | collective-permute-start | bytes 124424 | tf_op jit(solution)/shard_map/ppermute | solution.py:435
  31.2 3.1 %collective-permute-start.6 = (bf16[96,216]{1,0:T(8,128)(2,1)S(1)}, bf16[96,216]{1,0:T(8,128)(2,1)S(1)}, u32[]{:S(2)}, u32[]{:S(2)}) collective-permute-start(bf16[96,216]{1,0:T(8,128)(2,1)S(1)} %get-tuple-element.70), channel_id=1, source_target_pairs={{0,3},{1,0},{2,1},{3,2},{4,7},{5,4},{6,5},{7,6},{8,11},{9,8},{10,9... | collective-permute-start | bytes 124424 | tf_op jit(solution)/shard_map/ppermute | solution.py:435
  34.7 3.9 %collective-permute-start.7 = (bf16[512,128]{1,0:T(8,128)(2,1)S(1)}, bf16[512,128]{1,0:T(8,128)(2,1)S(1)}, u32[]{:S(2)}, u32[]{:S(2)}) collective-permute-start(bf16[512,128]{1,0:T(8,128)(2,1)S(1)} %pad_maximum_fusion), channel_id=1, source_target_pairs={{0,32},{16,48},{32,0},{48,16},{64,96},{80,112},{96,64},{112,80},{1... | collective-permute-start | bytes 393224 | tf_op jit(solution)/shard_map/ppermute | solution.py:426
  38.6 18.1 %collective-permute-start.10 = (bf16[1024,128]{1,0:T(8,128)(2,1)S(1)}, bf16[1024,128]{1,0:T(8,128)(2,1)S(1)}, u32[]{:S(2)}, u32[]{:S(2)}) collective-permute-start(bf16[1024,128]{1,0:T(8,128)(2,1)S(1)} %constant_dynamic-update-slice_fusion.11.refs_0_), channel_id=1, source_target_pairs={{0,192},{16,208},{32,224},{48,240},{64,0},{80,16},{96,32},{112,48}... | collective-permute-start | bytes 786440 | tf_op jit(solution)/shard_map/ppermute | solution.py:426
  42.1 14.7 %collective-permute-start.11 = (bf16[1024,128]{1,0:T(8,128)(2,1)S(1)}, bf16[1024,128]{1,0:T(8,128)(2,1)S(1)}, u32[]{:S(2)}, u32[]{:S(2)}) collective-permute-start(bf16[1024,128]{1,0:T(8,128)(2,1)S(1)} %constant_dynamic-update-slice_fusion.11.refs_0_), channel_id=1, source_target_pairs={{0,16},{16,0},{32,48},{48,32},{64,80},{80,64},{96,112},{112,96},{1... | collective-permute-start | bytes 786440 | tf_op jit(solution)/shard_map/ppermute | solution.py:426
  46.6 14.7 %collective-permute-start.8 = (bf16[1024,128]{1,0:T(8,128)(2,1)S(1)}, bf16[1024,128]{1,0:T(8,128)(2,1)S(1)}, u32[]{:S(2)}, u32[]{:S(2)}) collective-permute-start(bf16[1024,128]{1,0:T(8,128)(2,1)S(1)} %constant_dynamic-update-slice_fusion.11.refs_0_), channel_id=1, source_target_pairs={{0,64},{16,80},{32,96},{48,112},{64,128},{80,144},{96,160},{112,17... | collective-permute-start | bytes 786440 | tf_op jit(solution)/shard_map/ppermute | solution.py:426
  46.6 14.7 %collective-permute-start.9 = (bf16[1024,128]{1,0:T(8,128)(2,1)S(1)}, bf16[1024,128]{1,0:T(8,128)(2,1)S(1)}, u32[]{:S(2)}, u32[]{:S(2)}) collective-permute-start(bf16[1024,128]{1,0:T(8,128)(2,1)S(1)} %constant_dynamic-update-slice_fusion.11.refs_0_), channel_id=1, source_target_pairs={{0,128},{16,144},{32,160},{48,176},{64,192},{80,208},{96,224},{112... | collective-permute-start | bytes 786440 | tf_op jit(solution)/shard_map/ppermute | solution.py:426
  61.3 2.0 %collective-permute-start.12 = (bf16[1024,128]{1,0:T(8,128)(2,1)S(1)}, bf16[1024,128]{1,0:T(8,128)(2,1)S(1)}, u32[]{:S(2)}, u32[]{:S(2)}) collective-permute-start(bf16[1024,128]{1,0:T(8,128)(2,1)S(1)} %collective-permute-done.8.refs_1_), channel_id=1, source_target_pairs={{0,16},{16,0},{32,48},{48,32},{64,80},{80,64},{96,112},{112,96},{1... | collective-permute-start | bytes 786440 | tf_op jit(solution)/shard_map/ppermute | solution.py:426
  62.2 1.5 %collective-permute-start.13 = (bf16[1024,128]{1,0:T(8,128)(2,1)S(1)}, bf16[1024,128]{1,0:T(8,128)(2,1)S(1)}, u32[]{:S(2)}, u32[]{:S(2)}) collective-permute-start(bf16[1024,128]{1,0:T(8,128)(2,1)S(1)} %collective-permute-done.9.refs_2_), channel_id=1, source_target_pairs={{0,16},{16,0},{32,48},{48,32},{64,80},{80,64},{96,112},{112,96},{1... | collective-permute-start | bytes 786440 | tf_op jit(solution)/shard_map/ppermute | solution.py:426
  62.2 1.9 %collective-permute-start.14 = (bf16[1024,128]{1,0:T(8,128)(2,1)S(1)}, bf16[1024,128]{1,0:T(8,128)(2,1)S(1)}, u32[]{:S(2)}, u32[]{:S(2)}) collective-permute-start(bf16[1024,128]{1,0:T(8,128)(2,1)S(1)} %collective-permute-done.10.refs_3_), channel_id=1, source_target_pairs={{0,16},{16,0},{32,48},{48,32},{64,80},{80,64},{96,112},{112,96},{1... | collective-permute-start | bytes 786440 | tf_op jit(solution)/shard_map/ppermute | solution.py:426
  79.5 1.4 %collective-permute-start.15 = (f32[64,256]{1,0:T(8,128)S(1)}, f32[64,256]{1,0:T(8,128)S(1)}, u32[]{:S(2)}, u32[]{:S(2)}) collective-permute-start(f32[64,256]{1,0:T(8,128)S(1)} %constant_dynamic-slice_fusion.5), channel_id=1, source_target_pairs={{0,16},{16,0},{32,48},{48,32},{64,80},{80,64},{96,112},{112,96},{1... | collective-permute-start | bytes 196616 | tf_op jit(solution)/shard_map/ppermute | solution.py:426
  80.9 9.2 %collective-permute-start.16 = (f32[32,256]{1,0:T(8,128)S(1)}, f32[32,256]{1,0:T(8,128)S(1)}, u32[]{:S(2)}, u32[]{:S(2)}) collective-permute-start(f32[32,256]{1,0:T(8,128)S(1)} %constant_dynamic-slice_fusion.4), channel_id=1, source_target_pairs={{0,32},{16,48},{32,0},{48,16},{64,96},{80,112},{96,64},{112,80},{1... | collective-permute-start | bytes 98312 | tf_op jit(solution)/shard_map/ppermute | solution.py:426
  90.2 14.9 %collective-permute-start.17 = (f32[8,256]{1,0:T(8,128)S(1)}, f32[8,256]{1,0:T(8,128)S(1)}, u32[]{:S(2)}, u32[]{:S(2)}) collective-permute-start(f32[8,256]{1,0:T(8,128)S(1)} %get-tuple-element.69), channel_id=1, source_target_pairs={{0,64},{16,80},{32,96},{48,112},{64,128},{80,144},{96,160},{112,17... | collective-permute-start | bytes 24584 | tf_op jit(solution)/shard_map/ppermute | solution.py:426
  90.5 14.6 %collective-permute-start.18 = (f32[8,256]{1,0:T(8,128)S(1)}, f32[8,256]{1,0:T(8,128)S(1)}, u32[]{:S(2)}, u32[]{:S(2)}) collective-permute-start(f32[8,256]{1,0:T(8,128)S(1)} %get-tuple-element.68), channel_id=1, source_target_pairs={{0,128},{16,144},{32,160},{48,176},{64,192},{80,208},{96,224},{112... | collective-permute-start | bytes 24584 | tf_op jit(solution)/shard_map/ppermute | solution.py:426
  90.9 14.1 %collective-permute-start.19 = (f32[8,256]{1,0:T(8,128)S(1)}, f32[8,256]{1,0:T(8,128)S(1)}, u32[]{:S(2)}, u32[]{:S(2)}) collective-permute-start(f32[8,256]{1,0:T(8,128)S(1)} %get-tuple-element.67), channel_id=1, source_target_pairs={{0,192},{16,208},{32,224},{48,240},{64,0},{80,16},{96,32},{112,48}... | collective-permute-start | bytes 24584 | tf_op jit(solution)/shard_map/ppermute | solution.py:426

commit v5 on v4

--- a/solution.py
+++ b/solution.py
@@ -12,7 +12,7 @@
 VM = pl.BlockSpec(memory_space=pltpu.VMEM)
 SM = pl.BlockSpec(memory_space=pltpu.SMEM)
 HB = pl.BlockSpec(memory_space=pltpu.HBM)
-BLOCK = 512
+BLOCK = 496
 WIDE = 3456
 
 
@@ -53,17 +53,18 @@
     for e in (te, re, be):
         v = e[...].astype(F)
         parts.append(jnp.concatenate([v[:, j, :] for j in range(6)], axis=1))
+    bottom = parts.pop()
     row = lax.broadcasted_iota(jnp.int32, (8, 96), 0)
     lane = lax.broadcasted_iota(jnp.int32, (8, 96), 1)
     pick = ((lane == at_ref[0] + row) & (row < 6)).astype(B)
     turned[0:8, :] = dot(pick, tpt[...]).astype(B)
     turned[8:16, :] = dot(pick, bpt[...]).astype(B)
-    turned[16:24, :] = jnp.concatenate([parts[2].astype(B), zero], axis=0)
+    turned[16:24, :] = jnp.concatenate([bottom.astype(B), zero], axis=0)
     for c in (uct, rct, lct):
         parts.append(c[...].astype(F))
-    flat = jnp.concatenate(parts + [jnp.zeros((6, 88), F)], axis=1)
-    flat = jnp.concatenate([flat, jnp.zeros((2, 1024), F)], axis=0).astype(B)
-    for k in range(8):
+    flat = jnp.concatenate(parts + [jnp.zeros((6, 48), F)], axis=1)
+    flat = jnp.concatenate([flat, jnp.zeros((2, 768), F)], axis=0).astype(B)
+    for k in range(6):
         pack[8 * k:8 * k + 8, :] = flat[:, 128 * k:128 * k + 128]
 
 
@@ -95,18 +96,18 @@
     for rel in range(16):
         at = pl.multiple_of(order_ref[rel] * 8, 8)
         start = (rel % 2) * BLOCK + 432
-        for k in range(10):
+        for k in range(8):
             packs[k, pl.ds(at, 8), :] = bufs[rel // 2][start + 8 * k:start + 8 * k + 8, :].astype(F)
     row = lax.broadcasted_iota(jnp.int32, (128, 128), 0)
     lane = lax.broadcasted_iota(jnp.int32, (128, 128), 1)
     place = ((row % 8 < 6) & (lane == (row // 8) * 6 + row % 8)).astype(B)
-    for k in range(10):
+    for k in range(8):
         out_ref[k * 128:(k + 1) * 128, :] = dot(jnp.transpose(packs[k]).astype(B), place).astype(B)
 
 
 def gather_small(order, bufs):
-    return pl.pallas_call(gather_small_kernel, out_shape=shape_of(1280, 128), in_specs=[SM] + [VM] * 8, out_specs=VM,
-                          scratch_shapes=[pltpu.VMEM((10, 128, 128), F)], name="gather_small",
+    return pl.pallas_call(gather_small_kernel, out_shape=shape_of(1024, 128), in_specs=[SM] + [VM] * 8, out_specs=VM,
+                          scratch_shapes=[pltpu.VMEM((8, 128, 128), F)], name="gather_small",
                           compiler_params=params(6))(order, *bufs)
 
 
@@ -148,9 +149,9 @@
     small_ref, wtop_hbm, wright_hbm, out_ref, ct_ref, tef, pf, p1, p3, o1, o3, tps, wtop_ref, wright_ref, sems = refs[8:]
     copies = load([(wtop_hbm, wtop_ref), (wright_hbm, wright_ref)], sems)
     expand(order_ref, bufs, 0, tef)
-    uc = small_ref[648:744, :]
-    rc = small_ref[744:840, :]
-    tps[0:216, :] = small_ref[1024:1240, :].astype(F)
+    uc = small_ref[432:528, :]
+    rc = small_ref[528:624, :]
+    tps[0:216, :] = small_ref[768:984, :].astype(F)
     tps[216:320, :] = jnp.zeros((104, 128), F)
     lu = dot(bufs[0][216:432, :][:, :96], uc).astype(B)[:, :96]
     ar = dot(small_ref[216:432, :], rc, NT).astype(B)
@@ -190,28 +191,32 @@
 
 def left_kernel(order_ref, *refs):
     bufs = refs[:8]
-    small_ref, ber_ref, wtop_hbm, wbot_hbm, bpr_ref, out_ref, cb_ref, lef, pf, p2, p4, o2, o4, cbs, abf, wtop_ref, wbot_ref, sems = refs[8:]
+    small_ref, ber_ref, wtop_hbm, wbot_hbm, bpr_ref, out_ref, cb_ref, lef, pf, p2, p4, o2, o4, cbs, wtop_ref, wbot_ref, sems = refs[8:]
     copies = load([(wtop_hbm, wtop_ref), (wbot_hbm, wbot_ref)], sems)
     expand(order_ref, bufs, 216, lef)
-    uc = small_ref[648:744, :]
-    lc = small_ref[840:936, :]
+    uc = small_ref[432:528, :]
+    lc = small_ref[624:720, :]
     at = dot(small_ref[0:216, :], uc, NT).astype(B)
-    abf[0:216, :] = padded(dot(ber_ref[...], lc, NT))
-    ab = jnp.concatenate([abf[pl.ds(b * 36 + h, 12, stride=3), :] for b in range(6) for h in range(3)], axis=0).astype(B)[:, :96]
+    ab = dot(ber_ref[...], lc, NT).astype(B)[:, :96]
     for u in range(36):
         le = lef[pl.ds(u, 96, stride=36), :].astype(B)
         d2 = padded(dot(at, le[:, :96], NT))
         for b in range(6):
-            pf[b, pl.ds(u, 36, stride=36), :] = d2[b * 36:(b + 1) * 36, :]
-    to_bf16(pf, p2, 1296)
-    clear_gaps(pf)
+            pf[b, u * 36:(u + 1) * 36, :] = d2[b * 36:(b + 1) * 36, :]
+    for g in range(9):
+        for b in range(6):
+            p2[g * 144:(g + 1) * 144, b * 128:(b + 1) * 128] = jnp.concatenate(
+                [pf[b, pl.ds(4 * g + e, 36, stride=36), :] for e in range(4)], axis=0).astype(B)
     for u in range(36):
         le = lef[pl.ds(u, 96, stride=36), :].astype(B)
         d4 = dot(ab, le)
         for b in range(6):
-            for h in range(3):
-                pf[b, pl.ds(h * 36 + u, 12, stride=128), :] = d4[b * 36 + h * 12:b * 36 + h * 12 + 12, :]
-    to_bf16(pf, p4, 1536)
+            pf[b, u * 36:(u + 1) * 36, :] = d4[b * 36:(b + 1) * 36, :]
+    gap = jnp.zeros((20, 128), F)
+    for q in range(12):
+        for b in range(6):
+            p4[q * 128:(q + 1) * 128, b * 128:(b + 1) * 128] = jnp.concatenate(
+                [pf[b, pl.ds(3 * q + e, 36, stride=36), :] for e in range(3)] + [gap], axis=0).astype(B)
     copies[0].wait()
     big(wtop_ref, p2, 1296, o2)
     copies[1].wait()
@@ -244,7 +249,7 @@
 
 def prepare(at, *args):
     return pl.pallas_call(
-        prepare_kernel, out_shape=(shape_of(16, 216), shape_of(64, 128), shape_of(24, 216)),
+        prepare_kernel, out_shape=(shape_of(16, 216), shape_of(48, 128), shape_of(24, 216)),
         in_specs=[SM] + [HB] * 9, out_specs=(VM,) * 3,
         scratch_shapes=[pltpu.VMEM(x.shape, B) for x in args] + [pltpu.SemaphoreType.DMA((9,))],
         name="prepare")(at, *args)
@@ -271,7 +276,7 @@
     return pl.pallas_call(
         left_kernel, out_shape=(shape_of(216, 216), shape_of(128, 256, kind=F)),
         in_specs=[SM] + [VM] * 10 + [HB] * 2 + [VM], out_specs=(VM, VM),
-        scratch_shapes=scratch() + [pltpu.VMEM((288, 128), F), pltpu.VMEM((232, 128), F)] + form_copies(), name="left",
+        scratch_shapes=scratch() + [pltpu.VMEM((288, 128), F)] + form_copies(), name="left",
         compiler_params=params(50), cost_estimate=work(8 << 30))(order, *bufs, small, ber, wtop, wbot, bpr)
 
 
@@ -286,14 +291,18 @@
                           name="finish", compiler_params=params(4))(*parts)
 
 
-def lanes_shifted(a_ref, z_ref, pair):
+def lane_pattern(ref):
+    k = lax.broadcasted_iota(jnp.int32, (256, 256), 0)
+    n = lax.broadcasted_iota(jnp.int32, (256, 256), 1)
+    w = n % 128
+    ref[...] = jnp.where(w < 108, k - (n // 128) * 36 - w % 36, -1)
+
+
+def lanes_shifted(a_ref, z_ref, pattern, pair):
     tile = (pair * 72) // 128
     base = pl.multiple_of(tile * 128, 128)
     off = pair * 72 - tile * 128
-    k = lax.broadcasted_iota(jnp.int32, (256, 256), 0)
-    n = lax.broadcasted_iota(jnp.int32, (256, 256), 1)
-    w = n % 128
-    sel = ((k == off + (n // 128) * 36 + w % 36) & (w < 108)).astype(B)
+    sel = (pattern[...] == off).astype(B)
     z_ref[...] = dot(a_ref[:, pl.ds(base, 256)], sel)
 
 
@@ -302,7 +311,7 @@
     return load([(src.at[:, p:q], dst.at[:, p:q]) for p, q in zip(ends, ends[1:])], sems)
 
 
-def realign(a_ref, z_ref, o_ref, out_hbm, sem, chunks=()):
+def realign(a_ref, z_ref, o_ref, pattern, out_hbm, sem, chunks=()):
     lane = lax.broadcasted_iota(jnp.int32, (36, 128), 1)
 
     def f(g, _):
@@ -312,7 +321,7 @@
                 cp.wait()
         strips = []
         for h in range(2):
-            lanes_shifted(a_ref, z_ref.at[h], 2 * g + h)
+            lanes_shifted(a_ref, z_ref.at[h], pattern, 2 * g + h)
         for h in range(2):
             for q in range(2):
                 tiles = []
@@ -333,12 +342,15 @@
     lax.fori_loop(0, 9, w, 0)
 
 
-def right_form_kernel(s_hbm, wright_hbm, apad, z, o, sems, done):
-    realign(apad, z, o, wright_hbm, done, column_chunks(s_hbm, apad, sems))
-
-
-def left_forms_kernel(s_hbm, wtop_hbm, wbot_hbm, apad, z, o, sems, done, s_ref):
+def right_form_kernel(s_hbm, wright_hbm, apad, z, o, pattern, sems, done):
+    chunks = column_chunks(s_hbm, apad, sems)
+    lane_pattern(pattern)
+    realign(apad, z, o, pattern, wright_hbm, done, chunks)
+
+
+def left_forms_kernel(s_hbm, wtop_hbm, wbot_hbm, apad, z, o, pattern, sems, done, s_ref):
     chunks = column_chunks(s_hbm, s_ref, sems)
+    lane_pattern(pattern)
     eye = (lax.broadcasted_iota(jnp.int32, (128, 128), 0) == lax.broadcasted_iota(jnp.int32, (128, 128), 1)).astype(B)
     for b in range(11):
         n = min(128, 1296 - b * 128)
@@ -348,7 +360,7 @@
     apad[:, 1296:1408] = jnp.zeros((1296, 112), B)
     out = pltpu.make_async_copy(apad, wtop_hbm, sems.at[0])
     out.start()
-    realign(apad, z, o, wbot_hbm, done)
+    realign(apad, z, o, pattern, wbot_hbm, done)
     out.wait()
 
 
@@ -391,6 +403,7 @@
 
 def form_scratch():
     return [pltpu.VMEM((1296, 1408), B), pltpu.VMEM((2, 1296, 256), F), pltpu.VMEM((1296, 1536), B),
+            pltpu.VMEM((256, 256), jnp.int32),
             pltpu.SemaphoreType.DMA((4,)), pltpu.SemaphoreType.DMA((9,))]
 
 

time: 106 us -> 103 us (0.972)
  Pallas kernels: 53.3 us -> 50.8 us
    pallas_call x1, Pallas kernels: 14.5 us -> 12.1 us  [left(): pl.pallas_call(left_kernel, out_shape=(shape_of(216, 216), shape_of(128,...]
  transfers between devices with their start and end apart: 20 -> 20, of which waited for: 9 -> 9; matrix products, arithmetic and copies ran while one was open for 0% -> 0% of each run, Pallas kernels for 33% -> 34%
where the time goes in v5:
time: 103 us
  Pallas kernels  50.8 us (49%)
  starting transfers between devices  36.6 us (36%)
  waiting for transfers between devices  13.7 us (13%)
    ppermute x6, starting transfers between devices, col_permute(): return lax.ppermute(x, COL, pairs)  16.7 us
    ppermute x13, starting transfers between devices, row_permute(): return lax.ppermute(x, ROW, pairs)  15.5 us
    pallas_call x1, Pallas kernels, left(): pl.pallas_call(left_kernel, out_shape=(shape_of(216, 216), shape_of(128,...  12.1 us
    pallas_call x1, Pallas kernels, upper(): pl.pallas_call(upper_kernel, out_shape=(shape_of(216, 216), shape_of(6, 2...  11.9 us
    ppermute x13, waiting for transfers between devices, row_permute(): return lax.ppermute(x, ROW, pairs)  10.2 us
    pallas_call x1, Pallas kernels, left_forms(): pl.pallas_call(left_forms_kernel, out_shape=(shape_of(1296, 1408), shape_...  9.14 us
    pallas_call x1, Pallas kernels, right_form(): pl.pallas_call(right_form_kernel, out_shape=shape_of(1296, 1536), in_spec...  7.38 us
    pallas_call x1, Pallas kernels, flat_form(): pl.pallas_call(flat_form_kernel, out_shape=shape_of(1296, 1408), in_specs...  6.89 us
  transfers between devices with their start and end apart: 20, of which 9 were waited for; matrix products, arithmetic and copies ran while one was open for 0% of the time, Pallas kernels for 34%

profile of v5, /device:TPU:1, one launch (start us, length us, event | category | flops | bytes accessed | tf_op | source)
XLA Modules:
  0.0 102.6 jit_solution(6213256903942527251)
XLA Ops:
  0.6 1.8 %prepare.1 = (bf16[16,216]{1,0:T(8,128)(2,1)}, bf16[48,128]{1,0:T(8,128)(2,1)}, bf16[24,216]{1,0:T(8,128)(2,1)}) custom-call(s32[1]{0:T(128)} %bitcast.at_ref, bf16[6,6,36]{2,1,0:T(8,128)(2,1)} %refs_0_.1, bf16[6,6,36]{2,1,0:T(8,128)(2,1)} %refs_1_.1, bf16[6,6,36]{2,1,0:T(8,128)(2,1)} %refs_2_.1, bf16[6,6,36]{2,1,0:T(8,128)(2,1)} %refs_3_.1, ...), custom_call_target="tpu_custom_call" | custom-call | tf_op jit(solution)/shard_map/prepare/pallas_call | solution.py:251
  2.4 4.5 %collective-permute-start = (bf16[24,216]{1,0:T(8,128)(2,1)}, bf16[24,216]{1,0:T(8,128)(2,1)S(1)}, u32[]{:S(2)}, u32[]{:S(2)}) collective-permute-start(bf16[24,216]{1,0:T(8,128)(2,1)} %get-tuple-element.33), channel_id=1, source_target_pairs={{0,0},{1,16},{2,32},{3,48},{4,64},{5,80},{6,96},{7,112},{8,128},{9... | collective-permute-start | bytes 31112 | tf_op jit(solution)/shard_map/ppermute | solution.py:453
  6.9 0.0 copy-start
  6.9 0.0 copy-start.1
  6.9 6.9 %flat_form.1.s_hbm = bf16[1296,1408]{1,0:T(8,128)(2,1)} custom-call(bf16[13122,128]{1,0:T(8,128)(2,1)} %bitcast.13), custom_call_target="tpu_custom_call" | custom-call | flops 3221225472 | bytes 4194304 | tf_op jit(solution)/shard_map/flat_form/pallas_call | solution.py:411
  13.9 0.0 collective-permute-done.turned
  13.9 0.0 copy-done
  13.9 0.1 pieces.1
  14.0 3.2 %collective-permute-start.1 = (bf16[24,216]{1,0:T(8,128)(2,1)S(1)}, bf16[24,216]{1,0:T(8,128)(2,1)S(1)}, u32[]{:S(2)}, u32[]{:S(2)}) collective-permute-start(bf16[24,216]{1,0:T(8,128)(2,1)S(1)} %get-tuple-element.37), channel_id=1, source_target_pairs={{0,4},{1,5},{2,6},{3,7},{4,8},{5,9},{6,10},{7,11},{8,12},{9,13},{1... | collective-permute-start | bytes 31112 | tf_op jit(solution)/shard_map/ppermute | solution.py:448
  17.2 5.8 %collective-permute-start.2 = (bf16[24,216]{1,0:T(8,128)(2,1)S(1)}, bf16[24,216]{1,0:T(8,128)(2,1)S(1)}, u32[]{:S(2)}, u32[]{:S(2)}) collective-permute-start(bf16[24,216]{1,0:T(8,128)(2,1)S(1)} %get-tuple-element.37), channel_id=1, source_target_pairs={{0,8},{1,9},{2,10},{3,11},{4,12},{5,13},{6,14},{7,15},{8,0},{9,1},... | collective-permute-start | bytes 31112 | tf_op jit(solution)/shard_map/ppermute | solution.py:448
  22.9 3.5 %collective-permute-start.3 = (bf16[24,216]{1,0:T(8,128)(2,1)S(1)}, bf16[24,216]{1,0:T(8,128)(2,1)S(1)}, u32[]{:S(2)}, u32[]{:S(2)}) collective-permute-start(bf16[24,216]{1,0:T(8,128)(2,1)S(1)} %get-tuple-element.37), channel_id=1, source_target_pairs={{0,12},{1,13},{2,14},{3,15},{4,0},{5,1},{6,2},{7,3},{8,4},{9,5},{1... | collective-permute-start | bytes 31112 | tf_op jit(solution)/shard_map/ppermute | solution.py:448
  26.4 0.0 collective-permute-done.1
  26.4 0.0 collective-permute-done.2
  26.4 0.8 collective-permute-done.3
  27.2 0.0 collective-permute-start.4
  27.3 3.9 %collective-permute-start.5 = (bf16[96,216]{1,0:T(8,128)(2,1)S(1)}, bf16[96,216]{1,0:T(8,128)(2,1)S(1)}, u32[]{:S(2)}, u32[]{:S(2)}) collective-permute-start(bf16[96,216]{1,0:T(8,128)(2,1)S(1)} %get-tuple-element.70), channel_id=1, source_target_pairs={{0,2},{1,3},{2,0},{3,1},{4,6},{5,7},{6,4},{7,5},{8,10},{9,11},{10,... | collective-permute-start | bytes 124424 | tf_op jit(solution)/shard_map/ppermute | solution.py:448
  31.1 0.4 collective-permute-start.6
  31.5 0.0 collective-permute-done.4
  31.5 1.5 %collective-permute-done.5 = bf16[96,216]{1,0:T(8,128)(2,1)S(1)} collective-permute-done((bf16[96,216]{1,0:T(8,128)(2,1)S(1)}, bf16[96,216]{1,0:T(8,128)(2,1)S(1)}, u32[]{:S(2)}, u32[]{:S(2)}) %collective-permute-start.5) | collective-permute-done | bytes 41504 | tf_op jit(solution)/shard_map/ppermute | solution.py:448
  33.0 1.2 %collective-permute-done.6 = bf16[96,216]{1,0:T(8,128)(2,1)S(1)} collective-permute-done((bf16[96,216]{1,0:T(8,128)(2,1)S(1)}, bf16[96,216]{1,0:T(8,128)(2,1)S(1)}, u32[]{:S(2)}, u32[]{:S(2)}) %collective-permute-start.6) | collective-permute-done | bytes 41504 | tf_op jit(solution)/shard_map/ppermute | solution.py:448
  34.2 0.4 convolution_convert_fusion
  34.7 0.0 copy-done.1
  34.7 0.1 collective-permute-start.7
  34.8 3.7 %collective-permute-done.7 = bf16[496,128]{1,0:T(8,128)(2,1)S(1)} collective-permute-done((bf16[496,128]{1,0:T(8,128)(2,1)S(1)}, bf16[496,128]{1,0:T(8,128)(2,1)S(1)}, u32[]{:S(2)}, u32[]{:S(2)}) %collective-permute-start.7) | collective-permute-done | bytes 127008 | tf_op jit(solution)/shard_map/ppermute | solution.py:439
  38.6 3.5 %collective-permute-start.10 = (bf16[992,128]{1,0:T(8,128)(2,1)S(1)}, bf16[992,128]{1,0:T(8,128)(2,1)S(1)}, u32[]{:S(2)}, u32[]{:S(2)}) collective-permute-start(bf16[992,128]{1,0:T(8,128)(2,1)S(1)} %constant_dynamic-update-slice_fusion.11.refs_0_), channel_id=1, source_target_pairs={{0,192},{16,208},{32,224},{48,240},{64,0},{80,16},{96,32},{112,48}... | collective-permute-start | bytes 761864 | tf_op jit(solution)/shard_map/ppermute | solution.py:439
  42.1 4.5 %collective-permute-start.11 = (bf16[992,128]{1,0:T(8,128)(2,1)S(1)}, bf16[992,128]{1,0:T(8,128)(2,1)S(1)}, u32[]{:S(2)}, u32[]{:S(2)}) collective-permute-start(bf16[992,128]{1,0:T(8,128)(2,1)S(1)} %constant_dynamic-update-slice_fusion.11.refs_0_), channel_id=1, source_target_pairs={{0,16},{16,0},{32,48},{48,32},{64,80},{80,64},{96,112},{112,96},{1... | collective-permute-start | bytes 761864 | tf_op jit(solution)/shard_map/ppermute | solution.py:439
  46.5 0.0 collective-permute-start.8
  46.5 1.0 collective-permute-start.9
  47.5 9.1 %left_forms.1 = (bf16[1296,1408]{1,0:T(8,128)(2,1)}, bf16[1296,1536]{1,0:T(8,128)(2,1)}) custom-call(bf16[1296,1408]{1,0:T(8,128)(2,1)} %flat_form.1.s_hbm), custom_call_target="tpu_custom_call" | custom-call | flops 4294967296 | bytes 4194304 | tf_op jit(solution)/shard_map/left_forms/pallas_call | solution.py:424
  56.7 0.0 collective-permute-done.10.refs_3_
  56.7 0.0 collective-permute-done.11.refs_4_
  56.7 4.2 %collective-permute-done.8.refs_1_ = bf16[992,128]{1,0:T(8,128)(2,1)S(1)} collective-permute-done((bf16[992,128]{1,0:T(8,128)(2,1)S(1)}, bf16[992,128]{1,0:T(8,128)(2,1)S(1)}, u32[]{:S(2)}, u32[]{:S(2)}) %collective-permute-start.8) | collective-permute-done | bytes 253984 | tf_op jit(solution)/shard_map/ppermute | solution.py:439
  60.9 0.0 collective-permute-done.9.refs_2_
  60.9 0.9 collective-permute-start.12
  61.7 0.0 collective-permute-start.13
  61.8 0.5 collective-permute-start.14
  62.3 0.6 collective-permute-done.12.refs_5_
  62.9 0.4 collective-permute-done.13.refs_6_
  63.3 0.4 collective-permute-done.14.refs_7_
  63.6 0.9 gather_small.1.refs_8_
  64.5 12.1 %left.1 = (bf16[216,216]{1,0:T(8,128)(2,1)}, f32[128,256]{1,0:T(8,128)S(1)}) custom-call(s32[16]{0:T(128)S(1)} %fusion.26.order_ref, bf16[992,128]{1,0:T(8,128)(2,1)S(1)} %constant_dynamic-update-slice_fusion.11.refs_0_, bf16[992,128]{1,0:T(8,128)(2,1)S(1)} %collective-permute-done.8.refs_1_, bf16[992,128]{1,0:T(8,128)(2,1)S(1)} %collective-permute-done.9.refs_2_, ...), custom_call_target="tpu_custom_call" | custom-call | flops 8589934592 | bytes 4194304 | tf_op jit(solution)/shard_map/left/pallas_call | solution.py:276
  76.6 0.4 collective-permute-start.15
  77.1 0.9 collective-permute-done.15
  78.0 1.8 %collective-permute-start.16 = (f32[32,256]{1,0:T(8,128)S(1)}, f32[32,256]{1,0:T(8,128)S(1)}, u32[]{:S(2)}, u32[]{:S(2)}) collective-permute-start(f32[32,256]{1,0:T(8,128)S(1)} %constant_dynamic-slice_fusion.4), channel_id=1, source_target_pairs={{0,32},{16,48},{32,0},{48,16},{64,96},{80,112},{96,64},{112,80},{1... | collective-permute-start | bytes 98312 | tf_op jit(solution)/shard_map/ppermute | solution.py:439
  79.8 7.4 %right_form.1.refs_10_ = bf16[1296,1536]{1,0:T(8,128)(2,1)} custom-call(bf16[1296,1408]{1,0:T(8,128)(2,1)} %flat_form.1.s_hbm), custom_call_target="tpu_custom_call" | custom-call | flops 3221225472 | bytes 4194304 | tf_op jit(solution)/shard_map/right_form/pallas_call | solution.py:418
  87.2 0.0 collective-permute-done.16
  87.3 0.1 collective-permute-start.17
  87.4 0.4 collective-permute-start.18
  87.8 2.2 %collective-permute-start.19 = (f32[8,256]{1,0:T(8,128)S(1)}, f32[8,256]{1,0:T(8,128)S(1)}, u32[]{:S(2)}, u32[]{:S(2)}) collective-permute-start(f32[8,256]{1,0:T(8,128)S(1)} %get-tuple-element.67), channel_id=1, source_target_pairs={{0,192},{16,208},{32,224},{48,240},{64,0},{80,16},{96,32},{112,48}... | collective-permute-start | bytes 24584 | tf_op jit(solution)/shard_map/ppermute | solution.py:439
  90.0 11.9 %upper.1 = (bf16[216,216]{1,0:T(8,128)(2,1)}, bf16[6,216]{1,0:T(8,128)(2,1)}) custom-call(s32[16]{0:T(128)S(1)} %fusion.26.order_ref, bf16[992,128]{1,0:T(8,128)(2,1)S(1)} %constant_dynamic-update-slice_fusion.11.refs_0_, bf16[992,128]{1,0:T(8,128)(2,1)S(1)} %collective-permute-done.8.refs_1_, bf16[992,128]{1,0:T(8,128)(2,1)S(1)} %collective-permute-done.9.refs_2_, ...), custom_call_target="tpu_custom_call" | custom-call | flops 8589934592 | bytes 4194304 | tf_op jit(solution)/shard_map/upper/pallas_call | solution.py:269
  101.9 0.0 collective-permute-done.17.one
  101.9 0.0 collective-permute-done.18.two
  101.9 0.0 collective-permute-done.19.three
  101.9 0.7 finish.1
  (20 shorter events, 0.2 us)
Async XLA Ops:
  2.4 11.4 %collective-permute-start = (bf16[24,216]{1,0:T(8,128)(2,1)}, bf16[24,216]{1,0:T(8,128)(2,1)S(1)}, u32[]{:S(2)}, u32[]{:S(2)}) collective-permute-start(bf16[24,216]{1,0:T(8,128)(2,1)} %get-tuple-element.33), channel_id=1, source_target_pairs={{0,0},{1,16},{2,32},{3,48},{4,64},{5,80},{6,96},{7,112},{8,128},{9... | collective-permute-start | bytes 31112 | tf_op jit(solution)/shard_map/ppermute | solution.py:453
  6.9 6.9 %copy-start = (bf16[16,216]{1,0:T(8,128)(2,1)S(1)}, bf16[16,216]{1,0:T(8,128)(2,1)}, u32[]{:S(2)}) copy-start(bf16[16,216]{1,0:T(8,128)(2,1)} %get-tuple-element.36.piece) | copy-start | bytes 20740
  6.9 27.7 %copy-start.1 = (bf16[48,128]{1,0:T(8,128)(2,1)S(1)}, bf16[48,128]{1,0:T(8,128)(2,1)}, u32[]{:S(2)}) copy-start(bf16[48,128]{1,0:T(8,128)(2,1)} %get-tuple-element.38) | copy-start | bytes 36868
  14.0 12.4 %collective-permute-start.1 = (bf16[24,216]{1,0:T(8,128)(2,1)S(1)}, bf16[24,216]{1,0:T(8,128)(2,1)S(1)}, u32[]{:S(2)}, u32[]{:S(2)}) collective-permute-start(bf16[24,216]{1,0:T(8,128)(2,1)S(1)} %get-tuple-element.37), channel_id=1, source_target_pairs={{0,4},{1,5},{2,6},{3,7},{4,8},{5,9},{6,10},{7,11},{8,12},{9,13},{1... | collective-permute-start | bytes 31112 | tf_op jit(solution)/shard_map/ppermute | solution.py:448
  17.2 9.2 %collective-permute-start.2 = (bf16[24,216]{1,0:T(8,128)(2,1)S(1)}, bf16[24,216]{1,0:T(8,128)(2,1)S(1)}, u32[]{:S(2)}, u32[]{:S(2)}) collective-permute-start(bf16[24,216]{1,0:T(8,128)(2,1)S(1)} %get-tuple-element.37), channel_id=1, source_target_pairs={{0,8},{1,9},{2,10},{3,11},{4,12},{5,13},{6,14},{7,15},{8,0},{9,1},... | collective-permute-start | bytes 31112 | tf_op jit(solution)/shard_map/ppermute | solution.py:448
  22.9 4.3 %collective-permute-start.3 = (bf16[24,216]{1,0:T(8,128)(2,1)S(1)}, bf16[24,216]{1,0:T(8,128)(2,1)S(1)}, u32[]{:S(2)}, u32[]{:S(2)}) collective-permute-start(bf16[24,216]{1,0:T(8,128)(2,1)S(1)} %get-tuple-element.37), channel_id=1, source_target_pairs={{0,12},{1,13},{2,14},{3,15},{4,0},{5,1},{6,2},{7,3},{8,4},{9,5},{1... | collective-permute-start | bytes 31112 | tf_op jit(solution)/shard_map/ppermute | solution.py:448
  27.2 4.3 %collective-permute-start.4 = (bf16[96,216]{1,0:T(8,128)(2,1)S(1)}, bf16[96,216]{1,0:T(8,128)(2,1)S(1)}, u32[]{:S(2)}, u32[]{:S(2)}) collective-permute-start(bf16[96,216]{1,0:T(8,128)(2,1)S(1)} %get-tuple-element.70), channel_id=1, source_target_pairs={{0,1},{1,2},{2,3},{3,0},{4,5},{5,6},{6,7},{7,4},{8,9},{9,10},{10,1... | collective-permute-start | bytes 124424 | tf_op jit(solution)/shard_map/ppermute | solution.py:448
  27.3 5.8 %collective-permute-start.5 = (bf16[96,216]{1,0:T(8,128)(2,1)S(1)}, bf16[96,216]{1,0:T(8,128)(2,1)S(1)}, u32[]{:S(2)}, u32[]{:S(2)}) collective-permute-start(bf16[96,216]{1,0:T(8,128)(2,1)S(1)} %get-tuple-element.70), channel_id=1, source_target_pairs={{0,2},{1,3},{2,0},{3,1},{4,6},{5,7},{6,4},{7,5},{8,10},{9,11},{10,... | collective-permute-start | bytes 124424 | tf_op jit(solution)/shard_map/ppermute | solution.py:448
  31.1 3.1 %collective-permute-start.6 = (bf16[96,216]{1,0:T(8,128)(2,1)S(1)}, bf16[96,216]{1,0:T(8,128)(2,1)S(1)}, u32[]{:S(2)}, u32[]{:S(2)}) collective-permute-start(bf16[96,216]{1,0:T(8,128)(2,1)S(1)} %get-tuple-element.70), channel_id=1, source_target_pairs={{0,3},{1,0},{2,1},{3,2},{4,7},{5,4},{6,5},{7,6},{8,11},{9,8},{10,9... | collective-permute-start | bytes 124424 | tf_op jit(solution)/shard_map/ppermute | solution.py:448
  34.7 3.9 %collective-permute-start.7 = (bf16[496,128]{1,0:T(8,128)(2,1)S(1)}, bf16[496,128]{1,0:T(8,128)(2,1)S(1)}, u32[]{:S(2)}, u32[]{:S(2)}) collective-permute-start(bf16[496,128]{1,0:T(8,128)(2,1)S(1)} %pad_maximum_fusion), channel_id=1, source_target_pairs={{0,32},{16,48},{32,0},{48,16},{64,96},{80,112},{96,64},{112,80},{1... | collective-permute-start | bytes 380936 | tf_op jit(solution)/shard_map/ppermute | solution.py:439
  38.6 18.1 %collective-permute-start.10 = (bf16[992,128]{1,0:T(8,128)(2,1)S(1)}, bf16[992,128]{1,0:T(8,128)(2,1)S(1)}, u32[]{:S(2)}, u32[]{:S(2)}) collective-permute-start(bf16[992,128]{1,0:T(8,128)(2,1)S(1)} %constant_dynamic-update-slice_fusion.11.refs_0_), channel_id=1, source_target_pairs={{0,192},{16,208},{32,224},{48,240},{64,0},{80,16},{96,32},{112,48}... | collective-permute-start | bytes 761864 | tf_op jit(solution)/shard_map/ppermute | solution.py:439
  42.1 14.6 %collective-permute-start.11 = (bf16[992,128]{1,0:T(8,128)(2,1)S(1)}, bf16[992,128]{1,0:T(8,128)(2,1)S(1)}, u32[]{:S(2)}, u32[]{:S(2)}) collective-permute-start(bf16[992,128]{1,0:T(8,128)(2,1)S(1)} %constant_dynamic-update-slice_fusion.11.refs_0_), channel_id=1, source_target_pairs={{0,16},{16,0},{32,48},{48,32},{64,80},{80,64},{96,112},{112,96},{1... | collective-permute-start | bytes 761864 | tf_op jit(solution)/shard_map/ppermute | solution.py:439
  46.5 14.3 %collective-permute-start.8 = (bf16[992,128]{1,0:T(8,128)(2,1)S(1)}, bf16[992,128]{1,0:T(8,128)(2,1)S(1)}, u32[]{:S(2)}, u32[]{:S(2)}) collective-permute-start(bf16[992,128]{1,0:T(8,128)(2,1)S(1)} %constant_dynamic-update-slice_fusion.11.refs_0_), channel_id=1, source_target_pairs={{0,64},{16,80},{32,96},{48,112},{64,128},{80,144},{96,160},{112,17... | collective-permute-start | bytes 761864 | tf_op jit(solution)/shard_map/ppermute | solution.py:439
  46.5 14.3 %collective-permute-start.9 = (bf16[992,128]{1,0:T(8,128)(2,1)S(1)}, bf16[992,128]{1,0:T(8,128)(2,1)S(1)}, u32[]{:S(2)}, u32[]{:S(2)}) collective-permute-start(bf16[992,128]{1,0:T(8,128)(2,1)S(1)} %constant_dynamic-update-slice_fusion.11.refs_0_), channel_id=1, source_target_pairs={{0,128},{16,144},{32,160},{48,176},{64,192},{80,208},{96,224},{112... | collective-permute-start | bytes 761864 | tf_op jit(solution)/shard_map/ppermute | solution.py:439
  60.9 2.0 %collective-permute-start.12 = (bf16[992,128]{1,0:T(8,128)(2,1)S(1)}, bf16[992,128]{1,0:T(8,128)(2,1)S(1)}, u32[]{:S(2)}, u32[]{:S(2)}) collective-permute-start(bf16[992,128]{1,0:T(8,128)(2,1)S(1)} %collective-permute-done.8.refs_1_), channel_id=1, source_target_pairs={{0,16},{16,0},{32,48},{48,32},{64,80},{80,64},{96,112},{112,96},{1... | collective-permute-start | bytes 761864 | tf_op jit(solution)/shard_map/ppermute | solution.py:439
  61.7 1.5 %collective-permute-start.13 = (bf16[992,128]{1,0:T(8,128)(2,1)S(1)}, bf16[992,128]{1,0:T(8,128)(2,1)S(1)}, u32[]{:S(2)}, u32[]{:S(2)}) collective-permute-start(bf16[992,128]{1,0:T(8,128)(2,1)S(1)} %collective-permute-done.9.refs_2_), channel_id=1, source_target_pairs={{0,16},{16,0},{32,48},{48,32},{64,80},{80,64},{96,112},{112,96},{1... | collective-permute-start | bytes 761864 | tf_op jit(solution)/shard_map/ppermute | solution.py:439
  61.8 1.9 %collective-permute-start.14 = (bf16[992,128]{1,0:T(8,128)(2,1)S(1)}, bf16[992,128]{1,0:T(8,128)(2,1)S(1)}, u32[]{:S(2)}, u32[]{:S(2)}) collective-permute-start(bf16[992,128]{1,0:T(8,128)(2,1)S(1)} %collective-permute-done.10.refs_3_), channel_id=1, source_target_pairs={{0,16},{16,0},{32,48},{48,32},{64,80},{80,64},{96,112},{112,96},{1... | collective-permute-start | bytes 761864 | tf_op jit(solution)/shard_map/ppermute | solution.py:439
  76.6 1.4 %collective-permute-start.15 = (f32[64,256]{1,0:T(8,128)S(1)}, f32[64,256]{1,0:T(8,128)S(1)}, u32[]{:S(2)}, u32[]{:S(2)}) collective-permute-start(f32[64,256]{1,0:T(8,128)S(1)} %constant_dynamic-slice_fusion.5), channel_id=1, source_target_pairs={{0,16},{16,0},{32,48},{48,32},{64,80},{80,64},{96,112},{112,96},{1... | collective-permute-start | bytes 196616 | tf_op jit(solution)/shard_map/ppermute | solution.py:439
  78.0 9.2 %collective-permute-start.16 = (f32[32,256]{1,0:T(8,128)S(1)}, f32[32,256]{1,0:T(8,128)S(1)}, u32[]{:S(2)}, u32[]{:S(2)}) collective-permute-start(f32[32,256]{1,0:T(8,128)S(1)} %constant_dynamic-slice_fusion.4), channel_id=1, source_target_pairs={{0,32},{16,48},{32,0},{48,16},{64,96},{80,112},{96,64},{112,80},{1... | collective-permute-start | bytes 98312 | tf_op jit(solution)/shard_map/ppermute | solution.py:439
  87.3 14.7 %collective-permute-start.17 = (f32[8,256]{1,0:T(8,128)S(1)}, f32[8,256]{1,0:T(8,128)S(1)}, u32[]{:S(2)}, u32[]{:S(2)}) collective-permute-start(f32[8,256]{1,0:T(8,128)S(1)} %get-tuple-element.69), channel_id=1, source_target_pairs={{0,64},{16,80},{32,96},{48,112},{64,128},{80,144},{96,160},{112,17... | collective-permute-start | bytes 24584 | tf_op jit(solution)/shard_map/ppermute | solution.py:439
  87.4 14.6 %collective-permute-start.18 = (f32[8,256]{1,0:T(8,128)S(1)}, f32[8,256]{1,0:T(8,128)S(1)}, u32[]{:S(2)}, u32[]{:S(2)}) collective-permute-start(f32[8,256]{1,0:T(8,128)S(1)} %get-tuple-element.68), channel_id=1, source_target_pairs={{0,128},{16,144},{32,160},{48,176},{64,192},{80,208},{96,224},{112... | collective-permute-start | bytes 24584 | tf_op jit(solution)/shard_map/ppermute | solution.py:439
  87.8 14.1 %collective-permute-start.19 = (f32[8,256]{1,0:T(8,128)S(1)}, f32[8,256]{1,0:T(8,128)S(1)}, u32[]{:S(2)}, u32[]{:S(2)}) collective-permute-start(f32[8,256]{1,0:T(8,128)S(1)} %get-tuple-element.67), channel_id=1, source_target_pairs={{0,192},{16,208},{32,224},{48,240},{64,0},{80,16},{96,32},{112,48}... | collective-permute-start | bytes 24584 | tf_op jit(solution)/shard_map/ppermute | solution.py:439

commit v6 on v5

--- a/solution.py
+++ b/solution.py
@@ -493,7 +493,10 @@
     ber = rows[:, 256:]
 
     own = jnp.concatenate([rows[:, :128], rows[:, 128:256], pack, tpx], axis=0)
-    near = stacked(own, [other_z(own)])
+    beside = other_z(own)
+    wright = right_form(hold((s2, own))[0])
+    beside, wright = hold((beside, wright))
+    near = stacked(own, [beside])
     far = [along_y(near, s) for s in (1, 2, 3)]
     near_twin = other_core(near)
     wtop, wbot = left_forms(hold((s2, near))[0])
@@ -508,11 +511,10 @@
 
     lf, cb = left(order, bufs, small, ber, wtop, wbot, bpr)
     part = lambda v, n, size: lax.dynamic_slice_in_dim(v, n * size, size, 0)
-    cb = part(cb, core, 64) + other_core(part(cb, 1 - core, 64))
-    cb_z = other_z(part(cb, 1 - zlo, 32))
-    wright = right_form(hold((s2, cb))[0])
-    cb_z, wright = hold((cb_z, wright))
-    cb = part(cb, zlo, 32) + cb_z
+    mine = lambda k, z: part(cb, k * 2 + z, 32)
+    near_sums = [other_core(mine(1 - core, zlo)), other_z(mine(core, 1 - zlo)),
+                 row_permute(mine(1 - core, 1 - zlo), lambda a, b, k: (a, 1 - b, 1 - k))]
+    cb = mine(core, zlo) + near_sums[0] + near_sums[1] + near_sums[2]
     cb_y = [along_y(part(cb, (y + s) % 4, 8), s) for s in (1, 2, 3)]
     order = hold((order, cb))[0]
     up, corner_top = upper(order, bufs, small, wtop, wright)

time: 103 us -> 101 us (0.981)
  waiting for transfers between devices: 13.7 us -> 11.1 us
    ppermute x13 -> x14, waiting for transfers between devices: 10.2 us -> 7.53 us  [row_permute(): return lax.ppermute(x, ROW, pairs)]
    ppermute x13 -> x14, starting transfers between devices: 15.5 us -> 16.3 us  [row_permute(): return lax.ppermute(x, ROW, pairs)]
  transfers between devices with their start and end apart: 20 -> 21, of which waited for: 9 -> 9; matrix products, arithmetic and copies ran while one was open for 0% -> 0% of each run, Pallas kernels for 34% -> 35%
where the time goes in v6:
time: 101 us
  Pallas kernels  50.9 us (50%)
  starting transfers between devices  37.4 us (37%)
  waiting for transfers between devices  11.1 us (11%)
    ppermute x6, starting transfers between devices, col_permute(): return lax.ppermute(x, COL, pairs)  16.6 us
    ppermute x14, starting transfers between devices, row_permute(): return lax.ppermute(x, ROW, pairs)  16.3 us
    pallas_call x1, Pallas kernels, left(): pl.pallas_call(left_kernel, out_shape=(shape_of(216, 216), shape_of(128,...  12 us
    pallas_call x1, Pallas kernels, upper(): pl.pallas_call(upper_kernel, out_shape=(shape_of(216, 216), shape_of(6, 2...  11.9 us
    pallas_call x1, Pallas kernels, left_forms(): pl.pallas_call(left_forms_kernel, out_shape=(shape_of(1296, 1408), shape_...  9.19 us
    ppermute x14, waiting for transfers between devices, row_permute(): return lax.ppermute(x, ROW, pairs)  7.53 us
    pallas_call x1, Pallas kernels, right_form(): pl.pallas_call(right_form_kernel, out_shape=shape_of(1296, 1536), in_spec...  7.37 us
    pallas_call x1, Pallas kernels, flat_form(): pl.pallas_call(flat_form_kernel, out_shape=shape_of(1296, 1408), in_specs...  6.93 us
  transfers between devices with their start and end apart: 21, of which 9 were waited for; matrix products, arithmetic and copies ran while one was open for 0% of the time, Pallas kernels for 35%

profile of v6, /device:TPU:1, one launch (start us, length us, event | category | flops | bytes accessed | tf_op | source)
XLA Modules:
  0.0 100.9 jit_solution(7574882834973944124)
XLA Ops:
  0.6 1.8 %prepare.1 = (bf16[16,216]{1,0:T(8,128)(2,1)}, bf16[48,128]{1,0:T(8,128)(2,1)}, bf16[24,216]{1,0:T(8,128)(2,1)}) custom-call(s32[1]{0:T(128)} %bitcast.at_ref, bf16[6,6,36]{2,1,0:T(8,128)(2,1)} %refs_0_.1, bf16[6,6,36]{2,1,0:T(8,128)(2,1)} %refs_1_.1, bf16[6,6,36]{2,1,0:T(8,128)(2,1)} %refs_2_.1, bf16[6,6,36]{2,1,0:T(8,128)(2,1)} %refs_3_.1, ...), custom_call_target="tpu_custom_call" | custom-call | tf_op jit(solution)/shard_map/prepare/pallas_call | solution.py:251
  2.4 4.5 %collective-permute-start = (bf16[24,216]{1,0:T(8,128)(2,1)}, bf16[24,216]{1,0:T(8,128)(2,1)S(1)}, u32[]{:S(2)}, u32[]{:S(2)}) collective-permute-start(bf16[24,216]{1,0:T(8,128)(2,1)} %get-tuple-element.33), channel_id=1, source_target_pairs={{0,0},{1,16},{2,32},{3,48},{4,64},{5,80},{6,96},{7,112},{8,128},{9... | collective-permute-start | bytes 31112 | tf_op jit(solution)/shard_map/ppermute | solution.py:453
  6.9 0.0 copy-start
  6.9 0.0 copy-start.1
  6.9 6.9 %flat_form.1.s_hbm = bf16[1296,1408]{1,0:T(8,128)(2,1)} custom-call(bf16[13122,128]{1,0:T(8,128)(2,1)} %bitcast.13), custom_call_target="tpu_custom_call" | custom-call | flops 3221225472 | bytes 4194304 | tf_op jit(solution)/shard_map/flat_form/pallas_call | solution.py:411
  13.9 0.0 collective-permute-done.turned
  13.9 0.0 copy-done
  13.9 0.1 pieces.1
  14.0 3.2 %collective-permute-start.1 = (bf16[24,216]{1,0:T(8,128)(2,1)S(1)}, bf16[24,216]{1,0:T(8,128)(2,1)S(1)}, u32[]{:S(2)}, u32[]{:S(2)}) collective-permute-start(bf16[24,216]{1,0:T(8,128)(2,1)S(1)} %get-tuple-element.37), channel_id=1, source_target_pairs={{0,4},{1,5},{2,6},{3,7},{4,8},{5,9},{6,10},{7,11},{8,12},{9,13},{1... | collective-permute-start | bytes 31112 | tf_op jit(solution)/shard_map/ppermute | solution.py:448
  17.2 5.7 %collective-permute-start.2 = (bf16[24,216]{1,0:T(8,128)(2,1)S(1)}, bf16[24,216]{1,0:T(8,128)(2,1)S(1)}, u32[]{:S(2)}, u32[]{:S(2)}) collective-permute-start(bf16[24,216]{1,0:T(8,128)(2,1)S(1)} %get-tuple-element.37), channel_id=1, source_target_pairs={{0,8},{1,9},{2,10},{3,11},{4,12},{5,13},{6,14},{7,15},{8,0},{9,1},... | collective-permute-start | bytes 31112 | tf_op jit(solution)/shard_map/ppermute | solution.py:448
  22.9 3.5 %collective-permute-start.3 = (bf16[24,216]{1,0:T(8,128)(2,1)S(1)}, bf16[24,216]{1,0:T(8,128)(2,1)S(1)}, u32[]{:S(2)}, u32[]{:S(2)}) collective-permute-start(bf16[24,216]{1,0:T(8,128)(2,1)S(1)} %get-tuple-element.37), channel_id=1, source_target_pairs={{0,12},{1,13},{2,14},{3,15},{4,0},{5,1},{6,2},{7,3},{8,4},{9,5},{1... | collective-permute-start | bytes 31112 | tf_op jit(solution)/shard_map/ppermute | solution.py:448
  26.4 0.0 collective-permute-done.1
  26.4 0.0 collective-permute-done.2
  26.4 0.8 collective-permute-done.3
  27.2 0.0 collective-permute-start.4
  27.3 3.9 %collective-permute-start.5 = (bf16[96,216]{1,0:T(8,128)(2,1)S(1)}, bf16[96,216]{1,0:T(8,128)(2,1)S(1)}, u32[]{:S(2)}, u32[]{:S(2)}) collective-permute-start(bf16[96,216]{1,0:T(8,128)(2,1)S(1)} %get-tuple-element.73), channel_id=1, source_target_pairs={{0,2},{1,3},{2,0},{3,1},{4,6},{5,7},{6,4},{7,5},{8,10},{9,11},{10,... | collective-permute-start | bytes 124424 | tf_op jit(solution)/shard_map/ppermute | solution.py:448
  31.1 0.4 collective-permute-start.6
  31.5 0.0 collective-permute-done.4
  31.5 1.5 %collective-permute-done.5 = bf16[96,216]{1,0:T(8,128)(2,1)S(1)} collective-permute-done((bf16[96,216]{1,0:T(8,128)(2,1)S(1)}, bf16[96,216]{1,0:T(8,128)(2,1)S(1)}, u32[]{:S(2)}, u32[]{:S(2)}) %collective-permute-start.5) | collective-permute-done | bytes 41504 | tf_op jit(solution)/shard_map/ppermute | solution.py:448
  33.0 1.2 %collective-permute-done.6 = bf16[96,216]{1,0:T(8,128)(2,1)S(1)} collective-permute-done((bf16[96,216]{1,0:T(8,128)(2,1)S(1)}, bf16[96,216]{1,0:T(8,128)(2,1)S(1)}, u32[]{:S(2)}, u32[]{:S(2)}) %collective-permute-start.6) | collective-permute-done | bytes 41504 | tf_op jit(solution)/shard_map/ppermute | solution.py:448
  34.2 0.4 convolution_convert_fusion
  34.7 0.0 copy-done.1
  34.7 0.1 collective-permute-start.7
  34.8 7.4 %right_form.1.refs_10_ = bf16[1296,1536]{1,0:T(8,128)(2,1)} custom-call(bf16[1296,1408]{1,0:T(8,128)(2,1)} %flat_form.1.s_hbm), custom_call_target="tpu_custom_call" | custom-call | flops 3221225472 | bytes 4194304 | tf_op jit(solution)/shard_map/right_form/pallas_call | solution.py:418
  42.2 0.0 collective-permute-done.7
  42.3 4.6 %collective-permute-start.10 = (bf16[992,128]{1,0:T(8,128)(2,1)S(1)}, bf16[992,128]{1,0:T(8,128)(2,1)S(1)}, u32[]{:S(2)}, u32[]{:S(2)}) collective-permute-start(bf16[992,128]{1,0:T(8,128)(2,1)S(1)} %constant_dynamic-update-slice_fusion.11.refs_0_), channel_id=1, source_target_pairs={{0,192},{16,208},{32,224},{48,240},{64,0},{80,16},{96,32},{112,48}... | collective-permute-start | bytes 761864 | tf_op jit(solution)/shard_map/ppermute | solution.py:439
  46.9 4.2 %collective-permute-start.11 = (bf16[992,128]{1,0:T(8,128)(2,1)S(1)}, bf16[992,128]{1,0:T(8,128)(2,1)S(1)}, u32[]{:S(2)}, u32[]{:S(2)}) collective-permute-start(bf16[992,128]{1,0:T(8,128)(2,1)S(1)} %constant_dynamic-update-slice_fusion.11.refs_0_), channel_id=1, source_target_pairs={{0,16},{16,0},{32,48},{48,32},{64,80},{80,64},{96,112},{112,96},{1... | collective-permute-start | bytes 761864 | tf_op jit(solution)/shard_map/ppermute | solution.py:439
  51.1 0.0 collective-permute-start.8
  51.1 1.0 collective-permute-start.9
  52.1 9.2 %left_forms.1 = (bf16[1296,1408]{1,0:T(8,128)(2,1)}, bf16[1296,1536]{1,0:T(8,128)(2,1)}) custom-call(bf16[1296,1408]{1,0:T(8,128)(2,1)} %flat_form.1.s_hbm), custom_call_target="tpu_custom_call" | custom-call | flops 4294967296 | bytes 4194304 | tf_op jit(solution)/shard_map/left_forms/pallas_call | solution.py:424
  61.3 0.0 collective-permute-done.10.refs_3_
  61.3 0.0 collective-permute-done.11.refs_4_
  61.3 4.1 %collective-permute-done.8.refs_1_ = bf16[992,128]{1,0:T(8,128)(2,1)S(1)} collective-permute-done((bf16[992,128]{1,0:T(8,128)(2,1)S(1)}, bf16[992,128]{1,0:T(8,128)(2,1)S(1)}, u32[]{:S(2)}, u32[]{:S(2)}) %collective-permute-start.8) | collective-permute-done | bytes 253984 | tf_op jit(solution)/shard_map/ppermute | solution.py:439
  65.5 0.0 collective-permute-done.9.refs_2_
  65.5 0.9 collective-permute-start.12
  66.3 0.0 collective-permute-start.13
  66.3 0.5 collective-permute-start.14
  66.9 0.6 collective-permute-done.12.refs_5_
  67.5 0.4 collective-permute-done.13.refs_6_
  67.8 0.4 collective-permute-done.14.refs_7_
  68.2 0.9 gather_small.1.refs_8_
  69.1 12.0 %left.1 = (bf16[216,216]{1,0:T(8,128)(2,1)}, f32[128,256]{1,0:T(8,128)S(1)}) custom-call(s32[16]{0:T(128)S(1)} %fusion.26.order_ref, bf16[992,128]{1,0:T(8,128)(2,1)S(1)} %constant_dynamic-update-slice_fusion.11.refs_0_, bf16[992,128]{1,0:T(8,128)(2,1)S(1)} %collective-permute-done.8.refs_1_, bf16[992,128]{1,0:T(8,128)(2,1)S(1)} %collective-permute-done.9.refs_2_, ...), custom_call_target="tpu_custom_call" | custom-call | flops 8589934592 | bytes 4194304 | tf_op jit(solution)/shard_map/left/pallas_call | solution.py:276
  81.2 0.4 collective-permute-start.15
  81.6 0.0 collective-permute-start.16
  81.6 1.8 %collective-permute-start.17 = (f32[32,256]{1,0:T(8,128)S(1)}, f32[32,256]{1,0:T(8,128)S(1)}, u32[]{:S(2)}, u32[]{:S(2)}) collective-permute-start(f32[32,256]{1,0:T(8,128)S(1)} %get-tuple-element.67), channel_id=1, source_target_pairs={{0,48},{16,32},{32,16},{48,0},{64,112},{80,96},{96,80},{112,64},{1... | collective-permute-start | bytes 98312 | tf_op jit(solution)/shard_map/ppermute | solution.py:439
  83.4 0.0 collective-permute-done.15
  83.4 1.0 collective-permute-done.16
  84.4 1.1 %collective-permute-done.17 = f32[32,256]{1,0:T(8,128)S(1)} collective-permute-done((f32[32,256]{1,0:T(8,128)S(1)}, f32[32,256]{1,0:T(8,128)S(1)}, u32[]{:S(2)}, u32[]{:S(2)}) %collective-permute-start.17) | collective-permute-done | bytes 32800 | tf_op jit(solution)/shard_map/ppermute | solution.py:439
  85.5 0.1 collective-permute-start.18
  85.6 0.4 collective-permute-start.19
  86.0 2.2 %collective-permute-start.20 = (f32[8,256]{1,0:T(8,128)S(1)}, f32[8,256]{1,0:T(8,128)S(1)}, u32[]{:S(2)}, u32[]{:S(2)}) collective-permute-start(f32[8,256]{1,0:T(8,128)S(1)} %get-tuple-element.70), channel_id=1, source_target_pairs={{0,192},{16,208},{32,224},{48,240},{64,0},{80,16},{96,32},{112,48}... | collective-permute-start | bytes 24584 | tf_op jit(solution)/shard_map/ppermute | solution.py:439
  88.2 11.9 %upper.1 = (bf16[216,216]{1,0:T(8,128)(2,1)}, bf16[6,216]{1,0:T(8,128)(2,1)}) custom-call(s32[16]{0:T(128)S(1)} %fusion.26.order_ref, bf16[992,128]{1,0:T(8,128)(2,1)S(1)} %constant_dynamic-update-slice_fusion.11.refs_0_, bf16[992,128]{1,0:T(8,128)(2,1)S(1)} %collective-permute-done.8.refs_1_, bf16[992,128]{1,0:T(8,128)(2,1)S(1)} %collective-permute-done.9.refs_2_, ...), custom_call_target="tpu_custom_call" | custom-call | flops 8589934592 | bytes 4194304 | tf_op jit(solution)/shard_map/upper/pallas_call | solution.py:269
  100.1 0.0 collective-permute-done.18.one
  100.2 0.0 collective-permute-done.19.two
  100.2 0.0 collective-permute-done.20.three
  100.2 0.7 finish.1
  (18 shorter events, 0.2 us)
Async XLA Ops:
  2.4 11.5 %collective-permute-start = (bf16[24,216]{1,0:T(8,128)(2,1)}, bf16[24,216]{1,0:T(8,128)(2,1)S(1)}, u32[]{:S(2)}, u32[]{:S(2)}) collective-permute-start(bf16[24,216]{1,0:T(8,128)(2,1)} %get-tuple-element.33), channel_id=1, source_target_pairs={{0,0},{1,16},{2,32},{3,48},{4,64},{5,80},{6,96},{7,112},{8,128},{9... | collective-permute-start | bytes 31112 | tf_op jit(solution)/shard_map/ppermute | solution.py:453
  6.9 7.0 %copy-start = (bf16[16,216]{1,0:T(8,128)(2,1)S(1)}, bf16[16,216]{1,0:T(8,128)(2,1)}, u32[]{:S(2)}) copy-start(bf16[16,216]{1,0:T(8,128)(2,1)} %get-tuple-element.36.piece) | copy-start | bytes 20740
  6.9 27.7 %copy-start.1 = (bf16[48,128]{1,0:T(8,128)(2,1)S(1)}, bf16[48,128]{1,0:T(8,128)(2,1)}, u32[]{:S(2)}) copy-start(bf16[48,128]{1,0:T(8,128)(2,1)} %get-tuple-element.38) | copy-start | bytes 36868
  14.0 12.4 %collective-permute-start.1 = (bf16[24,216]{1,0:T(8,128)(2,1)S(1)}, bf16[24,216]{1,0:T(8,128)(2,1)S(1)}, u32[]{:S(2)}, u32[]{:S(2)}) collective-permute-start(bf16[24,216]{1,0:T(8,128)(2,1)S(1)} %get-tuple-element.37), channel_id=1, source_target_pairs={{0,4},{1,5},{2,6},{3,7},{4,8},{5,9},{6,10},{7,11},{8,12},{9,13},{1... | collective-permute-start | bytes 31112 | tf_op jit(solution)/shard_map/ppermute | solution.py:448
  17.2 9.2 %collective-permute-start.2 = (bf16[24,216]{1,0:T(8,128)(2,1)S(1)}, bf16[24,216]{1,0:T(8,128)(2,1)S(1)}, u32[]{:S(2)}, u32[]{:S(2)}) collective-permute-start(bf16[24,216]{1,0:T(8,128)(2,1)S(1)} %get-tuple-element.37), channel_id=1, source_target_pairs={{0,8},{1,9},{2,10},{3,11},{4,12},{5,13},{6,14},{7,15},{8,0},{9,1},... | collective-permute-start | bytes 31112 | tf_op jit(solution)/shard_map/ppermute | solution.py:448
  22.9 4.3 %collective-permute-start.3 = (bf16[24,216]{1,0:T(8,128)(2,1)S(1)}, bf16[24,216]{1,0:T(8,128)(2,1)S(1)}, u32[]{:S(2)}, u32[]{:S(2)}) collective-permute-start(bf16[24,216]{1,0:T(8,128)(2,1)S(1)} %get-tuple-element.37), channel_id=1, source_target_pairs={{0,12},{1,13},{2,14},{3,15},{4,0},{5,1},{6,2},{7,3},{8,4},{9,5},{1... | collective-permute-start | bytes 31112 | tf_op jit(solution)/shard_map/ppermute | solution.py:448
  27.2 4.3 %collective-permute-start.4 = (bf16[96,216]{1,0:T(8,128)(2,1)S(1)}, bf16[96,216]{1,0:T(8,128)(2,1)S(1)}, u32[]{:S(2)}, u32[]{:S(2)}) collective-permute-start(bf16[96,216]{1,0:T(8,128)(2,1)S(1)} %get-tuple-element.73), channel_id=1, source_target_pairs={{0,1},{1,2},{2,3},{3,0},{4,5},{5,6},{6,7},{7,4},{8,9},{9,10},{10,1... | collective-permute-start | bytes 124424 | tf_op jit(solution)/shard_map/ppermute | solution.py:448
  27.3 5.8 %collective-permute-start.5 = (bf16[96,216]{1,0:T(8,128)(2,1)S(1)}, bf16[96,216]{1,0:T(8,128)(2,1)S(1)}, u32[]{:S(2)}, u32[]{:S(2)}) collective-permute-start(bf16[96,216]{1,0:T(8,128)(2,1)S(1)} %get-tuple-element.73), channel_id=1, source_target_pairs={{0,2},{1,3},{2,0},{3,1},{4,6},{5,7},{6,4},{7,5},{8,10},{9,11},{10,... | collective-permute-start | bytes 124424 | tf_op jit(solution)/shard_map/ppermute | solution.py:448
  31.1 3.1 %collective-permute-start.6 = (bf16[96,216]{1,0:T(8,128)(2,1)S(1)}, bf16[96,216]{1,0:T(8,128)(2,1)S(1)}, u32[]{:S(2)}, u32[]{:S(2)}) collective-permute-start(bf16[96,216]{1,0:T(8,128)(2,1)S(1)} %get-tuple-element.73), channel_id=1, source_target_pairs={{0,3},{1,0},{2,1},{3,2},{4,7},{5,4},{6,5},{7,6},{8,11},{9,8},{10,9... | collective-permute-start | bytes 124424 | tf_op jit(solution)/shard_map/ppermute | solution.py:448
  34.7 7.5 %collective-permute-start.7 = (bf16[496,128]{1,0:T(8,128)(2,1)S(1)}, bf16[496,128]{1,0:T(8,128)(2,1)S(1)}, u32[]{:S(2)}, u32[]{:S(2)}) collective-permute-start(bf16[496,128]{1,0:T(8,128)(2,1)S(1)} %pad_maximum_fusion), channel_id=1, source_target_pairs={{0,32},{16,48},{32,0},{48,16},{64,96},{80,112},{96,64},{112,80},{1... | collective-permute-start | bytes 380936 | tf_op jit(solution)/shard_map/ppermute | solution.py:439
  42.3 19.1 %collective-permute-start.10 = (bf16[992,128]{1,0:T(8,128)(2,1)S(1)}, bf16[992,128]{1,0:T(8,128)(2,1)S(1)}, u32[]{:S(2)}, u32[]{:S(2)}) collective-permute-start(bf16[992,128]{1,0:T(8,128)(2,1)S(1)} %constant_dynamic-update-slice_fusion.11.refs_0_), channel_id=1, source_target_pairs={{0,192},{16,208},{32,224},{48,240},{64,0},{80,16},{96,32},{112,48}... | collective-permute-start | bytes 761864 | tf_op jit(solution)/shard_map/ppermute | solution.py:439
  46.9 14.5 %collective-permute-start.11 = (bf16[992,128]{1,0:T(8,128)(2,1)S(1)}, bf16[992,128]{1,0:T(8,128)(2,1)S(1)}, u32[]{:S(2)}, u32[]{:S(2)}) collective-permute-start(bf16[992,128]{1,0:T(8,128)(2,1)S(1)} %constant_dynamic-update-slice_fusion.11.refs_0_), channel_id=1, source_target_pairs={{0,16},{16,0},{32,48},{48,32},{64,80},{80,64},{96,112},{112,96},{1... | collective-permute-start | bytes 761864 | tf_op jit(solution)/shard_map/ppermute | solution.py:439
  51.1 14.3 %collective-permute-start.8 = (bf16[992,128]{1,0:T(8,128)(2,1)S(1)}, bf16[992,128]{1,0:T(8,128)(2,1)S(1)}, u32[]{:S(2)}, u32[]{:S(2)}) collective-permute-start(bf16[992,128]{1,0:T(8,128)(2,1)S(1)} %constant_dynamic-update-slice_fusion.11.refs_0_), channel_id=1, source_target_pairs={{0,64},{16,80},{32,96},{48,112},{64,128},{80,144},{96,160},{112,17... | collective-permute-start | bytes 761864 | tf_op jit(solution)/shard_map/ppermute | solution.py:439
  51.1 14.3 %collective-permute-start.9 = (bf16[992,128]{1,0:T(8,128)(2,1)S(1)}, bf16[992,128]{1,0:T(8,128)(2,1)S(1)}, u32[]{:S(2)}, u32[]{:S(2)}) collective-permute-start(bf16[992,128]{1,0:T(8,128)(2,1)S(1)} %constant_dynamic-update-slice_fusion.11.refs_0_), channel_id=1, source_target_pairs={{0,128},{16,144},{32,160},{48,176},{64,192},{80,208},{96,224},{112... | collective-permute-start | bytes 761864 | tf_op jit(solution)/shard_map/ppermute | solution.py:439
  65.5 2.0 %collective-permute-start.12 = (bf16[992,128]{1,0:T(8,128)(2,1)S(1)}, bf16[992,128]{1,0:T(8,128)(2,1)S(1)}, u32[]{:S(2)}, u32[]{:S(2)}) collective-permute-start(bf16[992,128]{1,0:T(8,128)(2,1)S(1)} %collective-permute-done.8.refs_1_), channel_id=1, source_target_pairs={{0,16},{16,0},{32,48},{48,32},{64,80},{80,64},{96,112},{112,96},{1... | collective-permute-start | bytes 761864 | tf_op jit(solution)/shard_map/ppermute | solution.py:439
  66.3 1.5 %collective-permute-start.13 = (bf16[992,128]{1,0:T(8,128)(2,1)S(1)}, bf16[992,128]{1,0:T(8,128)(2,1)S(1)}, u32[]{:S(2)}, u32[]{:S(2)}) collective-permute-start(bf16[992,128]{1,0:T(8,128)(2,1)S(1)} %collective-permute-done.9.refs_2_), channel_id=1, source_target_pairs={{0,16},{16,0},{32,48},{48,32},{64,80},{80,64},{96,112},{112,96},{1... | collective-permute-start | bytes 761864 | tf_op jit(solution)/shard_map/ppermute | solution.py:439
  66.3 1.9 %collective-permute-start.14 = (bf16[992,128]{1,0:T(8,128)(2,1)S(1)}, bf16[992,128]{1,0:T(8,128)(2,1)S(1)}, u32[]{:S(2)}, u32[]{:S(2)}) collective-permute-start(bf16[992,128]{1,0:T(8,128)(2,1)S(1)} %collective-permute-done.10.refs_3_), channel_id=1, source_target_pairs={{0,16},{16,0},{32,48},{48,32},{64,80},{80,64},{96,112},{112,96},{1... | collective-permute-start | bytes 761864 | tf_op jit(solution)/shard_map/ppermute | solution.py:439
  81.2 2.2 %collective-permute-start.15 = (f32[32,256]{1,0:T(8,128)S(1)}, f32[32,256]{1,0:T(8,128)S(1)}, u32[]{:S(2)}, u32[]{:S(2)}) collective-permute-start(f32[32,256]{1,0:T(8,128)S(1)} %get-tuple-element.66), channel_id=1, source_target_pairs={{0,16},{16,0},{32,48},{48,32},{64,80},{80,64},{96,112},{112,96},{1... | collective-permute-start | bytes 98312 | tf_op jit(solution)/shard_map/ppermute | solution.py:439
  81.6 2.8 %collective-permute-start.16 = (f32[32,256]{1,0:T(8,128)S(1)}, f32[32,256]{1,0:T(8,128)S(1)}, u32[]{:S(2)}, u32[]{:S(2)}) collective-permute-start(f32[32,256]{1,0:T(8,128)S(1)} %get-tuple-element.68), channel_id=1, source_target_pairs={{0,32},{16,48},{32,0},{48,16},{64,96},{80,112},{96,64},{112,80},{1... | collective-permute-start | bytes 98312 | tf_op jit(solution)/shard_map/ppermute | solution.py:439
  81.6 3.8 %collective-permute-start.17 = (f32[32,256]{1,0:T(8,128)S(1)}, f32[32,256]{1,0:T(8,128)S(1)}, u32[]{:S(2)}, u32[]{:S(2)}) collective-permute-start(f32[32,256]{1,0:T(8,128)S(1)} %get-tuple-element.67), channel_id=1, source_target_pairs={{0,48},{16,32},{32,16},{48,0},{64,112},{80,96},{96,80},{112,64},{1... | collective-permute-start | bytes 98312 | tf_op jit(solution)/shard_map/ppermute | solution.py:439
  85.5 14.7 %collective-permute-start.18 = (f32[8,256]{1,0:T(8,128)S(1)}, f32[8,256]{1,0:T(8,128)S(1)}, u32[]{:S(2)}, u32[]{:S(2)}) collective-permute-start(f32[8,256]{1,0:T(8,128)S(1)} %get-tuple-element.72), channel_id=1, source_target_pairs={{0,64},{16,80},{32,96},{48,112},{64,128},{80,144},{96,160},{112,17... | collective-permute-start | bytes 24584 | tf_op jit(solution)/shard_map/ppermute | solution.py:439
  85.6 14.6 %collective-permute-start.19 = (f32[8,256]{1,0:T(8,128)S(1)}, f32[8,256]{1,0:T(8,128)S(1)}, u32[]{:S(2)}, u32[]{:S(2)}) collective-permute-start(f32[8,256]{1,0:T(8,128)S(1)} %get-tuple-element.71), channel_id=1, source_target_pairs={{0,128},{16,144},{32,160},{48,176},{64,192},{80,208},{96,224},{112... | collective-permute-start | bytes 24584 | tf_op jit(solution)/shard_map/ppermute | solution.py:439
  86.0 14.2 %collective-permute-start.20 = (f32[8,256]{1,0:T(8,128)S(1)}, f32[8,256]{1,0:T(8,128)S(1)}, u32[]{:S(2)}, u32[]{:S(2)}) collective-permute-start(f32[8,256]{1,0:T(8,128)S(1)} %get-tuple-element.70), channel_id=1, source_target_pairs={{0,192},{16,208},{32,224},{48,240},{64,0},{80,16},{96,32},{112,48}... | collective-permute-start | bytes 24584 | tf_op jit(solution)/shard_map/ppermute | solution.py:439
